TPU v7x, 32 devices: a whole 2x2x4 slice. The times are simulated.
32 devices in a mesh: seq: 16 (over z, y, core), head: 2 (over x).
Axes of the slice: x: 2, y: 2, z: 4, core: 2. Of those that a mesh axis runs over, the one named last changes fastest.
Arguments:
- q_main: bfloat16 [2048, 128, 576], P('seq', 'head'), may hold values from -6 to 6
- latent_keys: bfloat16 [2048, 576], P('seq'), may hold values from -6 to 6
- lse_main: float32 [2048, 128], P('seq', 'head'), may hold values from 0.5 to 2.5
- index_queries: bfloat16 [2048, 64, 128], P('seq', 'head'), may hold values from -6 to 6
- index_weights: float32 [2048, 64], P('seq', 'head'), may hold values from -1.5 to 1.5
- index_keys: bfloat16 [2048, 128], P('seq'), may hold values from -6 to 6
- lse_index: float32 [2048], P('seq'), may hold values from 0 to 2
- slab_order: int32 [16], replicated, may hold values from 0 to 15, each once
- block_live: int32 [16, 16], replicated, may hold values 0 or 1
Outputs:
- key_grad: float32 [2048, 128], P('seq')
Inputs may be any that keep to these rules, and one draw needn't show every extreme that they name: `slab_order`: a permutation: every slab number once.
All inputs are finite; a program needn't handle non-finite values.
Results may differ from a plain program's by a relative error of at most 0.0028.
Values may be sent and summed in bfloat16 or wider, within the bound.
No kernel may reach another device: no remote copies, remote signals or barrier semaphores. Data moves between devices by JAX's collectives and lax.ppermute only.
A program may use at most 64 MiB of HBM per device.

v0:
```python
import functools
import math

import jax
import jax.numpy as jnp
from jax import lax
from jax.experimental import pallas as pl
from jax.experimental.pallas import tpu as pltpu
from jax.sharding import PartitionSpec as P


HEADS = 128
HOPS = 8
LAST = 2
PIECES = 8
LOG2E = math.log2(math.e)
MAIN_SCALE = 1.0 / 192.0**0.5
LIMIT = 20 * 2**20
WHOLE = 49 * 2**20
NT = (((1,), (1,)), ((), ()))
NN = (((1,), (0,)), ((), ()))
VMEM = pl.BlockSpec(memory_space=pltpu.VMEM)
SMEM = pl.BlockSpec(memory_space=pltpu.SMEM)
HBM = pl.BlockSpec(memory_space=pltpu.HBM)


def facts(slot, order_ref, live_ref):
    n = lax.axis_size("seq")
    me = lax.axis_index("seq")
    crossed = (slot % 2 == 1) & (me % 2 == 0)
    hop = jnp.where(crossed, jnp.where(slot == 1, HOPS - 1, slot - 2), slot)
    own = order_ref[me]
    slab = order_ref[lax.rem(me - hop + n, n)]
    return slab - own, (slab <= own) & (live_ref[own, slab] == 1)


def mass_of(keys, q_ref, lse_ref, span):
    tokens = q_ref.shape[2]
    total = None
    for h in span[::2]:
        pair = jnp.concatenate([q_ref[h], q_ref[h + 1]], axis=1)
        s = lax.dot_general(keys, pair, NN, preferred_element_type=jnp.float32)
        s = s * (MAIN_SCALE * LOG2E)
        for n in range(2):
            lse = lse_ref[h + n : h + n + 1, :] * LOG2E
            p = jnp.exp2(s[:, n * tokens : (n + 1) * tokens] - lse)
            total = p if total is None else total + p
    return total


def cost(flops):
    return pl.CostEstimate(flops=flops, transcendentals=0, bytes_accessed=flops // 256)


def score_kernel(first, n_blocks, n_head, order_ref, live_ref, q_hbm, lse_ref, *refs):
    n_outs = n_head if n_blocks > 1 else 1
    blocks, known = refs[:n_blocks], refs[n_blocks : -n_outs - 4]
    outs, (q_ref, keys, mass, sems) = refs[-n_outs - 4 : -4], refs[-4:]
    heads, latent, tokens = q_ref.shape
    rows = blocks[0].shape[1]
    base = len(known)
    piece = max(2, heads // PIECES)
    spans = [range(h, h + piece) for h in range(0, heads, piece)]
    copies = []
    for i, span in enumerate(spans):
        part = pl.ds(span[0], piece)
        copies.append(pltpu.make_async_copy(q_hbm.at[part], q_ref.at[part], sems.at[i]))
        copies[i].start()
    for i in range(base):
        mass[i] = known[i][...]
    for i in range(n_blocks):
        keys[i] = blocks[i][:latent, :].T
    total = None
    for i, span in enumerate(spans):
        copies[i].wait()
        part = mass_of(keys[0], q_ref, lse_ref, span)
        total = part if total is None else total + part
    mass[base] = total

    def one_slot(i, carry):
        alive = facts(first + i, order_ref, live_ref)[1]

        @pl.when(alive)
        def _():
            mass[base + i] = mass_of(keys[i], q_ref, lse_ref, range(heads))

        @pl.when(jnp.logical_not(alive))
        def _():
            mass[base + i] = jnp.zeros((rows, tokens), jnp.float32)

        return carry

    if n_blocks == 1:
        outs[0][...] = total
        return
    lax.fori_loop(1, n_blocks, one_slot, 0)
    share = tokens // n_head
    turn = tokens - lax.axis_index("head") * share
    for c in range((base + n_blocks) // 2):
        pair = [pltpu.roll(mass[2 * c + n], turn, 1) if n_head > 1 else mass[2 * c + n] for n in range(2)]
        for n, out in enumerate(outs):
            span = slice(n * share, (n + 1) * share)
            out[c * rows : (c + 1) * rows, :] = jnp.concatenate([x[:, span] for x in pair], axis=1)


def head_mass(order, live, q, lse, blocks, known, first, n_head):
    heads, latent, tokens = q.shape
    rows = blocks[0].shape[1]
    share = tokens // n_head
    total = len(blocks) + len(known)
    shape = jax.ShapeDtypeStruct((total // 2 * rows, 2 * share), jnp.float32)
    shapes = [shape] * n_head
    if total == 1:
        shapes = [jax.ShapeDtypeStruct((rows, tokens), jnp.float32)]
    return pl.pallas_call(
        functools.partial(score_kernel, first, len(blocks), n_head),
        in_specs=[SMEM, SMEM, HBM] + [VMEM] * (1 + total),
        out_specs=[VMEM] * len(shapes),
        out_shape=shapes,
        scratch_shapes=[
            pltpu.VMEM(q.shape, q.dtype),
            pltpu.VMEM((len(blocks), rows, latent), jnp.bfloat16),
            pltpu.VMEM((total, rows, tokens), jnp.float32),
            pltpu.SemaphoreType.DMA((heads // max(2, heads // PIECES),)),
        ],
        cost_estimate=cost(2 * tokens * heads * latent * len(blocks) * rows),
        compiler_params=pltpu.CompilerParams(vmem_limit_bytes=WHOLE),
        name="score_mass",
    )(order, live, q, lse, *blocks, *known)


def lanes_of(part, share):
    return max(1, min(part.shape[0], 128 // share))


def pieces(part, share, width):
    side = lanes_of(part, share)
    step = part.shape[0] // side
    run = max(1, min(step, width))
    for first in range(0, step, run):
        heads = [part[k + n * step] for k in range(first, first + run) for n in range(side)]
        yield first, run, jnp.concatenate(heads, axis=0)


def lay_weights(parts, w_refs, w_lanes):
    at = 0
    for part, w_ref in zip(parts, w_refs):
        index_here, tokens = w_ref.shape
        share = part.shape[1]
        w = w_ref[...]
        if share < tokens:
            w = pltpu.roll(w, tokens - lax.axis_index("head") * share, 1)
        side = lanes_of(part, share)
        step = index_here // side
        tile = [w[n * step : (n + 1) * step, :share] for n in range(side)]
        w_lanes[at : at + step, :] = jnp.concatenate(tile, axis=1)
        at += step


def logit_kernel(latent, n_head, order_ref, live_ref, *refs):
    parts, w_refs, lse_ref = refs[:n_head], refs[n_head : 2 * n_head], refs[2 * n_head]
    blocks, (out_ref, w_ref, keys, values) = refs[2 * n_head + 1 : -4], refs[-4:]
    rows, idx_width = keys.shape[1:]
    share = parts[0].shape[1]
    scale = 1.0 / idx_width**0.5
    lay_weights(parts, w_refs, w_ref)
    tile = w_ref.shape[1]
    lse = lse_ref[...]
    if share < lse.shape[1]:
        lse = pltpu.roll(lse, lse.shape[1] - lax.axis_index("head") * share, 1)[:, :share]
    for i, block in enumerate(blocks):
        keys[i] = block[latent:, :]

    def one_slot(i, carry):
        @pl.when(facts(i, order_ref, live_ref)[1])
        def _():
            held = keys[i]
            acc = jnp.zeros((rows, tile), jnp.float32)
            at = 0
            for part in parts:
                for _, run, piece in pieces(part, share, 8):
                    r = lax.dot_general(held, piece, NT, preferred_element_type=jnp.float32)
                    for k in range(run):
                        relu = jnp.maximum(r[:, k * tile : (k + 1) * tile], 0.0)
                        acc = acc + relu * w_ref[at + k : at + k + 1, :]
                    at += run
            logits = acc[:, :share]
            for first in range(share, tile, share):
                logits = logits + acc[:, first : first + share]
            values[i] = jnp.exp(logits * scale - lse)

        return carry

    lax.fori_loop(0, len(blocks), one_slot, 0)
    for c in range(len(blocks) // 2):
        pair = [values[2 * c], values[2 * c + 1]]
        out_ref[c * rows : (c + 1) * rows, :] = jnp.concatenate(pair, axis=1)


def index_logits(order, live, parts, weights, lse, blocks, latent):
    n_head, (index_here, share, idx_width) = len(parts), parts[0].shape
    rows = blocks[0].shape[1]
    side = lanes_of(parts[0], share)
    return pl.pallas_call(
        functools.partial(logit_kernel, latent, n_head),
        in_specs=[SMEM, SMEM] + [VMEM] * (2 * n_head + 1 + len(blocks)),
        out_specs=VMEM,
        out_shape=jax.ShapeDtypeStruct((len(blocks) // 2 * rows, 2 * share), jnp.float32),
        scratch_shapes=[
            pltpu.VMEM((n_head * index_here // side, side * share), jnp.float32),
            pltpu.VMEM((len(blocks), rows, idx_width), jnp.bfloat16),
            pltpu.VMEM((len(blocks), rows, share), jnp.float32),
        ],
        cost_estimate=cost(2 * len(blocks) * rows * share * n_head * index_here * idx_width),
        compiler_params=pltpu.CompilerParams(vmem_limit_bytes=LIMIT),
        name="index_logits",
    )(order, live, *parts, *weights, lse, *blocks)


def grad_kernel(latent, first, n_head, order_ref, live_ref, *refs):
    parts, w_refs, masses = refs[:n_head], refs[n_head : 2 * n_head], refs[2 * n_head : 3 * n_head]
    target_ref, w_ref = refs[3 * n_head], refs[-1]
    n_blocks = (len(refs) - 3 * n_head - 2) // 2
    blocks, outs = refs[3 * n_head + 1 : -n_blocks - 1], refs[-n_blocks - 1 : -1]
    rows = blocks[0].shape[1]
    share, idx_width = parts[0].shape[1:]
    scale = 1.0 / idx_width**0.5
    lay_weights(parts, w_refs, w_ref)
    tile = w_ref.shape[1]
    start = lax.axis_index("head") * share
    for i in range(n_blocks):
        later, alive = facts(first + i, order_ref, live_ref)

        @pl.when(alive)
        def _(i=i, later=later):
            here = slice(i // 2 * rows, (i // 2 + 1) * rows)
            span = slice(i % 2 * share, (i % 2 + 1) * share)
            mass = masses[0][here, span]
            for other in masses[1:]:
                mass = mass + other[here, span]
            at = (first + i) // 2 * rows
            value = target_ref[at : at + rows, span] - mass * (1.0 / HEADS)
            within = lax.broadcasted_iota(jnp.int32, (rows, share), 0)
            token = lax.broadcasted_iota(jnp.int32, (rows, share), 1) + start
            grad = jnp.where(within + later * rows <= token, value, 0.0)
            grad = jnp.concatenate([grad] * (tile // share), axis=1)
            held = blocks[i][latent:, :]
            total = jnp.zeros((rows, idx_width), jnp.float32)
            at = 0
            for part in parts:
                for _, run, piece in pieces(part, share, 8):
                    r = lax.dot_general(held, piece, NT, preferred_element_type=jnp.float32)
                    weighted = []
                    for k in range(run):
                        w = grad * w_ref[at + k : at + k + 1, :]
                        w = jnp.where(r[:, k * tile : (k + 1) * tile] > 0.0, w, 0.0)
                        weighted.append(w.astype(jnp.bfloat16))
                    at += run
                    total = total + lax.dot_general(
                        jnp.concatenate(weighted, axis=1),
                        piece,
                        NN,
                        preferred_element_type=jnp.float32,
                    )
            outs[i][...] = total * scale

        @pl.when(jnp.logical_not(alive))
        def _(i=i):
            outs[i][...] = jnp.zeros((rows, idx_width), jnp.float32)


def index_grad(order, live, parts, weights, masses, target, blocks, first, latent):
    n_head, (index_here, share, idx_width) = len(parts), parts[0].shape
    rows = blocks[0].shape[1]
    side = lanes_of(parts[0], share)
    return pl.pallas_call(
        functools.partial(grad_kernel, latent, first, n_head),
        in_specs=[SMEM, SMEM] + [VMEM] * (3 * n_head + 1 + len(blocks)),
        out_specs=[VMEM] * len(blocks),
        out_shape=[jax.ShapeDtypeStruct((rows, idx_width), jnp.float32)] * len(blocks),
        scratch_shapes=[pltpu.VMEM((n_head * index_here // side, side * share), jnp.float32)],
        cost_estimate=cost(4 * len(blocks) * rows * share * n_head * index_here * idx_width),
        compiler_params=pltpu.CompilerParams(vmem_limit_bytes=LIMIT),
        name="index_grad",
    )(order, live, *parts, *weights, *masses, target, *blocks)


def body(
    q_main,
    latent_keys,
    lse_main,
    index_queries,
    index_weights,
    index_keys,
    lse_index,
    slab_order,
    block_live,
):
    n_seq = lax.axis_size("seq")
    n_head = lax.axis_size("head")
    head_place = lax.axis_index("head")
    latent = latent_keys.shape[1]
    share = q_main.shape[0] // n_head
    devices = range(n_seq)

    def ring(distance):
        return [(i, (i + distance) % n_seq) for i in devices]

    def around(array, turn):
        return lax.ppermute(array, "head", [(i, (i + turn) % n_head) for i in range(n_head)])

    forward = [(i, (i + (HOPS - 1 if i % 2 else 1)) % n_seq) for i in devices]
    back = [(b, a) for a, b in forward]
    swap = [(i, i ^ 1) for i in devices]
    own = jnp.concatenate([latent_keys.T, index_keys], axis=0)
    arrived = [lax.ppermute(own, "seq", ring(2))]
    arrived.append(lax.ppermute(own, "seq", ring(4)))
    slots = [own, lax.ppermute(own, "seq", forward)]
    for m in range(1, HOPS // 2):
        if m > 2:
            arrived.append(lax.ppermute(arrived[m - 3], "seq", ring(4)))
        slots += [arrived[m - 1], lax.ppermute(arrived[m - 1], "seq", swap)]

    def to_share(array, turn):
        start = lax.rem(head_place + turn, n_head) * share
        part = lax.dynamic_slice_in_dim(array, start, share, 0)
        return part if turn == 0 else around(part, turn)

    turns = range(n_head)
    weights = [around(index_weights.T, turn) if turn else index_weights.T for turn in turns]
    parts = [to_share(index_queries, turn).transpose(1, 0, 2) for turn in turns]

    tables = slab_order, block_live
    lse = lse_main.T
    early = HOPS - LAST
    q = q_main.transpose(1, 2, 0)
    near = head_mass(*tables, q, lse, slots[:1], [], 0, n_head)
    masses = [
        list(head_mass(*tables, q, lse, slots[1:early], near, 1, n_head)),
        list(head_mass(*tables, q, lse, slots[early:], [], early, n_head)),
    ]
    for group in masses:
        for turn in range(1, n_head):
            group[turn] = around(group[turn], turn)
    target = index_logits(*tables, parts, weights, lse_index[None, :], slots, latent)
    grads = []
    for group, first, end in ((masses[0], 0, early), (masses[1], early, HOPS)):
        grads += index_grad(
            *tables, parts, weights, group, target, slots[first:end], first, latent
        )

    total = grads[0] + lax.ppermute(grads[1], "seq", back)
    for m in range(1, HOPS // 2):
        both = grads[2 * m] + lax.ppermute(grads[2 * m + 1], "seq", swap)
        if n_head == 2 and m == HOPS // 2 - 1:
            break
        total = total + lax.ppermute(both, "seq", ring(-2 * m))
    if n_head != 2:
        return lax.psum(total, "head")
    straight, across = [], []
    for i in devices:
        for x in range(2):
            goal = (i - 2 * m) % n_seq
            straight.append((2 * i + x, 2 * goal + x))
            across.append((2 * i + x, 2 * goal + 1 - x))
    axes = ("seq", "head")
    last = lax.ppermute(both, axes, straight) + lax.ppermute(both, axes, across)
    return total + around(total, 1) + last


def solution(mesh):
    placed = (
        P("seq", "head", None),
        P("seq", None),
        P("seq", "head"),
        P("seq", "head", None),
        P("seq", "head"),
        P("seq", None),
        P("seq"),
        P(),
        P(),
    )
    return jax.shard_map(
        body, mesh=mesh, in_specs=placed, out_specs=P("seq", None), check_vma=False
    )
```

profile of v0, /device:TPU:0, one launch (start us, length us, event | category | flops | bytes accessed | tf_op | source)
XLA Modules:
  0.0 77.0 jit_solution(1209272227904539751)
XLA Ops:
  0.0 0.0 copy-start.3
  0.0 1.0 %pad_maximum_fusion.refs_0_.refs_5_.refs_7_ = bf16[704,128]{1,0:T(8,128)(2,1)S(1)} fusion(bf16[128,128]{1,0:T(8,128)(2,1)} %param.14, bf16[576,128]{1,0:T(8,128)(2,1)} %bitcast.26), kind=kLoop, calls=%fused_computation.1 | loop fusion | flops 360448 | bytes 360448 | tf_op jit(solution)/shard_map/concatenate | solution.py:315
  1.0 3.0 %collective-permute-start.3 = (bf16[704,128]{1,0:T(8,128)(2,1)S(1)}, bf16[704,128]{1,0:T(8,128)(2,1)S(1)}, u32[]{:S(2)}, u32[]{:S(2)}) collective-permute-start(bf16[704,128]{1,0:T(8,128)(2,1)S(1)} %pad_maximum_fusion.refs_0_.refs_5_.refs_7_), channel_id=1, source_target_pairs={{0,4},{2,6},{4,8},{6,10},{8,12},{10,14},{12,16},{14,18},{16,20},{1... | collective-permute-start | bytes 540680 | tf_op jit(solution)/shard_map/ppermute | solution.py:316
  4.0 1.6 %collective-permute-start.5 = (bf16[704,128]{1,0:T(8,128)(2,1)S(1)}, bf16[704,128]{1,0:T(8,128)(2,1)S(1)}, u32[]{:S(2)}, u32[]{:S(2)}) collective-permute-start(bf16[704,128]{1,0:T(8,128)(2,1)S(1)} %pad_maximum_fusion.refs_0_.refs_5_.refs_7_), channel_id=1, source_target_pairs={{0,8},{2,10},{4,12},{6,14},{8,16},{10,18},{12,20},{14,22},{16,24},... | collective-permute-start | bytes 540680 | tf_op jit(solution)/shard_map/ppermute | solution.py:317
  5.6 0.0 collective-permute-start.2
  5.6 7.0 %collective-permute-done.3.refs_1_.refs_7_.refs_9_ = bf16[704,128]{1,0:T(8,128)(2,1)S(1)} collective-permute-done((bf16[704,128]{1,0:T(8,128)(2,1)S(1)}, bf16[704,128]{1,0:T(8,128)(2,1)S(1)}, u32[]{:S(2)}, u32[]{:S(2)}) %collective-permute-start.3) | collective-permute-done | bytes 180256 | tf_op jit(solution)/shard_map/ppermute | solution.py:316
  12.5 0.0 collective-permute-start.8
  12.6 0.0 collective-permute-start.4
  12.6 0.8 %collective-permute-done.5.refs_3_.refs_9_.refs_11_ = bf16[704,128]{1,0:T(8,128)(2,1)S(1)} collective-permute-done((bf16[704,128]{1,0:T(8,128)(2,1)S(1)}, bf16[704,128]{1,0:T(8,128)(2,1)S(1)}, u32[]{:S(2)}, u32[]{:S(2)}) %collective-permute-start.5) | collective-permute-done | bytes 180256 | tf_op jit(solution)/shard_map/ppermute | solution.py:317
  13.3 0.0 collective-permute-start.6
  13.3 1.3 %constant_dynamic-slice_fusion = (bf16[64,32,128]{2,1,0:T(8,128)(2,1)S(1)}, bf16[64,32,128]{2,1,0:T(8,128)(2,1)S(1)}) fusion(bf16[128,32,128]{2,1,0:T(8,128)(2,1)} %param.12, s32[]{:T(128)S(6)} %select_n.7, s32[]{:T(128)S(6)} %select_n.6), kind=kLoop, calls=%fused_computation.4 | loop fusion | bytes 2097160 | tf_op jit(solution)/shard_map/dynamic_slice | solution.py:326
  14.6 0.2 copy.13
  14.8 1.6 %collective-permute-start = (bf16[64,32,128]{2,0,1:T(8,128)(2,1)S(1)}, bf16[64,32,128]{2,0,1:T(8,128)(2,1)S(1)}, u32[]{:S(2)}, u32[]{:S(2)}) collective-permute-start(bf16[64,32,128]{2,0,1:T(8,128)(2,1)S(1)} %copy.13), channel_id=1, source_target_pairs={{0,1},{1,0},{2,3},{3,2},{4,5},{5,4},{6,7},{7,6},{8,9},{9,8},{10,11... | collective-permute-start | bytes 1572872 | tf_op jit(solution)/shard_map/ppermute | solution.py:310
  16.4 0.2 copy.15
  16.6 0.0 copy-start
  16.6 0.7 copy-done
  17.3 0.0 copy-start.1
  17.3 0.7 copy-done.1
  18.0 0.0 copy-start.2
  18.0 0.7 copy-done.2
  18.7 5.1 %score_mass.3.refs_5_ = f32[128,128]{1,0:T(8,128)S(1)} custom-call(s32[16]{0:T(128)S(1)} %copy-done.2, s32[16,16]{1,0:T(8,128)S(1)} %copy-done.1, bf16[64,576,128]{2,1,0:T(8,128)(2,1)} %bitcast.23, f32[64,128]{1,0:T(8,128)S(1)} %bitcast.12, bf16[704,128]{1,0:T(8,128)(2,1)S(1)} %pad_maximum_fusion.refs_0_.refs_5_.refs_7_), custom_call_target="tpu_custom_call" | custom-call | flops 1207959552 | bytes 4718592 | tf_op jit(solution)/shard_map/score_mass/pallas_call | solution.py:115
  23.8 0.0 collective-permute-done.2.refs_0_.refs_6_.refs_8_
  23.8 0.0 copy-done.3
  23.8 0.6 collective-permute-start.1
  24.4 0.0 collective-permute-done.8.refs_11_.refs_0_.refs_7_
  24.4 0.0 collective-permute-start.9
  24.4 0.0 collective-permute-done.4.refs_2_.refs_8_.refs_10_
  24.4 0.0 collective-permute-done.6.refs_4_.refs_10_.refs_12_
  24.4 7.5 %score_mass.4 = (f32[384,128]{1,0:T(8,128)S(1)}, f32[384,128]{1,0:T(8,128)S(1)}) custom-call(s32[16]{0:T(128)S(1)} %copy-done.2, s32[16,16]{1,0:T(8,128)S(1)} %copy-done.1, bf16[64,576,128]{2,1,0:T(8,128)(2,1)} %bitcast.24, f32[64,128]{1,0:T(8,128)S(1)} %bitcast.13, bf16[704,128]{1,0:T(8,128)(2,1)S(1)} %collective-permute-done.2.refs_0_.refs_6_.refs_8_, ...), custom_call_target="tpu_custom_call" | custom-call | flops 6039797760 | bytes 23592960 | tf_op jit(solution)/shard_map/score_mass/pallas_call | solution.py:115
  31.9 0.0 copy-start.4
  32.0 1.6 %collective-permute-start.7 = (f32[384,128]{1,0:T(8,128)S(1)}, f32[384,128]{1,0:T(8,128)S(1)}, u32[]{:S(2)}, u32[]{:S(2)}) collective-permute-start(f32[384,128]{1,0:T(8,128)S(1)} %get-tuple-element.18), channel_id=1, source_target_pairs={{0,1},{1,0},{2,3},{3,2},{4,5},{5,4},{6,7},{7,6},{8,9},{9,8},{10,11... | collective-permute-start | bytes 589832 | tf_op jit(solution)/shard_map/ppermute | solution.py:310
  33.5 0.0 collective-permute-done.9.refs_12_.refs_1_.refs_8_
  33.5 5.5 %score_mass.5 = (f32[128,128]{1,0:T(8,128)S(1)}, f32[128,128]{1,0:T(8,128)S(1)}) custom-call(s32[16]{0:T(128)S(1)} %copy-done.2, s32[16,16]{1,0:T(8,128)S(1)} %copy-done.1, bf16[64,576,128]{2,1,0:T(8,128)(2,1)} %bitcast.25, f32[64,128]{1,0:T(8,128)S(1)} %bitcast.14, bf16[704,128]{1,0:T(8,128)(2,1)S(1)} %collective-permute-done.8.refs_11_.refs_0_.refs_7_, ...), custom_call_target="tpu_custom_call" | custom-call | flops 2415919104 | bytes 9437184 | tf_op jit(solution)/shard_map/score_mass/pallas_call | solution.py:115
  39.0 0.6 collective-permute-start.16
  39.6 0.0 collective-permute-done.1.refs_3_
  39.6 0.0 collective-permute-done
  39.6 0.0 copy-done.4
  39.6 2.2 %index_logits.1.refs_6_ = f32[512,128]{1,0:T(8,128)S(1)} custom-call(s32[16]{0:T(128)S(1)} %copy-done.2, s32[16,16]{1,0:T(8,128)S(1)} %copy-done.1, bf16[32,64,128]{2,1,0:T(8,128)(2,1)S(1)} %bitcast.9, bf16[32,64,128]{2,1,0:T(8,128)(2,1)S(1)} %bitcast.15, f32[32,128]{1,0:T(8,128)S(1)} %bitcast.19, f32[32,128]{1,0:T(8,128)S(1)} %collective-permute-done.1.refs_3_, ...), custom_call_target="tpu_custom_call" | custom-call | flops 1073741824 | bytes 4194304 | tf_op jit(solution)/shard_map/index_logits/pallas_call | solution.py:204
  41.8 0.0 collective-permute-done.7.refs_5_
  41.8 2.8 %index_grad.2 = (f32[128,128]{1,0:T(8,128)S(1)}, f32[128,128]{1,0:T(8,128)S(1)}, f32[128,128]{1,0:T(8,128)S(1)}, f32[128,128]{1,0:T(8,128)S(1)}, f32[128,128]{1,0:T(8,128)S(1)}, /*index=5*/f32[128,128]{1,0:T(8,128)S(1)}) custom-call(s32[16]{0:T(128)S(1)} %copy-done.2, s32[16,16]{1,0:T(8,128)S(1)} %copy-done.1, bf16[32,64,128]{2,1,0:T(8,128)(2,1)S(1)} %bitcast.10, ...), custom_call_target="tpu_custom_call" | custom-call | flops 1610612736 | bytes 6291456 | tf_op jit(solution)/shard_map/index_grad/pallas_call | solution.py:276
  44.7 0.1 collective-permute-start.13
  44.8 0.5 collective-permute-start.11
  45.3 7.0 %collective-permute-start.10 = (f32[128,128]{1,0:T(8,128)S(1)}, f32[128,128]{1,0:T(8,128)S(1)}, u32[]{:S(2)}, u32[]{:S(2)}) collective-permute-start(f32[128,128]{1,0:T(8,128)S(1)} %get-tuple-element.20), channel_id=1, source_target_pairs={{2,0},{16,2},{6,4},{20,6},{10,8},{24,10},{14,12},{28,14},{18,16},{... | collective-permute-start | bytes 196616 | tf_op jit(solution)/shard_map/ppermute | solution.py:352
  52.3 0.0 collective-permute-done.16.refs_5_
  52.3 0.8 %index_grad.3 = (f32[128,128]{1,0:T(8,128)S(1)}, f32[128,128]{1,0:T(8,128)S(1)}) custom-call(s32[16]{0:T(128)S(1)} %copy-done.2, s32[16,16]{1,0:T(8,128)S(1)} %copy-done.1, bf16[32,64,128]{2,1,0:T(8,128)(2,1)S(1)} %bitcast.11, bf16[32,64,128]{2,1,0:T(8,128)(2,1)S(1)} %bitcast.17, f32[32,128]{1,0:T(8,128)S(1)} %bitcast.21, ...), custom_call_target="tpu_custom_call" | custom-call | flops 536870912 | bytes 2097152 | tf_op jit(solution)/shard_map/index_grad/pallas_call | solution.py:276
  53.1 0.1 collective-permute-start.17
  53.2 0.0 collective-permute-done.13
  53.2 6.0 %collective-permute-start.14 = (f32[128,128]{1,0:T(8,128)S(1)}, f32[128,128]{1,0:T(8,128)S(1)}, u32[]{:S(2)}, u32[]{:S(2)}) collective-permute-start(f32[128,128]{1,0:T(8,128)S(1)} %add.42), channel_id=1, source_target_pairs={{0,24},{2,26},{4,28},{6,30},{8,0},{10,2},{12,4},{14,6},{16,8},{18,... | collective-permute-start | bytes 196616 | tf_op jit(solution)/shard_map/ppermute | solution.py:357
  59.2 0.0 collective-permute-done.11
  59.2 8.9 %collective-permute-start.12 = (f32[128,128]{1,0:T(8,128)S(1)}, f32[128,128]{1,0:T(8,128)S(1)}, u32[]{:S(2)}, u32[]{:S(2)}) collective-permute-start(f32[128,128]{1,0:T(8,128)S(1)} %add.40), channel_id=1, source_target_pairs={{0,28},{2,30},{4,0},{6,2},{8,4},{10,6},{12,8},{14,10},{16,12},{18,... | collective-permute-start | bytes 196616 | tf_op jit(solution)/shard_map/ppermute | solution.py:357
  68.1 0.0 collective-permute-done.17
  68.1 0.1 collective-permute-start.18
  68.2 3.6 %collective-permute-start.19 = (f32[128,128]{1,0:T(8,128)S(1)}, f32[128,128]{1,0:T(8,128)S(1)}, u32[]{:S(2)}, u32[]{:S(2)}) collective-permute-start(f32[128,128]{1,0:T(8,128)S(1)} %add.45), channel_id=1, source_target_pairs={{0,21},{1,20},{2,23},{3,22},{4,25},{5,24},{6,27},{7,26},{8,29},{9,... | collective-permute-start | bytes 196616 | tf_op jit(solution)/shard_map/ppermute | solution.py:367
  71.8 0.0 collective-permute-done.10
  71.8 0.0 collective-permute-done.14
  71.8 0.0 collective-permute-done.12
  71.8 0.6 collective-permute-start.15
  72.4 1.8 %collective-permute-done.18 = f32[128,128]{1,0:T(8,128)S(1)} collective-permute-done((f32[128,128]{1,0:T(8,128)S(1)}, f32[128,128]{1,0:T(8,128)S(1)}, u32[]{:S(2)}, u32[]{:S(2)}) %collective-permute-start.18) | collective-permute-done | bytes 65568 | tf_op jit(solution)/shard_map/ppermute | solution.py:367
  74.2 1.2 %collective-permute-done.19 = f32[128,128]{1,0:T(8,128)S(1)} collective-permute-done((f32[128,128]{1,0:T(8,128)S(1)}, f32[128,128]{1,0:T(8,128)S(1)}, u32[]{:S(2)}, u32[]{:S(2)}) %collective-permute-start.19) | collective-permute-done | bytes 65568 | tf_op jit(solution)/shard_map/ppermute | solution.py:367
  75.4 0.9 %collective-permute-done.15 = f32[128,128]{1,0:T(8,128)S(1)} collective-permute-done((f32[128,128]{1,0:T(8,128)S(1)}, f32[128,128]{1,0:T(8,128)S(1)}, u32[]{:S(2)}, u32[]{:S(2)}) %collective-permute-start.15) | collective-permute-done | bytes 65568 | tf_op jit(solution)/shard_map/ppermute | solution.py:310
  76.3 0.6 add_add_fusion
  (4 shorter events, 0.0 us)
Async XLA Ops:
  0.0 23.8 %copy-start.3 = (f32[128,32]{0,1:T(8,128)S(1)}, f32[128,32]{0,1:T(8,128)}, u32[]{:S(2)}) copy-start(f32[128,32]{0,1:T(8,128)} %param.13) | copy-start | bytes 49156
  1.0 11.6 %collective-permute-start.3 = (bf16[704,128]{1,0:T(8,128)(2,1)S(1)}, bf16[704,128]{1,0:T(8,128)(2,1)S(1)}, u32[]{:S(2)}, u32[]{:S(2)}) collective-permute-start(bf16[704,128]{1,0:T(8,128)(2,1)S(1)} %pad_maximum_fusion.refs_0_.refs_5_.refs_7_), channel_id=1, source_target_pairs={{0,4},{2,6},{4,8},{6,10},{8,12},{10,14},{12,16},{14,18},{16,20},{1... | collective-permute-start | bytes 540680 | tf_op jit(solution)/shard_map/ppermute | solution.py:316
  4.0 9.3 %collective-permute-start.5 = (bf16[704,128]{1,0:T(8,128)(2,1)S(1)}, bf16[704,128]{1,0:T(8,128)(2,1)S(1)}, u32[]{:S(2)}, u32[]{:S(2)}) collective-permute-start(bf16[704,128]{1,0:T(8,128)(2,1)S(1)} %pad_maximum_fusion.refs_0_.refs_5_.refs_7_), channel_id=1, source_target_pairs={{0,8},{2,10},{4,12},{6,14},{8,16},{10,18},{12,20},{14,22},{16,24},... | collective-permute-start | bytes 540680 | tf_op jit(solution)/shard_map/ppermute | solution.py:317
  5.6 18.2 %collective-permute-start.2 = (bf16[704,128]{1,0:T(8,128)(2,1)S(1)}, bf16[704,128]{1,0:T(8,128)(2,1)S(1)}, u32[]{:S(2)}, u32[]{:S(2)}) collective-permute-start(bf16[704,128]{1,0:T(8,128)(2,1)S(1)} %pad_maximum_fusion.refs_0_.refs_5_.refs_7_), channel_id=1, source_target_pairs={{0,2},{2,16},{4,6},{6,20},{8,10},{10,24},{12,14},{14,28},{16,18},{... | collective-permute-start | bytes 540680 | tf_op jit(solution)/shard_map/ppermute | solution.py:318
  12.5 11.9 %collective-permute-start.8 = (bf16[704,128]{1,0:T(8,128)(2,1)S(1)}, bf16[704,128]{1,0:T(8,128)(2,1)S(1)}, u32[]{:S(2)}, u32[]{:S(2)}) collective-permute-start(bf16[704,128]{1,0:T(8,128)(2,1)S(1)} %collective-permute-done.3.refs_1_.refs_7_.refs_9_), channel_id=1, source_target_pairs={{0,8},{2,10},{4,12},{6,14},{8,16},{10,18},{12,20},{14,22},{16,24},... | collective-permute-start | bytes 540680 | tf_op jit(solution)/shard_map/ppermute | solution.py:321
  12.6 11.9 %collective-permute-start.4 = (bf16[704,128]{1,0:T(8,128)(2,1)S(1)}, bf16[704,128]{1,0:T(8,128)(2,1)S(1)}, u32[]{:S(2)}, u32[]{:S(2)}) collective-permute-start(bf16[704,128]{1,0:T(8,128)(2,1)S(1)} %collective-permute-done.3.refs_1_.refs_7_.refs_9_), channel_id=1, source_target_pairs={{0,2},{2,0},{4,6},{6,4},{8,10},{10,8},{12,14},{14,12},{16,18},{18,... | collective-permute-start | bytes 540680 | tf_op jit(solution)/shard_map/ppermute | solution.py:322
  13.3 11.1 %collective-permute-start.6 = (bf16[704,128]{1,0:T(8,128)(2,1)S(1)}, bf16[704,128]{1,0:T(8,128)(2,1)S(1)}, u32[]{:S(2)}, u32[]{:S(2)}) collective-permute-start(bf16[704,128]{1,0:T(8,128)(2,1)S(1)} %collective-permute-done.5.refs_3_.refs_9_.refs_11_), channel_id=1, source_target_pairs={{0,2},{2,0},{4,6},{6,4},{8,10},{10,8},{12,14},{14,12},{16,18},{18,... | collective-permute-start | bytes 540680 | tf_op jit(solution)/shard_map/ppermute | solution.py:322
  14.8 24.8 %collective-permute-start = (bf16[64,32,128]{2,0,1:T(8,128)(2,1)S(1)}, bf16[64,32,128]{2,0,1:T(8,128)(2,1)S(1)}, u32[]{:S(2)}, u32[]{:S(2)}) collective-permute-start(bf16[64,32,128]{2,0,1:T(8,128)(2,1)S(1)} %copy.13), channel_id=1, source_target_pairs={{0,1},{1,0},{2,3},{3,2},{4,5},{5,4},{6,7},{7,6},{8,9},{9,8},{10,11... | collective-permute-start | bytes 1572872 | tf_op jit(solution)/shard_map/ppermute | solution.py:310
  16.6 0.8 copy-start
  17.3 0.7 copy-start.1
  18.0 0.7 copy-start.2
  23.8 15.8 %collective-permute-start.1 = (f32[32,128]{1,0:T(8,128)S(1)}, f32[32,128]{1,0:T(8,128)S(1)}, u32[]{:S(2)}, u32[]{:S(2)}) collective-permute-start(f32[32,128]{1,0:T(8,128)S(1)} %bitcast.18), channel_id=1, source_target_pairs={{0,1},{1,0},{2,3},{3,2},{4,5},{5,4},{6,7},{7,6},{8,9},{9,8},{10,11... | collective-permute-start | bytes 49160 | tf_op jit(solution)/shard_map/ppermute | solution.py:310
  24.4 9.1 %collective-permute-start.9 = (bf16[704,128]{1,0:T(8,128)(2,1)S(1)}, bf16[704,128]{1,0:T(8,128)(2,1)S(1)}, u32[]{:S(2)}, u32[]{:S(2)}) collective-permute-start(bf16[704,128]{1,0:T(8,128)(2,1)S(1)} %collective-permute-done.8.refs_11_.refs_0_.refs_7_), channel_id=1, source_target_pairs={{0,2},{2,0},{4,6},{6,4},{8,10},{10,8},{12,14},{14,12},{16,18},{18,... | collective-permute-start | bytes 540680 | tf_op jit(solution)/shard_map/ppermute | solution.py:322
  31.9 7.7 %copy-start.4 = (f32[128]{0:T(128)S(1)}, f32[128]{0:T(128)}, u32[]{:S(2)}) copy-start(f32[128]{0:T(128)} %param.15) | copy-start | bytes 1540
  32.0 9.9 %collective-permute-start.7 = (f32[384,128]{1,0:T(8,128)S(1)}, f32[384,128]{1,0:T(8,128)S(1)}, u32[]{:S(2)}, u32[]{:S(2)}) collective-permute-start(f32[384,128]{1,0:T(8,128)S(1)} %get-tuple-element.18), channel_id=1, source_target_pairs={{0,1},{1,0},{2,3},{3,2},{4,5},{5,4},{6,7},{7,6},{8,9},{9,8},{10,11... | collective-permute-start | bytes 589832 | tf_op jit(solution)/shard_map/ppermute | solution.py:310
  39.0 13.3 %collective-permute-start.16 = (f32[128,128]{1,0:T(8,128)S(1)}, f32[128,128]{1,0:T(8,128)S(1)}, u32[]{:S(2)}, u32[]{:S(2)}) collective-permute-start(f32[128,128]{1,0:T(8,128)S(1)} %get-tuple-element.26), channel_id=1, source_target_pairs={{0,1},{1,0},{2,3},{3,2},{4,5},{5,4},{6,7},{7,6},{8,9},{9,8},{10,11... | collective-permute-start | bytes 196616 | tf_op jit(solution)/shard_map/ppermute | solution.py:310
  44.7 8.5 %collective-permute-start.13 = (f32[128,128]{1,0:T(8,128)S(1)}, f32[128,128]{1,0:T(8,128)S(1)}, u32[]{:S(2)}, u32[]{:S(2)}) collective-permute-start(f32[128,128]{1,0:T(8,128)S(1)} %get-tuple-element.24), channel_id=1, source_target_pairs={{0,2},{2,0},{4,6},{6,4},{8,10},{10,8},{12,14},{14,12},{16,18},{18,... | collective-permute-start | bytes 196616 | tf_op jit(solution)/shard_map/ppermute | solution.py:354
  44.8 14.5 %collective-permute-start.11 = (f32[128,128]{1,0:T(8,128)S(1)}, f32[128,128]{1,0:T(8,128)S(1)}, u32[]{:S(2)}, u32[]{:S(2)}) collective-permute-start(f32[128,128]{1,0:T(8,128)S(1)} %get-tuple-element.22), channel_id=1, source_target_pairs={{0,2},{2,0},{4,6},{6,4},{8,10},{10,8},{12,14},{14,12},{16,18},{18,... | collective-permute-start | bytes 196616 | tf_op jit(solution)/shard_map/ppermute | solution.py:354
  45.3 26.5 %collective-permute-start.10 = (f32[128,128]{1,0:T(8,128)S(1)}, f32[128,128]{1,0:T(8,128)S(1)}, u32[]{:S(2)}, u32[]{:S(2)}) collective-permute-start(f32[128,128]{1,0:T(8,128)S(1)} %get-tuple-element.20), channel_id=1, source_target_pairs={{2,0},{16,2},{6,4},{20,6},{10,8},{24,10},{14,12},{28,14},{18,16},{... | collective-permute-start | bytes 196616 | tf_op jit(solution)/shard_map/ppermute | solution.py:352
  53.1 15.0 %collective-permute-start.17 = (f32[128,128]{1,0:T(8,128)S(1)}, f32[128,128]{1,0:T(8,128)S(1)}, u32[]{:S(2)}, u32[]{:S(2)}) collective-permute-start(f32[128,128]{1,0:T(8,128)S(1)} %get-tuple-element.28), channel_id=1, source_target_pairs={{0,2},{2,0},{4,6},{6,4},{8,10},{10,8},{12,14},{14,12},{16,18},{18,... | collective-permute-start | bytes 196616 | tf_op jit(solution)/shard_map/ppermute | solution.py:354
  53.2 18.6 %collective-permute-start.14 = (f32[128,128]{1,0:T(8,128)S(1)}, f32[128,128]{1,0:T(8,128)S(1)}, u32[]{:S(2)}, u32[]{:S(2)}) collective-permute-start(f32[128,128]{1,0:T(8,128)S(1)} %add.42), channel_id=1, source_target_pairs={{0,24},{2,26},{4,28},{6,30},{8,0},{10,2},{12,4},{14,6},{16,8},{18,... | collective-permute-start | bytes 196616 | tf_op jit(solution)/shard_map/ppermute | solution.py:357
  59.2 12.5 %collective-permute-start.12 = (f32[128,128]{1,0:T(8,128)S(1)}, f32[128,128]{1,0:T(8,128)S(1)}, u32[]{:S(2)}, u32[]{:S(2)}) collective-permute-start(f32[128,128]{1,0:T(8,128)S(1)} %add.40), channel_id=1, source_target_pairs={{0,28},{2,30},{4,0},{6,2},{8,4},{10,6},{12,8},{14,10},{16,12},{18,... | collective-permute-start | bytes 196616 | tf_op jit(solution)/shard_map/ppermute | solution.py:357
  68.1 6.1 %collective-permute-start.18 = (f32[128,128]{1,0:T(8,128)S(1)}, f32[128,128]{1,0:T(8,128)S(1)}, u32[]{:S(2)}, u32[]{:S(2)}) collective-permute-start(f32[128,128]{1,0:T(8,128)S(1)} %add.45), channel_id=1, source_target_pairs={{0,20},{1,21},{2,22},{3,23},{4,24},{5,25},{6,26},{7,27},{8,28},{9,... | collective-permute-start | bytes 196616 | tf_op jit(solution)/shard_map/ppermute | solution.py:367
  68.2 7.2 %collective-permute-start.19 = (f32[128,128]{1,0:T(8,128)S(1)}, f32[128,128]{1,0:T(8,128)S(1)}, u32[]{:S(2)}, u32[]{:S(2)}) collective-permute-start(f32[128,128]{1,0:T(8,128)S(1)} %add.45), channel_id=1, source_target_pairs={{0,21},{1,20},{2,23},{3,22},{4,25},{5,24},{6,27},{7,26},{8,29},{9,... | collective-permute-start | bytes 196616 | tf_op jit(solution)/shard_map/ppermute | solution.py:367
  71.8 4.5 %collective-permute-start.15 = (f32[128,128]{1,0:T(8,128)S(1)}, f32[128,128]{1,0:T(8,128)S(1)}, u32[]{:S(2)}, u32[]{:S(2)}) collective-permute-start(f32[128,128]{1,0:T(8,128)S(1)} %add_add_fusion.1), channel_id=1, source_target_pairs={{0,1},{1,0},{2,3},{3,2},{4,5},{5,4},{6,7},{7,6},{8,9},{9,8},{10,11... | collective-permute-start | bytes 196616 | tf_op jit(solution)/shard_map/ppermute | solution.py:310
where the time goes:
time: 78 us; the launch traced here: 77 us
  starting transfers between devices  35.7 us (46%)
  Pallas kernels  23.9 us (31%)
  waiting for transfers between devices  11.6 us (15%)
  local copies, waits for them, and re-layouts  3.79 us (5%)
  other arithmetic  1.65 us (2%)
    pallas_call x3, Pallas kernels, head_mass(): pl.pallas_call(functools.partial(score_kernel, first, len(blocks), n_head...  18.1 us
    ppermute x2, starting transfers between devices, body(): total = total + lax.ppermute(both, 'seq', ring(-2 * m))  14.9 us
    ppermute x1, starting transfers between devices, body(): total = grads[0] + lax.ppermute(grads[1], 'seq', back)  7 us
    ppermute x1, waiting for transfers between devices, body(): arrived = [lax.ppermute(own, 'seq', ring(2))]  6.96 us
    ppermute x5, starting transfers between devices, around(): lax.ppermute(array, 'head', [(i, (i + turn) % n_head) for i in range(n_he...  4.93 us
    pallas_call x2, Pallas kernels, index_grad(): pl.pallas_call(functools.partial(grad_kernel, latent, first, n_head), in_...  3.67 us
    ppermute x2, starting transfers between devices, body(): last = lax.ppermute(both, axes, straight) + lax.ppermute(both, axes, across)  3.62 us
    ppermute x1, starting transfers between devices, body(): arrived = [lax.ppermute(own, 'seq', ring(2))]  3.05 us
  transfers between devices with their start and end apart: 20, of which 5 were waited for; matrix products, arithmetic and copies ran while one was open for 2% of the time, Pallas kernels for 31%

commit v1 on v0

v1 whole, which is shorter than its diff:
```python
import functools
import math

import jax
import jax.numpy as jnp
from jax import lax
from jax.experimental import pallas as pl
from jax.experimental.pallas import tpu as pltpu
from jax.sharding import PartitionSpec as P


HEADS = 128
HOPS = 8
LAST = 2
LOG2E = math.log2(math.e)
MAIN_SCALE = 1.0 / 192.0**0.5
LIMIT = 20 * 2**20
NT = (((1,), (1,)), ((), ()))
NN = (((1,), (0,)), ((), ()))
VMEM = pl.BlockSpec(memory_space=pltpu.VMEM)
SMEM = pl.BlockSpec(memory_space=pltpu.SMEM)


def facts(slot, order_ref, live_ref):
    n = lax.axis_size("seq")
    me = lax.axis_index("seq")
    crossed = (slot % 2 == 1) & (me % 2 == 0)
    hop = jnp.where(crossed, jnp.where(slot == 1, HOPS - 1, slot - 2), slot)
    own = order_ref[me]
    slab = order_ref[lax.rem(me - hop + n, n)]
    return slab - own, (slab <= own) & (live_ref[own, slab] == 1)


def packed(first, n, order_ref, live_ref):
    count, slots = jnp.int32(0), []
    for i in range(n):
        later, alive = facts(first + i, order_ref, live_ref)
        slots.append((count, later, alive))
        count = count + alive.astype(jnp.int32)
    return slots, count


def at(place, rows, blocks=1):
    return pl.ds(pl.multiple_of(place * rows, rows), blocks * rows)


def in_pairs(count, rows, work):
    def two(i, carry):
        work(at(2 * i, rows, 2))
        return carry

    lax.fori_loop(0, count // 2, two, 0)

    @pl.when(count % 2 == 1)
    def _():
        work(at(count - 1, rows))


def cost(flops):
    return pl.CostEstimate(flops=flops, transcendentals=0, bytes_accessed=flops // 256)


def score_kernel(first, n_blocks, n_head, order_ref, live_ref, q_ref, lse_ref, *refs):
    n_outs = n_head if n_blocks > 1 else 1
    blocks, known = refs[:n_blocks], refs[n_blocks : -n_outs - 2]
    outs, (keys, mass) = refs[-n_outs - 2 : -2], refs[-2:]
    heads, latent, tokens = q_ref.shape
    rows = blocks[0].shape[1]
    slots, count = packed(first, n_blocks, order_ref, live_ref)
    for block, (place, _, alive) in zip(blocks, slots):

        @pl.when(alive)
        def _(block=block, place=place):
            keys[at(place, rows), :] = block[:latent, :].T

    def work(here):
        held = keys[here, :]
        total = None
        for h in range(0, heads, 2):
            pair = jnp.concatenate([q_ref[h], q_ref[h + 1]], axis=1)
            s = lax.dot_general(held, pair, NN, preferred_element_type=jnp.float32)
            s = s * (MAIN_SCALE * LOG2E)
            for n in range(2):
                lse = lse_ref[h + n : h + n + 1, :] * LOG2E
                p = jnp.exp2(s[:, n * tokens : (n + 1) * tokens] - lse)
                total = p if total is None else total + p
        mass[here, :] = total

    in_pairs(count, rows, work)
    values = [ref[...] for ref in known]
    values += [jnp.where(alive, mass[at(place, rows), :], 0.0) for place, _, alive in slots]
    if len(values) == 1:
        outs[0][...] = values[0]
        return
    share = tokens // n_head
    if n_head > 1:
        turn = tokens - lax.axis_index("head") * share
        values = [pltpu.roll(value, turn, 1) for value in values]
    for c in range(len(values) // 2):
        for n, out in enumerate(outs):
            pair = [value[:, n * share : (n + 1) * share] for value in values[2 * c : 2 * c + 2]]
            out[c * rows : (c + 1) * rows, :] = jnp.concatenate(pair, axis=1)


def head_mass(order, live, q, lse, blocks, known, first, n_head):
    heads, latent, tokens = q.shape
    n, rows = len(blocks), blocks[0].shape[1]
    total = n + len(known)
    shapes = [jax.ShapeDtypeStruct((total // 2 * rows, 2 * tokens // n_head), jnp.float32)] * n_head
    if total == 1:
        shapes = [jax.ShapeDtypeStruct((rows, tokens), jnp.float32)]
    return pl.pallas_call(
        functools.partial(score_kernel, first, n, n_head),
        in_specs=[SMEM, SMEM] + [VMEM] * (2 + total),
        out_specs=[VMEM] * len(shapes),
        out_shape=shapes,
        scratch_shapes=[
            pltpu.VMEM((n * rows, latent), jnp.bfloat16),
            pltpu.VMEM((n * rows, tokens), jnp.float32),
        ],
        cost_estimate=cost(2 * tokens * heads * latent * n * rows),
        compiler_params=pltpu.CompilerParams(vmem_limit_bytes=LIMIT),
        name="score_mass",
    )(order, live, q, lse, *blocks, *known)


def lanes_of(part, share):
    return max(1, min(part.shape[0], 128 // share))


def pieces(part, share, width):
    side = lanes_of(part, share)
    step = part.shape[0] // side
    run = max(1, min(step, width))
    for first in range(0, step, run):
        heads = [part[k + n * step] for k in range(first, first + run) for n in range(side)]
        yield run, jnp.concatenate(heads, axis=0)


def lay_weights(parts, w_refs, w_lanes):
    row = 0
    for part, w_ref in zip(parts, w_refs):
        index_here, tokens = w_ref.shape
        share = part.shape[1]
        w = w_ref[...]
        if share < tokens:
            w = pltpu.roll(w, tokens - lax.axis_index("head") * share, 1)
        side = lanes_of(part, share)
        step = index_here // side
        tile = [w[n * step : (n + 1) * step, :share] for n in range(side)]
        w_lanes[row : row + step, :] = jnp.concatenate(tile, axis=1)
        row += step


def logit_kernel(latent, n_head, order_ref, live_ref, *refs):
    parts, w_refs, lse_ref = refs[:n_head], refs[n_head : 2 * n_head], refs[2 * n_head]
    blocks, (out_ref, w_ref, keys, values) = refs[2 * n_head + 1 : -4], refs[-4:]
    rows, idx_width = blocks[0].shape[1], keys.shape[1]
    share = parts[0].shape[1]
    scale = 1.0 / idx_width**0.5
    lay_weights(parts, w_refs, w_ref)
    tile = w_ref.shape[1]
    lse = lse_ref[...]
    if share < lse.shape[1]:
        lse = pltpu.roll(lse, lse.shape[1] - lax.axis_index("head") * share, 1)[:, :share]
    slots, count = packed(0, len(blocks), order_ref, live_ref)
    for block, (place, _, alive) in zip(blocks, slots):

        @pl.when(alive)
        def _(block=block, place=place):
            keys[at(place, rows), :] = block[latent:, :]

    def work(here):
        held = keys[here, :]
        acc = jnp.zeros((held.shape[0], tile), jnp.float32)
        row = 0
        for part in parts:
            for run, piece in pieces(part, share, 8):
                r = lax.dot_general(held, piece, NT, preferred_element_type=jnp.float32)
                for k in range(run):
                    relu = jnp.maximum(r[:, k * tile : (k + 1) * tile], 0.0)
                    acc = acc + relu * w_ref[row + k : row + k + 1, :]
                row += run
        logits = acc[:, :share]
        for first in range(share, tile, share):
            logits = logits + acc[:, first : first + share]
        values[here, :] = jnp.exp(logits * scale - lse)

    in_pairs(count, rows, work)
    for c in range(len(blocks) // 2):
        pair = [jnp.where(s[2], values[at(s[0], rows), :], 0.0) for s in slots[2 * c : 2 * c + 2]]
        out_ref[c * rows : (c + 1) * rows, :] = jnp.concatenate(pair, axis=1)


def index_logits(order, live, parts, weights, lse, blocks, latent):
    n_head, (index_here, share, idx_width) = len(parts), parts[0].shape
    rows = blocks[0].shape[1]
    side = lanes_of(parts[0], share)
    return pl.pallas_call(
        functools.partial(logit_kernel, latent, n_head),
        in_specs=[SMEM, SMEM] + [VMEM] * (2 * n_head + 1 + len(blocks)),
        out_specs=VMEM,
        out_shape=jax.ShapeDtypeStruct((len(blocks) // 2 * rows, 2 * share), jnp.float32),
        scratch_shapes=[
            pltpu.VMEM((n_head * index_here // side, side * share), jnp.float32),
            pltpu.VMEM((len(blocks) * rows, idx_width), jnp.bfloat16),
            pltpu.VMEM((len(blocks) * rows, share), jnp.float32),
        ],
        cost_estimate=cost(2 * len(blocks) * rows * share * n_head * index_here * idx_width),
        compiler_params=pltpu.CompilerParams(vmem_limit_bytes=LIMIT),
        name="index_logits",
    )(order, live, *parts, *weights, lse, *blocks)


def grad_kernel(latent, first, n_head, order_ref, live_ref, *refs):
    parts, w_refs, masses = refs[:n_head], refs[n_head : 2 * n_head], refs[2 * n_head : 3 * n_head]
    target_ref, (w_ref, keys, grads, results) = refs[3 * n_head], refs[-4:]
    n_blocks = (len(refs) - 3 * n_head - 5) // 2
    blocks, outs = refs[3 * n_head + 1 : -n_blocks - 4], refs[-n_blocks - 4 : -4]
    rows = blocks[0].shape[1]
    share, idx_width = parts[0].shape[1:]
    scale = 1.0 / idx_width**0.5
    lay_weights(parts, w_refs, w_ref)
    tile = w_ref.shape[1]
    start = lax.axis_index("head") * share
    slots, count = packed(first, n_blocks, order_ref, live_ref)
    for i, (place, later, alive) in enumerate(slots):

        @pl.when(alive)
        def _(i=i, place=place, later=later):
            here = slice(i // 2 * rows, (i // 2 + 1) * rows)
            span = slice(i % 2 * share, (i % 2 + 1) * share)
            mass = masses[0][here, span]
            for other in masses[1:]:
                mass = mass + other[here, span]
            there = (first + i) // 2 * rows
            value = target_ref[there : there + rows, span] - mass * (1.0 / HEADS)
            within = lax.broadcasted_iota(jnp.int32, (rows, share), 0)
            token = lax.broadcasted_iota(jnp.int32, (rows, share), 1) + start
            grad = jnp.where(within + later * rows <= token, value, 0.0)
            grads[at(place, rows), :] = jnp.concatenate([grad] * (tile // share), axis=1)
            keys[at(place, rows), :] = blocks[i][latent:, :]

    def work(here):
        held = keys[here, :]
        grad = grads[here, :]
        total = jnp.zeros((held.shape[0], idx_width), jnp.float32)
        row = 0
        for part in parts:
            for run, piece in pieces(part, share, 8):
                r = lax.dot_general(held, piece, NT, preferred_element_type=jnp.float32)
                weighted = []
                for k in range(run):
                    w = grad * w_ref[row + k : row + k + 1, :]
                    w = jnp.where(r[:, k * tile : (k + 1) * tile] > 0.0, w, 0.0)
                    weighted.append(w.astype(jnp.bfloat16))
                row += run
                total = total + lax.dot_general(
                    jnp.concatenate(weighted, axis=1), piece, NN, preferred_element_type=jnp.float32
                )
        results[here, :] = total * scale

    in_pairs(count, rows, work)
    for out, (place, _, alive) in zip(outs, slots):
        out[...] = jnp.where(alive, results[at(place, rows), :], 0.0)


def index_grad(order, live, parts, weights, masses, target, blocks, first, latent):
    n_head, (index_here, share, idx_width) = len(parts), parts[0].shape
    rows = blocks[0].shape[1]
    side = lanes_of(parts[0], share)
    return pl.pallas_call(
        functools.partial(grad_kernel, latent, first, n_head),
        in_specs=[SMEM, SMEM] + [VMEM] * (3 * n_head + 1 + len(blocks)),
        out_specs=[VMEM] * len(blocks),
        out_shape=[jax.ShapeDtypeStruct((rows, idx_width), jnp.float32)] * len(blocks),
        scratch_shapes=[
            pltpu.VMEM((n_head * index_here // side, side * share), jnp.float32),
            pltpu.VMEM((len(blocks) * rows, idx_width), jnp.bfloat16),
            pltpu.VMEM((len(blocks) * rows, side * share), jnp.float32),
            pltpu.VMEM((len(blocks) * rows, idx_width), jnp.float32),
        ],
        cost_estimate=cost(4 * len(blocks) * rows * share * n_head * index_here * idx_width),
        compiler_params=pltpu.CompilerParams(vmem_limit_bytes=LIMIT),
        name="index_grad",
    )(order, live, *parts, *weights, *masses, target, *blocks)


def body(
    q_main,
    latent_keys,
    lse_main,
    index_queries,
    index_weights,
    index_keys,
    lse_index,
    slab_order,
    block_live,
):
    n_seq = lax.axis_size("seq")
    n_head = lax.axis_size("head")
    head_place = lax.axis_index("head")
    latent = latent_keys.shape[1]
    share = q_main.shape[0] // n_head
    devices = range(n_seq)

    def ring(distance):
        return [(i, (i + distance) % n_seq) for i in devices]

    def around(array, turn):
        return lax.ppermute(array, "head", [(i, (i + turn) % n_head) for i in range(n_head)])

    forward = [(i, (i + (HOPS - 1 if i % 2 else 1)) % n_seq) for i in devices]
    back = [(b, a) for a, b in forward]
    swap = [(i, i ^ 1) for i in devices]
    own = jnp.concatenate([latent_keys.T, index_keys], axis=0)
    arrived = [lax.ppermute(own, "seq", ring(2))]
    arrived.append(lax.ppermute(own, "seq", ring(4)))
    slots = [own, lax.ppermute(own, "seq", forward)]
    for m in range(1, HOPS // 2):
        if m > 2:
            arrived.append(lax.ppermute(arrived[m - 3], "seq", ring(4)))
        slots += [arrived[m - 1], lax.ppermute(arrived[m - 1], "seq", swap)]

    def to_share(array, turn):
        start = lax.rem(head_place + turn, n_head) * share
        part = lax.dynamic_slice_in_dim(array, start, share, 0)
        return part if turn == 0 else around(part, turn)

    turns = range(n_head)
    weights = [around(index_weights.T, turn) if turn else index_weights.T for turn in turns]
    parts = [to_share(index_queries, turn).transpose(1, 0, 2) for turn in turns]

    tables = slab_order, block_live
    lse = lse_main.T
    early = HOPS - LAST
    q = q_main.transpose(1, 2, 0)
    own_mass = head_mass(*tables, q, lse, slots[:1], [], 0, n_head)
    masses = [
        list(head_mass(*tables, q, lse, slots[1:early], own_mass, 1, n_head)),
        list(head_mass(*tables, q, lse, slots[early:], [], early, n_head)),
    ]
    for group in masses:
        for turn in range(1, n_head):
            group[turn] = around(group[turn], turn)
    target = index_logits(*tables, parts, weights, lse_index[None, :], slots, latent)
    grads = []
    for group, (first, end) in zip(masses, ((0, early), (early, HOPS))):
        blocks = slots[first:end]
        grads += index_grad(*tables, parts, weights, group, target, blocks, first, latent)

    total = grads[0] + lax.ppermute(grads[1], "seq", back)
    for m in range(1, HOPS // 2):
        both = grads[2 * m] + lax.ppermute(grads[2 * m + 1], "seq", swap)
        if n_head == 2 and m == HOPS // 2 - 1:
            break
        total = total + lax.ppermute(both, "seq", ring(-2 * m))
    if n_head != 2:
        return lax.psum(total, "head")
    straight, across = [], []
    for i in devices:
        for x in range(2):
            goal = (i - 2 * m) % n_seq
            straight.append((2 * i + x, 2 * goal + x))
            across.append((2 * i + x, 2 * goal + 1 - x))
    axes = ("seq", "head")
    last = lax.ppermute(both, axes, straight) + lax.ppermute(both, axes, across)
    return total + around(total, 1) + last


def solution(mesh):
    placed = (
        P("seq", "head", None),
        P("seq", None),
        P("seq", "head"),
        P("seq", "head", None),
        P("seq", "head"),
        P("seq", None),
        P("seq"),
        P(),
        P(),
    )
    return jax.shard_map(
        body, mesh=mesh, in_specs=placed, out_specs=P("seq", None), check_vma=False
    )
```

time: 78 us -> 70.7 us (0.906)
  Pallas kernels: 23.9 us -> 11.7 us
  local copies, waits for them, and re-layouts: 3.79 us -> 7.47 us
  waiting for transfers between devices: 11.6 us -> 12.6 us
    pallas_call x3, Pallas kernels: 18.1 us -> 6.83 us  [head_mass(): pl.pallas_call(functools.partial(score_kernel, first, n, n_head), in_spec...]
    unnamed x12 -> x14, local copies, waits for them, and re-layouts: 2.53 us -> 6.2 us
    ppermute x5, waiting for transfers between devices: 0.95 us -> 1.8 us  [around(): lax.ppermute(array, 'head', [(i, (i + turn) % n_head) for i in range(n_he...]
  transfers between devices with their start and end apart: 20 -> 20, of which waited for: 5 -> 6; matrix products, arithmetic and copies ran while one was open for 2% -> 2% of each run, Pallas kernels for 31% -> 17%
where the time goes in v1:
time: 70.7 us; the launch traced here: 69.7 us
  starting transfers between devices  36 us (51%)
  waiting for transfers between devices  12.6 us (18%)
  Pallas kernels  11.7 us (17%)
  local copies, waits for them, and re-layouts  7.47 us (11%)
  other arithmetic  1.65 us (2%)
    ppermute x2, starting transfers between devices, body(): total = total + lax.ppermute(both, 'seq', ring(-2 * m))  14.9 us
    ppermute x1, starting transfers between devices, body(): total = grads[0] + lax.ppermute(grads[1], 'seq', back)  7.44 us
    ppermute x1, waiting for transfers between devices, body(): arrived = [lax.ppermute(own, 'seq', ring(2))]  6.96 us
    pallas_call x3, Pallas kernels, head_mass(): pl.pallas_call(functools.partial(score_kernel, first, n, n_head), in_spec...  6.83 us
    unnamed x14, local copies, waits for them, and re-layouts  6.2 us
    ppermute x5, starting transfers between devices, around(): lax.ppermute(array, 'head', [(i, (i + turn) % n_head) for i in range(n_he...  4.93 us
    ppermute x2, starting transfers between devices, body(): last = lax.ppermute(both, axes, straight) + lax.ppermute(both, axes, across)  3.52 us
    pallas_call x2, Pallas kernels, index_grad(): pl.pallas_call(functools.partial(grad_kernel, latent, first, n_head), in_...  3.15 us
  transfers between devices with their start and end apart: 20, of which 6 were waited for; matrix products, arithmetic and copies ran while one was open for 2% of the time, Pallas kernels for 17%

profile of v1, /device:TPU:0, one launch (start us, length us, event | category | flops | bytes accessed | tf_op | source)
XLA Modules:
  0.0 69.7 jit_solution(5167089768476038404)
XLA Ops:
  0.0 0.0 copy-start.4
  0.0 1.0 %pad_maximum_fusion.refs_0_.refs_5_.refs_7_ = bf16[704,128]{1,0:T(8,128)(2,1)S(1)} fusion(bf16[128,128]{1,0:T(8,128)(2,1)} %param.14, bf16[576,128]{1,0:T(8,128)(2,1)} %bitcast.26), kind=kLoop, calls=%fused_computation.1 | loop fusion | flops 360448 | bytes 360448 | tf_op jit(solution)/shard_map/concatenate | solution.py:316
  1.0 3.0 %collective-permute-start.3 = (bf16[704,128]{1,0:T(8,128)(2,1)S(1)}, bf16[704,128]{1,0:T(8,128)(2,1)S(1)}, u32[]{:S(2)}, u32[]{:S(2)}) collective-permute-start(bf16[704,128]{1,0:T(8,128)(2,1)S(1)} %pad_maximum_fusion.refs_0_.refs_5_.refs_7_), channel_id=1, source_target_pairs={{0,4},{2,6},{4,8},{6,10},{8,12},{10,14},{12,16},{14,18},{16,20},{1... | collective-permute-start | bytes 540680 | tf_op jit(solution)/shard_map/ppermute | solution.py:317
  4.0 1.6 %collective-permute-start.5 = (bf16[704,128]{1,0:T(8,128)(2,1)S(1)}, bf16[704,128]{1,0:T(8,128)(2,1)S(1)}, u32[]{:S(2)}, u32[]{:S(2)}) collective-permute-start(bf16[704,128]{1,0:T(8,128)(2,1)S(1)} %pad_maximum_fusion.refs_0_.refs_5_.refs_7_), channel_id=1, source_target_pairs={{0,8},{2,10},{4,12},{6,14},{8,16},{10,18},{12,20},{14,22},{16,24},... | collective-permute-start | bytes 540680 | tf_op jit(solution)/shard_map/ppermute | solution.py:318
  5.6 0.0 collective-permute-start.2
  5.6 7.0 %collective-permute-done.3.refs_1_.refs_7_.refs_9_ = bf16[704,128]{1,0:T(8,128)(2,1)S(1)} collective-permute-done((bf16[704,128]{1,0:T(8,128)(2,1)S(1)}, bf16[704,128]{1,0:T(8,128)(2,1)S(1)}, u32[]{:S(2)}, u32[]{:S(2)}) %collective-permute-start.3) | collective-permute-done | bytes 180256 | tf_op jit(solution)/shard_map/ppermute | solution.py:317
  12.5 0.0 collective-permute-start.8
  12.6 0.0 collective-permute-start.4
  12.6 0.8 %collective-permute-done.5.refs_3_.refs_9_.refs_11_ = bf16[704,128]{1,0:T(8,128)(2,1)S(1)} collective-permute-done((bf16[704,128]{1,0:T(8,128)(2,1)S(1)}, bf16[704,128]{1,0:T(8,128)(2,1)S(1)}, u32[]{:S(2)}, u32[]{:S(2)}) %collective-permute-start.5) | collective-permute-done | bytes 180256 | tf_op jit(solution)/shard_map/ppermute | solution.py:318
  13.3 0.0 collective-permute-start.6
  13.3 1.3 %constant_dynamic-slice_fusion = (bf16[64,32,128]{2,1,0:T(8,128)(2,1)S(1)}, bf16[64,32,128]{2,1,0:T(8,128)(2,1)S(1)}) fusion(bf16[128,32,128]{2,1,0:T(8,128)(2,1)} %param.12, s32[]{:T(128)S(6)} %select_n.7, s32[]{:T(128)S(6)} %select_n.6), kind=kLoop, calls=%fused_computation.4 | loop fusion | bytes 2097160 | tf_op jit(solution)/shard_map/dynamic_slice | solution.py:327
  14.6 0.2 copy.13
  14.8 1.6 %collective-permute-start = (bf16[64,32,128]{2,0,1:T(8,128)(2,1)S(1)}, bf16[64,32,128]{2,0,1:T(8,128)(2,1)S(1)}, u32[]{:S(2)}, u32[]{:S(2)}) collective-permute-start(bf16[64,32,128]{2,0,1:T(8,128)(2,1)S(1)} %copy.13), channel_id=1, source_target_pairs={{0,1},{1,0},{2,3},{3,2},{4,5},{5,4},{6,7},{7,6},{8,9},{9,8},{10,11... | collective-permute-start | bytes 1572872 | tf_op jit(solution)/shard_map/ppermute | solution.py:311
  16.4 0.2 copy.15
  16.6 0.0 copy-start
  16.6 3.7 %copy-done = bf16[128,64,576]{0,2,1:T(8,128)(2,1)S(1)} copy-done((bf16[128,64,576]{0,2,1:T(8,128)(2,1)S(1)}, bf16[128,64,576]{0,2,1:T(8,128)(2,1)}, u32[]{:S(2)}) %copy-start) | copy-done | bytes 9437208
  20.3 0.0 copy-start.1
  20.3 0.8 %copy-done.1 = f32[128,64]{0,1:T(8,128)S(1)} copy-done((f32[128,64]{0,1:T(8,128)S(1)}, f32[128,64]{0,1:T(8,128)}, u32[]{:S(2)}) %copy-start.1) | copy-done | bytes 32792
  21.0 0.0 copy-start.2
  21.0 0.7 copy-done.2
  21.7 0.0 copy-start.3
  21.7 0.7 copy-done.3
  22.4 2.7 %score_mass.3.refs_5_ = f32[128,128]{1,0:T(8,128)S(1)} custom-call(s32[16]{0:T(128)S(1)} %copy-done.3, s32[16,16]{1,0:T(8,128)S(1)} %copy-done.2, bf16[64,576,128]{2,1,0:T(8,128)(2,1)S(1)} %bitcast.9, f32[64,128]{1,0:T(8,128)S(1)} %bitcast.15, bf16[704,128]{1,0:T(8,128)(2,1)S(1)} %pad_maximum_fusion.refs_0_.refs_5_.refs_7_), custom_call_target="tpu_custom_call" | custom-call | flops 1207959552 | bytes 4718592 | tf_op jit(solution)/shard_map/score_mass/pallas_call | solution.py:112
  25.1 0.0 collective-permute-done.2.refs_0_.refs_6_.refs_8_
  25.1 0.0 copy-done.4
  25.1 0.6 collective-permute-start.1
  25.7 0.0 collective-permute-done.8.refs_11_.refs_0_.refs_7_
  25.7 0.0 collective-permute-start.9
  25.7 0.0 collective-permute-done.4.refs_2_.refs_8_.refs_10_
  25.7 0.0 collective-permute-done.6.refs_4_.refs_10_.refs_12_
  25.8 3.0 %score_mass.4 = (f32[384,128]{1,0:T(8,128)S(1)}, f32[384,128]{1,0:T(8,128)S(1)}) custom-call(s32[16]{0:T(128)S(1)} %copy-done.3, s32[16,16]{1,0:T(8,128)S(1)} %copy-done.2, bf16[64,576,128]{2,1,0:T(8,128)(2,1)S(1)} %bitcast.10, f32[64,128]{1,0:T(8,128)S(1)} %bitcast.16, bf16[704,128]{1,0:T(8,128)(2,1)S(1)} %collective-permute-done.2.refs_0_.refs_6_.refs_8_, ...), custom_call_target="tpu_custom_call" | custom-call | flops 6039797760 | bytes 23592960 | tf_op jit(solution)/shard_map/score_mass/pallas_call | solution.py:112
  28.8 0.0 copy-start.5
  28.8 1.6 %collective-permute-start.7 = (f32[384,128]{1,0:T(8,128)S(1)}, f32[384,128]{1,0:T(8,128)S(1)}, u32[]{:S(2)}, u32[]{:S(2)}) collective-permute-start(f32[384,128]{1,0:T(8,128)S(1)} %get-tuple-element.18), channel_id=1, source_target_pairs={{0,1},{1,0},{2,3},{3,2},{4,5},{5,4},{6,7},{7,6},{8,9},{9,8},{10,11... | collective-permute-start | bytes 589832 | tf_op jit(solution)/shard_map/ppermute | solution.py:311
  30.4 0.0 collective-permute-done.9.refs_12_.refs_1_.refs_8_
  30.4 1.1 %score_mass.5 = (f32[128,128]{1,0:T(8,128)S(1)}, f32[128,128]{1,0:T(8,128)S(1)}) custom-call(s32[16]{0:T(128)S(1)} %copy-done.3, s32[16,16]{1,0:T(8,128)S(1)} %copy-done.2, bf16[64,576,128]{2,1,0:T(8,128)(2,1)S(1)} %bitcast.11, f32[64,128]{1,0:T(8,128)S(1)} %bitcast.17, bf16[704,128]{1,0:T(8,128)(2,1)S(1)} %collective-permute-done.8.refs_11_.refs_0_.refs_7_, ...), custom_call_target="tpu_custom_call" | custom-call | flops 2415919104 | bytes 9437184 | tf_op jit(solution)/shard_map/score_mass/pallas_call | solution.py:112
  31.4 0.6 collective-permute-start.16
  32.0 0.0 collective-permute-done.1.refs_3_
  32.1 0.0 collective-permute-done
  32.1 0.0 copy-done.5
  32.1 1.8 %index_logits.1.refs_6_ = f32[512,128]{1,0:T(8,128)S(1)} custom-call(s32[16]{0:T(128)S(1)} %copy-done.3, s32[16,16]{1,0:T(8,128)S(1)} %copy-done.2, bf16[32,64,128]{2,1,0:T(8,128)(2,1)S(1)} %bitcast.12, bf16[32,64,128]{2,1,0:T(8,128)(2,1)S(1)} %bitcast.18, f32[32,128]{1,0:T(8,128)S(1)} %bitcast.22, f32[32,128]{1,0:T(8,128)S(1)} %collective-permute-done.1.refs_3_, ...), custom_call_target="tpu_custom_call" | custom-call | flops 1073741824 | bytes 4194304 | tf_op jit(solution)/shard_map/index_logits/pallas_call | solution.py:199
  33.8 0.9 %collective-permute-done.7.refs_5_ = f32[384,128]{1,0:T(8,128)S(1)} collective-permute-done((f32[384,128]{1,0:T(8,128)S(1)}, f32[384,128]{1,0:T(8,128)S(1)}, u32[]{:S(2)}, u32[]{:S(2)}) %collective-permute-start.7) | collective-permute-done | bytes 196640 | tf_op jit(solution)/shard_map/ppermute | solution.py:311
  34.8 2.3 %index_grad.2 = (f32[128,128]{1,0:T(8,128)S(1)}, f32[128,128]{1,0:T(8,128)S(1)}, f32[128,128]{1,0:T(8,128)S(1)}, f32[128,128]{1,0:T(8,128)S(1)}, f32[128,128]{1,0:T(8,128)S(1)}, /*index=5*/f32[128,128]{1,0:T(8,128)S(1)}) custom-call(s32[16]{0:T(128)S(1)} %copy-done.3, s32[16,16]{1,0:T(8,128)S(1)} %copy-done.2, bf16[32,64,128]{2,1,0:T(8,128)(2,1)S(1)} %bitcast.13, ...), custom_call_target="tpu_custom_call" | custom-call | flops 1610612736 | bytes 6291456 | tf_op jit(solution)/shard_map/index_grad/pallas_call | solution.py:272
  37.1 0.1 collective-permute-start.13
  37.2 0.5 collective-permute-start.11
  37.7 7.4 %collective-permute-start.10 = (f32[128,128]{1,0:T(8,128)S(1)}, f32[128,128]{1,0:T(8,128)S(1)}, u32[]{:S(2)}, u32[]{:S(2)}) collective-permute-start(f32[128,128]{1,0:T(8,128)S(1)} %get-tuple-element.20), channel_id=1, source_target_pairs={{2,0},{16,2},{6,4},{20,6},{10,8},{24,10},{14,12},{28,14},{18,16},{... | collective-permute-start | bytes 196616 | tf_op jit(solution)/shard_map/ppermute | solution.py:352
  45.1 0.0 collective-permute-done.16.refs_5_
  45.1 0.8 %index_grad.3 = (f32[128,128]{1,0:T(8,128)S(1)}, f32[128,128]{1,0:T(8,128)S(1)}) custom-call(s32[16]{0:T(128)S(1)} %copy-done.3, s32[16,16]{1,0:T(8,128)S(1)} %copy-done.2, bf16[32,64,128]{2,1,0:T(8,128)(2,1)S(1)} %bitcast.14, bf16[32,64,128]{2,1,0:T(8,128)(2,1)S(1)} %bitcast.20, f32[32,128]{1,0:T(8,128)S(1)} %bitcast.24, ...), custom_call_target="tpu_custom_call" | custom-call | flops 536870912 | bytes 2097152 | tf_op jit(solution)/shard_map/index_grad/pallas_call | solution.py:272
  45.9 0.1 collective-permute-start.17
  46.0 0.0 collective-permute-done.13
  46.0 7.4 %collective-permute-start.14 = (f32[128,128]{1,0:T(8,128)S(1)}, f32[128,128]{1,0:T(8,128)S(1)}, u32[]{:S(2)}, u32[]{:S(2)}) collective-permute-start(f32[128,128]{1,0:T(8,128)S(1)} %add.42), channel_id=1, source_target_pairs={{0,24},{2,26},{4,28},{6,30},{8,0},{10,2},{12,4},{14,6},{16,8},{18,... | collective-permute-start | bytes 196616 | tf_op jit(solution)/shard_map/ppermute | solution.py:357
  53.4 0.0 collective-permute-done.11
  53.4 7.5 %collective-permute-start.12 = (f32[128,128]{1,0:T(8,128)S(1)}, f32[128,128]{1,0:T(8,128)S(1)}, u32[]{:S(2)}, u32[]{:S(2)}) collective-permute-start(f32[128,128]{1,0:T(8,128)S(1)} %add.40), channel_id=1, source_target_pairs={{0,28},{2,30},{4,0},{6,2},{8,4},{10,6},{12,8},{14,10},{16,12},{18,... | collective-permute-start | bytes 196616 | tf_op jit(solution)/shard_map/ppermute | solution.py:357
  60.9 0.0 collective-permute-done.17
  60.9 0.1 collective-permute-start.18
  61.0 3.5 %collective-permute-start.19 = (f32[128,128]{1,0:T(8,128)S(1)}, f32[128,128]{1,0:T(8,128)S(1)}, u32[]{:S(2)}, u32[]{:S(2)}) collective-permute-start(f32[128,128]{1,0:T(8,128)S(1)} %add.45), channel_id=1, source_target_pairs={{0,21},{1,20},{2,23},{3,22},{4,25},{5,24},{6,27},{7,26},{8,29},{9,... | collective-permute-start | bytes 196616 | tf_op jit(solution)/shard_map/ppermute | solution.py:367
  64.5 0.0 collective-permute-done.10
  64.5 0.0 collective-permute-done.14
  64.5 0.0 collective-permute-done.12
  64.5 0.6 collective-permute-start.15
  65.1 1.9 %collective-permute-done.18 = f32[128,128]{1,0:T(8,128)S(1)} collective-permute-done((f32[128,128]{1,0:T(8,128)S(1)}, f32[128,128]{1,0:T(8,128)S(1)}, u32[]{:S(2)}, u32[]{:S(2)}) %collective-permute-start.18) | collective-permute-done | bytes 65568 | tf_op jit(solution)/shard_map/ppermute | solution.py:367
  67.0 1.2 %collective-permute-done.19 = f32[128,128]{1,0:T(8,128)S(1)} collective-permute-done((f32[128,128]{1,0:T(8,128)S(1)}, f32[128,128]{1,0:T(8,128)S(1)}, u32[]{:S(2)}, u32[]{:S(2)}) %collective-permute-start.19) | collective-permute-done | bytes 65568 | tf_op jit(solution)/shard_map/ppermute | solution.py:367
  68.2 0.9 %collective-permute-done.15 = f32[128,128]{1,0:T(8,128)S(1)} collective-permute-done((f32[128,128]{1,0:T(8,128)S(1)}, f32[128,128]{1,0:T(8,128)S(1)}, u32[]{:S(2)}, u32[]{:S(2)}) %collective-permute-start.15) | collective-permute-done | bytes 65568 | tf_op jit(solution)/shard_map/ppermute | solution.py:311
  69.0 0.6 add_add_fusion
  (4 shorter events, 0.0 us)
Async XLA Ops:
  0.0 25.1 %copy-start.4 = (f32[128,32]{0,1:T(8,128)S(1)}, f32[128,32]{0,1:T(8,128)}, u32[]{:S(2)}) copy-start(f32[128,32]{0,1:T(8,128)} %param.13) | copy-start | bytes 49156
  1.0 11.6 %collective-permute-start.3 = (bf16[704,128]{1,0:T(8,128)(2,1)S(1)}, bf16[704,128]{1,0:T(8,128)(2,1)S(1)}, u32[]{:S(2)}, u32[]{:S(2)}) collective-permute-start(bf16[704,128]{1,0:T(8,128)(2,1)S(1)} %pad_maximum_fusion.refs_0_.refs_5_.refs_7_), channel_id=1, source_target_pairs={{0,4},{2,6},{4,8},{6,10},{8,12},{10,14},{12,16},{14,18},{16,20},{1... | collective-permute-start | bytes 540680 | tf_op jit(solution)/shard_map/ppermute | solution.py:317
  4.0 9.3 %collective-permute-start.5 = (bf16[704,128]{1,0:T(8,128)(2,1)S(1)}, bf16[704,128]{1,0:T(8,128)(2,1)S(1)}, u32[]{:S(2)}, u32[]{:S(2)}) collective-permute-start(bf16[704,128]{1,0:T(8,128)(2,1)S(1)} %pad_maximum_fusion.refs_0_.refs_5_.refs_7_), channel_id=1, source_target_pairs={{0,8},{2,10},{4,12},{6,14},{8,16},{10,18},{12,20},{14,22},{16,24},... | collective-permute-start | bytes 540680 | tf_op jit(solution)/shard_map/ppermute | solution.py:318
  5.6 19.5 %collective-permute-start.2 = (bf16[704,128]{1,0:T(8,128)(2,1)S(1)}, bf16[704,128]{1,0:T(8,128)(2,1)S(1)}, u32[]{:S(2)}, u32[]{:S(2)}) collective-permute-start(bf16[704,128]{1,0:T(8,128)(2,1)S(1)} %pad_maximum_fusion.refs_0_.refs_5_.refs_7_), channel_id=1, source_target_pairs={{0,2},{2,16},{4,6},{6,20},{8,10},{10,24},{12,14},{14,28},{16,18},{... | collective-permute-start | bytes 540680 | tf_op jit(solution)/shard_map/ppermute | solution.py:319
  12.5 13.2 %collective-permute-start.8 = (bf16[704,128]{1,0:T(8,128)(2,1)S(1)}, bf16[704,128]{1,0:T(8,128)(2,1)S(1)}, u32[]{:S(2)}, u32[]{:S(2)}) collective-permute-start(bf16[704,128]{1,0:T(8,128)(2,1)S(1)} %collective-permute-done.3.refs_1_.refs_7_.refs_9_), channel_id=1, source_target_pairs={{0,8},{2,10},{4,12},{6,14},{8,16},{10,18},{12,20},{14,22},{16,24},... | collective-permute-start | bytes 540680 | tf_op jit(solution)/shard_map/ppermute | solution.py:322
  12.6 13.2 %collective-permute-start.4 = (bf16[704,128]{1,0:T(8,128)(2,1)S(1)}, bf16[704,128]{1,0:T(8,128)(2,1)S(1)}, u32[]{:S(2)}, u32[]{:S(2)}) collective-permute-start(bf16[704,128]{1,0:T(8,128)(2,1)S(1)} %collective-permute-done.3.refs_1_.refs_7_.refs_9_), channel_id=1, source_target_pairs={{0,2},{2,0},{4,6},{6,4},{8,10},{10,8},{12,14},{14,12},{16,18},{18,... | collective-permute-start | bytes 540680 | tf_op jit(solution)/shard_map/ppermute | solution.py:323
  13.3 12.4 %collective-permute-start.6 = (bf16[704,128]{1,0:T(8,128)(2,1)S(1)}, bf16[704,128]{1,0:T(8,128)(2,1)S(1)}, u32[]{:S(2)}, u32[]{:S(2)}) collective-permute-start(bf16[704,128]{1,0:T(8,128)(2,1)S(1)} %collective-permute-done.5.refs_3_.refs_9_.refs_11_), channel_id=1, source_target_pairs={{0,2},{2,0},{4,6},{6,4},{8,10},{10,8},{12,14},{14,12},{16,18},{18,... | collective-permute-start | bytes 540680 | tf_op jit(solution)/shard_map/ppermute | solution.py:323
  14.8 17.2 %collective-permute-start = (bf16[64,32,128]{2,0,1:T(8,128)(2,1)S(1)}, bf16[64,32,128]{2,0,1:T(8,128)(2,1)S(1)}, u32[]{:S(2)}, u32[]{:S(2)}) collective-permute-start(bf16[64,32,128]{2,0,1:T(8,128)(2,1)S(1)} %copy.13), channel_id=1, source_target_pairs={{0,1},{1,0},{2,3},{3,2},{4,5},{5,4},{6,7},{7,6},{8,9},{9,8},{10,11... | collective-permute-start | bytes 1572872 | tf_op jit(solution)/shard_map/ppermute | solution.py:311
  16.6 3.7 %copy-start = (bf16[128,64,576]{0,2,1:T(8,128)(2,1)S(1)}, bf16[128,64,576]{0,2,1:T(8,128)(2,1)}, u32[]{:S(2)}) copy-start(bf16[128,64,576]{0,2,1:T(8,128)(2,1)} %param.9) | copy-start | bytes 28311556
  20.3 0.8 %copy-start.1 = (f32[128,64]{0,1:T(8,128)S(1)}, f32[128,64]{0,1:T(8,128)}, u32[]{:S(2)}) copy-start(f32[128,64]{0,1:T(8,128)} %param.11) | copy-start | bytes 98308
  21.0 0.7 copy-start.2
  21.7 0.7 copy-start.3
  25.1 6.9 %collective-permute-start.1 = (f32[32,128]{1,0:T(8,128)S(1)}, f32[32,128]{1,0:T(8,128)S(1)}, u32[]{:S(2)}, u32[]{:S(2)}) collective-permute-start(f32[32,128]{1,0:T(8,128)S(1)} %bitcast.21), channel_id=1, source_target_pairs={{0,1},{1,0},{2,3},{3,2},{4,5},{5,4},{6,7},{7,6},{8,9},{9,8},{10,11... | collective-permute-start | bytes 49160 | tf_op jit(solution)/shard_map/ppermute | solution.py:311
  25.7 4.6 %collective-permute-start.9 = (bf16[704,128]{1,0:T(8,128)(2,1)S(1)}, bf16[704,128]{1,0:T(8,128)(2,1)S(1)}, u32[]{:S(2)}, u32[]{:S(2)}) collective-permute-start(bf16[704,128]{1,0:T(8,128)(2,1)S(1)} %collective-permute-done.8.refs_11_.refs_0_.refs_7_), channel_id=1, source_target_pairs={{0,2},{2,0},{4,6},{6,4},{8,10},{10,8},{12,14},{14,12},{16,18},{18,... | collective-permute-start | bytes 540680 | tf_op jit(solution)/shard_map/ppermute | solution.py:323
  28.8 3.3 %copy-start.5 = (f32[128]{0:T(128)S(1)}, f32[128]{0:T(128)}, u32[]{:S(2)}) copy-start(f32[128]{0:T(128)} %param.15) | copy-start | bytes 1540
  28.8 6.0 %collective-permute-start.7 = (f32[384,128]{1,0:T(8,128)S(1)}, f32[384,128]{1,0:T(8,128)S(1)}, u32[]{:S(2)}, u32[]{:S(2)}) collective-permute-start(f32[384,128]{1,0:T(8,128)S(1)} %get-tuple-element.18), channel_id=1, source_target_pairs={{0,1},{1,0},{2,3},{3,2},{4,5},{5,4},{6,7},{7,6},{8,9},{9,8},{10,11... | collective-permute-start | bytes 589832 | tf_op jit(solution)/shard_map/ppermute | solution.py:311
  31.4 13.7 %collective-permute-start.16 = (f32[128,128]{1,0:T(8,128)S(1)}, f32[128,128]{1,0:T(8,128)S(1)}, u32[]{:S(2)}, u32[]{:S(2)}) collective-permute-start(f32[128,128]{1,0:T(8,128)S(1)} %get-tuple-element.26), channel_id=1, source_target_pairs={{0,1},{1,0},{2,3},{3,2},{4,5},{5,4},{6,7},{7,6},{8,9},{9,8},{10,11... | collective-permute-start | bytes 196616 | tf_op jit(solution)/shard_map/ppermute | solution.py:311
  37.1 8.9 %collective-permute-start.13 = (f32[128,128]{1,0:T(8,128)S(1)}, f32[128,128]{1,0:T(8,128)S(1)}, u32[]{:S(2)}, u32[]{:S(2)}) collective-permute-start(f32[128,128]{1,0:T(8,128)S(1)} %get-tuple-element.24), channel_id=1, source_target_pairs={{0,2},{2,0},{4,6},{6,4},{8,10},{10,8},{12,14},{14,12},{16,18},{18,... | collective-permute-start | bytes 196616 | tf_op jit(solution)/shard_map/ppermute | solution.py:354
  37.2 16.2 %collective-permute-start.11 = (f32[128,128]{1,0:T(8,128)S(1)}, f32[128,128]{1,0:T(8,128)S(1)}, u32[]{:S(2)}, u32[]{:S(2)}) collective-permute-start(f32[128,128]{1,0:T(8,128)S(1)} %get-tuple-element.22), channel_id=1, source_target_pairs={{0,2},{2,0},{4,6},{6,4},{8,10},{10,8},{12,14},{14,12},{16,18},{18,... | collective-permute-start | bytes 196616 | tf_op jit(solution)/shard_map/ppermute | solution.py:354
  37.7 26.8 %collective-permute-start.10 = (f32[128,128]{1,0:T(8,128)S(1)}, f32[128,128]{1,0:T(8,128)S(1)}, u32[]{:S(2)}, u32[]{:S(2)}) collective-permute-start(f32[128,128]{1,0:T(8,128)S(1)} %get-tuple-element.20), channel_id=1, source_target_pairs={{2,0},{16,2},{6,4},{20,6},{10,8},{24,10},{14,12},{28,14},{18,16},{... | collective-permute-start | bytes 196616 | tf_op jit(solution)/shard_map/ppermute | solution.py:352
  45.9 15.0 %collective-permute-start.17 = (f32[128,128]{1,0:T(8,128)S(1)}, f32[128,128]{1,0:T(8,128)S(1)}, u32[]{:S(2)}, u32[]{:S(2)}) collective-permute-start(f32[128,128]{1,0:T(8,128)S(1)} %get-tuple-element.28), channel_id=1, source_target_pairs={{0,2},{2,0},{4,6},{6,4},{8,10},{10,8},{12,14},{14,12},{16,18},{18,... | collective-permute-start | bytes 196616 | tf_op jit(solution)/shard_map/ppermute | solution.py:354
  46.0 18.4 %collective-permute-start.14 = (f32[128,128]{1,0:T(8,128)S(1)}, f32[128,128]{1,0:T(8,128)S(1)}, u32[]{:S(2)}, u32[]{:S(2)}) collective-permute-start(f32[128,128]{1,0:T(8,128)S(1)} %add.42), channel_id=1, source_target_pairs={{0,24},{2,26},{4,28},{6,30},{8,0},{10,2},{12,4},{14,6},{16,8},{18,... | collective-permute-start | bytes 196616 | tf_op jit(solution)/shard_map/ppermute | solution.py:357
  53.4 11.1 %collective-permute-start.12 = (f32[128,128]{1,0:T(8,128)S(1)}, f32[128,128]{1,0:T(8,128)S(1)}, u32[]{:S(2)}, u32[]{:S(2)}) collective-permute-start(f32[128,128]{1,0:T(8,128)S(1)} %add.40), channel_id=1, source_target_pairs={{0,28},{2,30},{4,0},{6,2},{8,4},{10,6},{12,8},{14,10},{16,12},{18,... | collective-permute-start | bytes 196616 | tf_op jit(solution)/shard_map/ppermute | solution.py:357
  60.9 6.1 %collective-permute-start.18 = (f32[128,128]{1,0:T(8,128)S(1)}, f32[128,128]{1,0:T(8,128)S(1)}, u32[]{:S(2)}, u32[]{:S(2)}) collective-permute-start(f32[128,128]{1,0:T(8,128)S(1)} %add.45), channel_id=1, source_target_pairs={{0,20},{1,21},{2,22},{3,23},{4,24},{5,25},{6,26},{7,27},{8,28},{9,... | collective-permute-start | bytes 196616 | tf_op jit(solution)/shard_map/ppermute | solution.py:367
  61.0 7.2 %collective-permute-start.19 = (f32[128,128]{1,0:T(8,128)S(1)}, f32[128,128]{1,0:T(8,128)S(1)}, u32[]{:S(2)}, u32[]{:S(2)}) collective-permute-start(f32[128,128]{1,0:T(8,128)S(1)} %add.45), channel_id=1, source_target_pairs={{0,21},{1,20},{2,23},{3,22},{4,25},{5,24},{6,27},{7,26},{8,29},{9,... | collective-permute-start | bytes 196616 | tf_op jit(solution)/shard_map/ppermute | solution.py:367
  64.5 4.5 %collective-permute-start.15 = (f32[128,128]{1,0:T(8,128)S(1)}, f32[128,128]{1,0:T(8,128)S(1)}, u32[]{:S(2)}, u32[]{:S(2)}) collective-permute-start(f32[128,128]{1,0:T(8,128)S(1)} %add_add_fusion.1), channel_id=1, source_target_pairs={{0,1},{1,0},{2,3},{3,2},{4,5},{5,4},{6,7},{7,6},{8,9},{9,8},{10,11... | collective-permute-start | bytes 196616 | tf_op jit(solution)/shard_map/ppermute | solution.py:311

commit v2 on v1

--- a/solution.py
+++ b/solution.py
@@ -11,7 +11,6 @@
 
 HEADS = 128
 HOPS = 8
-LAST = 2
 LOG2E = math.log2(math.e)
 MAIN_SCALE = 1.0 / 192.0**0.5
 LIMIT = 20 * 2**20
@@ -31,13 +30,24 @@
     return slab - own, (slab <= own) & (live_ref[own, slab] == 1)
 
 
-def packed(first, n, order_ref, live_ref):
+def packed(ids, order_ref, live_ref):
     count, slots = jnp.int32(0), []
-    for i in range(n):
-        later, alive = facts(first + i, order_ref, live_ref)
+    for i in ids:
+        later, alive = facts(i, order_ref, live_ref)
         slots.append((count, later, alive))
         count = count + alive.astype(jnp.int32)
     return slots, count
+
+
+def side_by_side(values):
+    if len(values) % 2:
+        values = values + [jnp.zeros_like(values[0])]
+    pairs = [jnp.concatenate(values[i : i + 2], axis=1) for i in range(0, len(values), 2)]
+    return jnp.concatenate(pairs, axis=0)
+
+
+def side_by_side_shape(n, rows, share):
+    return jax.ShapeDtypeStruct(((n + 1) // 2 * rows, 2 * share), jnp.float32)
 
 
 def at(place, rows, blocks=1):
@@ -60,13 +70,12 @@
     return pl.CostEstimate(flops=flops, transcendentals=0, bytes_accessed=flops // 256)
 
 
-def score_kernel(first, n_blocks, n_head, order_ref, live_ref, q_ref, lse_ref, *refs):
-    n_outs = n_head if n_blocks > 1 else 1
-    blocks, known = refs[:n_blocks], refs[n_blocks : -n_outs - 2]
+def score_kernel(ids, n_outs, pack, order_ref, live_ref, q_ref, lse_ref, *refs):
+    blocks, known = refs[: len(ids)], refs[len(ids) : -n_outs - 2]
     outs, (keys, mass) = refs[-n_outs - 2 : -2], refs[-2:]
     heads, latent, tokens = q_ref.shape
     rows = blocks[0].shape[1]
-    slots, count = packed(first, n_blocks, order_ref, live_ref)
+    slots, count = packed(ids, order_ref, live_ref)
     for block, (place, _, alive) in zip(blocks, slots):
 
         @pl.when(alive)
@@ -87,31 +96,29 @@
         mass[here, :] = total
 
     in_pairs(count, rows, work)
-    values = [ref[...] for ref in known]
-    values += [jnp.where(alive, mass[at(place, rows), :], 0.0) for place, _, alive in slots]
-    if len(values) == 1:
-        outs[0][...] = values[0]
+    values = [jnp.where(alive, mass[at(place, rows), :], 0.0) for place, _, alive in slots]
+    if not pack:
+        for out, value in zip(outs, values):
+            out[...] = value
         return
-    share = tokens // n_head
-    if n_head > 1:
+    values = [ref[...] for ref in known] + values
+    share = tokens // n_outs
+    if n_outs > 1:
         turn = tokens - lax.axis_index("head") * share
         values = [pltpu.roll(value, turn, 1) for value in values]
-    for c in range(len(values) // 2):
-        for n, out in enumerate(outs):
-            pair = [value[:, n * share : (n + 1) * share] for value in values[2 * c : 2 * c + 2]]
-            out[c * rows : (c + 1) * rows, :] = jnp.concatenate(pair, axis=1)
-
-
-def head_mass(order, live, q, lse, blocks, known, first, n_head):
+    for n, out in enumerate(outs):
+        out[...] = side_by_side([value[:, n * share : (n + 1) * share] for value in values])
+
+
+def head_mass(tables, q, lse, ids, blocks, known=(), n_head=0):
     heads, latent, tokens = q.shape
-    n, rows = len(blocks), blocks[0].shape[1]
-    total = n + len(known)
-    shapes = [jax.ShapeDtypeStruct((total // 2 * rows, 2 * tokens // n_head), jnp.float32)] * n_head
-    if total == 1:
-        shapes = [jax.ShapeDtypeStruct((rows, tokens), jnp.float32)]
+    n, rows = len(ids), blocks[0].shape[1]
+    shapes = [jax.ShapeDtypeStruct((rows, tokens), jnp.float32)] * n
+    if n_head:
+        shapes = [side_by_side_shape(n + len(known), rows, tokens // n_head)] * n_head
     return pl.pallas_call(
-        functools.partial(score_kernel, first, n, n_head),
-        in_specs=[SMEM, SMEM] + [VMEM] * (2 + total),
+        functools.partial(score_kernel, ids, len(shapes), n_head > 0),
+        in_specs=[SMEM, SMEM] + [VMEM] * (2 + n + len(known)),
         out_specs=[VMEM] * len(shapes),
         out_shape=shapes,
         scratch_shapes=[
@@ -121,7 +128,7 @@
         cost_estimate=cost(2 * tokens * heads * latent * n * rows),
         compiler_params=pltpu.CompilerParams(vmem_limit_bytes=LIMIT),
         name="score_mass",
-    )(order, live, q, lse, *blocks, *known)
+    )(*tables, q, lse, *blocks, *known)
 
 
 def lanes_of(part, share):
@@ -152,7 +159,7 @@
         row += step
 
 
-def logit_kernel(latent, n_head, order_ref, live_ref, *refs):
+def logit_kernel(latent, ids, n_head, order_ref, live_ref, *refs):
     parts, w_refs, lse_ref = refs[:n_head], refs[n_head : 2 * n_head], refs[2 * n_head]
     blocks, (out_ref, w_ref, keys, values) = refs[2 * n_head + 1 : -4], refs[-4:]
     rows, idx_width = blocks[0].shape[1], keys.shape[1]
@@ -163,7 +170,7 @@
     lse = lse_ref[...]
     if share < lse.shape[1]:
         lse = pltpu.roll(lse, lse.shape[1] - lax.axis_index("head") * share, 1)[:, :share]
-    slots, count = packed(0, len(blocks), order_ref, live_ref)
+    slots, count = packed(ids, order_ref, live_ref)
     for block, (place, _, alive) in zip(blocks, slots):
 
         @pl.when(alive)
@@ -187,20 +194,18 @@
         values[here, :] = jnp.exp(logits * scale - lse)
 
     in_pairs(count, rows, work)
-    for c in range(len(blocks) // 2):
-        pair = [jnp.where(s[2], values[at(s[0], rows), :], 0.0) for s in slots[2 * c : 2 * c + 2]]
-        out_ref[c * rows : (c + 1) * rows, :] = jnp.concatenate(pair, axis=1)
-
-
-def index_logits(order, live, parts, weights, lse, blocks, latent):
+    out_ref[...] = side_by_side([jnp.where(s[2], values[at(s[0], rows), :], 0.0) for s in slots])
+
+
+def index_logits(tables, parts, weights, lse, ids, blocks, latent):
     n_head, (index_here, share, idx_width) = len(parts), parts[0].shape
     rows = blocks[0].shape[1]
     side = lanes_of(parts[0], share)
     return pl.pallas_call(
-        functools.partial(logit_kernel, latent, n_head),
+        functools.partial(logit_kernel, latent, ids, n_head),
         in_specs=[SMEM, SMEM] + [VMEM] * (2 * n_head + 1 + len(blocks)),
         out_specs=VMEM,
-        out_shape=jax.ShapeDtypeStruct((len(blocks) // 2 * rows, 2 * share), jnp.float32),
+        out_shape=side_by_side_shape(len(blocks), rows, share),
         scratch_shapes=[
             pltpu.VMEM((n_head * index_here // side, side * share), jnp.float32),
             pltpu.VMEM((len(blocks) * rows, idx_width), jnp.bfloat16),
@@ -209,10 +214,10 @@
         cost_estimate=cost(2 * len(blocks) * rows * share * n_head * index_here * idx_width),
         compiler_params=pltpu.CompilerParams(vmem_limit_bytes=LIMIT),
         name="index_logits",
-    )(order, live, *parts, *weights, lse, *blocks)
-
-
-def grad_kernel(latent, first, n_head, order_ref, live_ref, *refs):
+    )(*tables, *parts, *weights, lse, *blocks)
+
+
+def grad_kernel(latent, ids, n_head, order_ref, live_ref, *refs):
     parts, w_refs, masses = refs[:n_head], refs[n_head : 2 * n_head], refs[2 * n_head : 3 * n_head]
     target_ref, (w_ref, keys, grads, results) = refs[3 * n_head], refs[-4:]
     n_blocks = (len(refs) - 3 * n_head - 5) // 2
@@ -223,7 +228,7 @@
     lay_weights(parts, w_refs, w_ref)
     tile = w_ref.shape[1]
     start = lax.axis_index("head") * share
-    slots, count = packed(first, n_blocks, order_ref, live_ref)
+    slots, count = packed(ids, order_ref, live_ref)
     for i, (place, later, alive) in enumerate(slots):
 
         @pl.when(alive)
@@ -233,8 +238,7 @@
             mass = masses[0][here, span]
             for other in masses[1:]:
                 mass = mass + other[here, span]
-            there = (first + i) // 2 * rows
-            value = target_ref[there : there + rows, span] - mass * (1.0 / HEADS)
+            value = target_ref[here, span] - mass * (1.0 / HEADS)
             within = lax.broadcasted_iota(jnp.int32, (rows, share), 0)
             token = lax.broadcasted_iota(jnp.int32, (rows, share), 1) + start
             grad = jnp.where(within + later * rows <= token, value, 0.0)
@@ -265,12 +269,12 @@
         out[...] = jnp.where(alive, results[at(place, rows), :], 0.0)
 
 
-def index_grad(order, live, parts, weights, masses, target, blocks, first, latent):
+def index_grad(tables, parts, weights, masses, target, ids, blocks, latent):
     n_head, (index_here, share, idx_width) = len(parts), parts[0].shape
     rows = blocks[0].shape[1]
     side = lanes_of(parts[0], share)
     return pl.pallas_call(
-        functools.partial(grad_kernel, latent, first, n_head),
+        functools.partial(grad_kernel, latent, ids, n_head),
         in_specs=[SMEM, SMEM] + [VMEM] * (3 * n_head + 1 + len(blocks)),
         out_specs=[VMEM] * len(blocks),
         out_shape=[jax.ShapeDtypeStruct((rows, idx_width), jnp.float32)] * len(blocks),
@@ -283,7 +287,7 @@
         cost_estimate=cost(4 * len(blocks) * rows * share * n_head * index_here * idx_width),
         compiler_params=pltpu.CompilerParams(vmem_limit_bytes=LIMIT),
         name="index_grad",
-    )(order, live, *parts, *weights, *masses, target, *blocks)
+    )(*tables, *parts, *weights, *masses, target, *blocks)
 
 
 def body(
@@ -332,40 +336,44 @@
     parts = [to_share(index_queries, turn).transpose(1, 0, 2) for turn in turns]
 
     tables = slab_order, block_live
-    lse = lse_main.T
-    early = HOPS - LAST
-    q = q_main.transpose(1, 2, 0)
-    own_mass = head_mass(*tables, q, lse, slots[:1], [], 0, n_head)
-    masses = [
-        list(head_mass(*tables, q, lse, slots[1:early], own_mass, 1, n_head)),
-        list(head_mass(*tables, q, lse, slots[early:], [], early, n_head)),
-    ]
-    for group in masses:
+    q, lse, lse_share = q_main.transpose(1, 2, 0), lse_main.T, lse_index[None, :]
+
+    def blocks(ids):
+        return [slots[i] for i in ids]
+
+    runs = [(0,)] + [(2 * m, 2 * m + 1) for m in range(1, HOPS // 2 - 1)]
+    runs[-1] += (1,)
+    early = tuple(i for run in runs for i in run)
+    late = (HOPS - 2, HOPS - 1)
+    known = []
+    for run in runs[:-1]:
+        known += head_mass(tables, q, lse, run, blocks(run))
+    group = head_mass(tables, q, lse, runs[-1], blocks(runs[-1]), known, n_head)
+    masses = [list(group)]
+    masses.append(list(head_mass(tables, q, lse, late, blocks(late), (), n_head)))
+    grads = {}
+    for ids, mass in zip((early, late), masses):
         for turn in range(1, n_head):
-            group[turn] = around(group[turn], turn)
-    target = index_logits(*tables, parts, weights, lse_index[None, :], slots, latent)
-    grads = []
-    for group, (first, end) in zip(masses, ((0, early), (early, HOPS))):
-        blocks = slots[first:end]
-        grads += index_grad(*tables, parts, weights, group, target, blocks, first, latent)
+            mass[turn] = around(mass[turn], turn)
+        target = index_logits(tables, parts, weights, lse_share, ids, blocks(ids), latent)
+        found = index_grad(tables, parts, weights, mass, target, ids, blocks(ids), latent)
+        grads.update(zip(ids, found))
 
     total = grads[0] + lax.ppermute(grads[1], "seq", back)
     for m in range(1, HOPS // 2):
         both = grads[2 * m] + lax.ppermute(grads[2 * m + 1], "seq", swap)
-        if n_head == 2 and m == HOPS // 2 - 1:
-            break
-        total = total + lax.ppermute(both, "seq", ring(-2 * m))
+        if m < HOPS // 2 - 1:
+            total = total + lax.ppermute(both, "seq", ring(-2 * m))
     if n_head != 2:
-        return lax.psum(total, "head")
-    straight, across = [], []
-    for i in devices:
-        for x in range(2):
-            goal = (i - 2 * m) % n_seq
-            straight.append((2 * i + x, 2 * goal + x))
-            across.append((2 * i + x, 2 * goal + 1 - x))
-    axes = ("seq", "head")
-    last = lax.ppermute(both, axes, straight) + lax.ppermute(both, axes, across)
-    return total + around(total, 1) + last
+        return lax.psum(total + lax.ppermute(both, "seq", ring(-2 * m)), "head")
+    last = []
+    for turn in range(2):
+        route = [
+            (2 * i + x, 2 * ((i - 2 * m) % n_seq) + (x + turn) % 2) for i in devices for x in range(2)
+        ]
+        last.append(lax.ppermute(both, ("seq", "head"), route))
+    total = total + around(total, 1)
+    return total + (last[0] + last[1])
 
 
 def solution(mesh):

time: 70.7 us -> 67.5 us (0.955); the launches traced: 69.7 us -> 67.2 us
  starting transfers between devices: 36 us -> 32.4 us
  Pallas kernels: 11.7 us -> 13.6 us
  waiting for transfers between devices: 12.6 us -> 11.7 us
    ppermute x2, starting transfers between devices: 14.9 us -> 9.84 us  [body(): total = total + lax.ppermute(both, 'seq', ring(-2 * m))]
    pallas_call x6 -> x8, Pallas kernels: 11.7 us -> 13.6 us  [the longest x4 7.56 us: head_mass(): pl.pallas_call(functools.partial(score_kernel, ids, len(shapes), n_head >...]
    ppermute x2, waiting for transfers between devices: 3.06 us -> 1.75 us  [body(): last.append(lax.ppermute(both, ('seq', 'head'), route))]
    ppermute x2, waiting for transfers between devices: 0.01 us -> 0.98 us  [body(): total = total + lax.ppermute(both, 'seq', ring(-2 * m))]
    ppermute x5, starting transfers between devices: 4.93 us -> 5.87 us  [around(): lax.ppermute(array, 'head', [(i, (i + turn) % n_head) for i in range(n_he...]
    ppermute x1, waiting for transfers between devices: 0.77 us -> 0.01 us  [body(): arrived.append(lax.ppermute(own, 'seq', ring(4)))]
    unnamed x14 -> x22, local copies, waits for them, and re-layouts: 6.2 us -> 6.22 us
  transfers between devices with their start and end apart: 20 -> 20, of which waited for: 6 -> 6; matrix products, arithmetic and copies ran while one was open for 2% -> 3% of each run, Pallas kernels for 17% -> 20%
where the time goes in v2:
time: 67.5 us; the launch traced here: 67.2 us
  starting transfers between devices  32.4 us (48%)
  Pallas kernels  13.6 us (20%)
  waiting for transfers between devices  11.7 us (17%)
  local copies, waits for them, and re-layouts  7.49 us (11%)
  other arithmetic  1.65 us (2%)
    ppermute x2, starting transfers between devices, body(): total = total + lax.ppermute(both, 'seq', ring(-2 * m))  9.84 us
    ppermute x1, starting transfers between devices, body(): total = grads[0] + lax.ppermute(grads[1], 'seq', back)  7.97 us
    pallas_call x4, Pallas kernels, head_mass(): pl.pallas_call(functools.partial(score_kernel, ids, len(shapes), n_head >...  7.56 us
    ppermute x1, waiting for transfers between devices, body(): arrived = [lax.ppermute(own, 'seq', ring(2))]  6.96 us
    unnamed x22, local copies, waits for them, and re-layouts  6.22 us
    ppermute x5, starting transfers between devices, around(): lax.ppermute(array, 'head', [(i, (i + turn) % n_head) for i in range(n_he...  5.87 us
    pallas_call x2, Pallas kernels, index_grad(): pl.pallas_call(functools.partial(grad_kernel, latent, ids, n_head), in_sp...  3.45 us
    ppermute x1, starting transfers between devices, body(): arrived = [lax.ppermute(own, 'seq', ring(2))]  3.05 us
  transfers between devices with their start and end apart: 20, of which 6 were waited for; matrix products, arithmetic and copies ran while one was open for 3% of the time, Pallas kernels for 20%

profile of v2, /device:TPU:0, one launch (start us, length us, event | category | flops | bytes accessed | tf_op | source)
XLA Modules:
  0.0 67.2 jit_solution(400687933490050957)
XLA Ops:
  0.0 1.0 %pad_maximum_fusion.refs_0_.refs_5_.refs_7_ = bf16[704,128]{1,0:T(8,128)(2,1)S(1)} fusion(bf16[128,128]{1,0:T(8,128)(2,1)} %param.14, bf16[576,128]{1,0:T(8,128)(2,1)} %bitcast.34), kind=kLoop, calls=%fused_computation.1 | loop fusion | flops 360448 | bytes 360448 | tf_op jit(solution)/shard_map/concatenate | solution.py:320
  1.0 3.0 %collective-permute-start.5 = (bf16[704,128]{1,0:T(8,128)(2,1)S(1)}, bf16[704,128]{1,0:T(8,128)(2,1)S(1)}, u32[]{:S(2)}, u32[]{:S(2)}) collective-permute-start(bf16[704,128]{1,0:T(8,128)(2,1)S(1)} %pad_maximum_fusion.refs_0_.refs_5_.refs_7_), channel_id=1, source_target_pairs={{0,4},{2,6},{4,8},{6,10},{8,12},{10,14},{12,16},{14,18},{16,20},{1... | collective-permute-start | bytes 540680 | tf_op jit(solution)/shard_map/ppermute | solution.py:321
  4.0 1.6 %collective-permute-start.2 = (bf16[704,128]{1,0:T(8,128)(2,1)S(1)}, bf16[704,128]{1,0:T(8,128)(2,1)S(1)}, u32[]{:S(2)}, u32[]{:S(2)}) collective-permute-start(bf16[704,128]{1,0:T(8,128)(2,1)S(1)} %pad_maximum_fusion.refs_0_.refs_5_.refs_7_), channel_id=1, source_target_pairs={{0,8},{2,10},{4,12},{6,14},{8,16},{10,18},{12,20},{14,22},{16,24},... | collective-permute-start | bytes 540680 | tf_op jit(solution)/shard_map/ppermute | solution.py:322
  5.6 0.0 collective-permute-start.4
  5.6 7.0 %collective-permute-done.5.refs_0_.refs_6_.refs_8_ = bf16[704,128]{1,0:T(8,128)(2,1)S(1)} collective-permute-done((bf16[704,128]{1,0:T(8,128)(2,1)S(1)}, bf16[704,128]{1,0:T(8,128)(2,1)S(1)}, u32[]{:S(2)}, u32[]{:S(2)}) %collective-permute-start.5) | collective-permute-done | bytes 180256 | tf_op jit(solution)/shard_map/ppermute | solution.py:321
  12.6 0.0 collective-permute-start.6
  12.6 0.0 collective-permute-start.14
  12.6 1.3 %constant_dynamic-slice_fusion = (bf16[64,32,128]{2,1,0:T(8,128)(2,1)S(1)}, bf16[64,32,128]{2,1,0:T(8,128)(2,1)S(1)}) fusion(bf16[128,32,128]{2,1,0:T(8,128)(2,1)} %param.12, s32[]{:T(128)S(6)} %select_n.7, s32[]{:T(128)S(6)} %select_n.6), kind=kLoop, calls=%fused_computation.4 | loop fusion | bytes 2097160 | tf_op jit(solution)/shard_map/dynamic_slice | solution.py:331
  13.8 0.2 copy.13
  14.0 1.7 %collective-permute-start = (bf16[64,32,128]{2,0,1:T(8,128)(2,1)S(1)}, bf16[64,32,128]{2,0,1:T(8,128)(2,1)S(1)}, u32[]{:S(2)}, u32[]{:S(2)}) collective-permute-start(bf16[64,32,128]{2,0,1:T(8,128)(2,1)S(1)} %copy.13), channel_id=1, source_target_pairs={{0,1},{1,0},{2,3},{3,2},{4,5},{5,4},{6,7},{7,6},{8,9},{9,8},{10,11... | collective-permute-start | bytes 1572872 | tf_op jit(solution)/shard_map/ppermute | solution.py:315
  15.8 0.2 copy.15
  16.0 0.0 copy-start
  16.0 3.7 %copy-done = bf16[128,64,576]{0,2,1:T(8,128)(2,1)S(1)} copy-done((bf16[128,64,576]{0,2,1:T(8,128)(2,1)S(1)}, bf16[128,64,576]{0,2,1:T(8,128)(2,1)}, u32[]{:S(2)}) %copy-start) | copy-done | bytes 9437208
  19.7 0.8 %copy-done.1 = f32[128,64]{0,1:T(8,128)S(1)} copy-done((f32[128,64]{0,1:T(8,128)S(1)}, f32[128,64]{0,1:T(8,128)}, u32[]{:S(2)}) %copy-start.1) | copy-done | bytes 32792
  20.4 0.7 %copy-done.3 = s32[16,16]{1,0:T(8,128)S(1)} copy-done((s32[16,16]{1,0:T(8,128)S(1)}, s32[16,16]{1,0:T(8,128)}, u32[]{:S(2)}) %copy-start.3) | copy-done | bytes 1048
  21.1 0.7 copy-done.5
  21.8 2.7 %score_mass.4.refs_3_ = f32[128,128]{1,0:T(8,128)S(1)} custom-call(s32[16]{0:T(128)S(1)} %copy-done.5, s32[16,16]{1,0:T(8,128)S(1)} %copy-done.3, bf16[64,576,128]{2,1,0:T(8,128)(2,1)S(1)} %bitcast.9, f32[64,128]{1,0:T(8,128)S(1)} %bitcast.23, bf16[704,128]{1,0:T(8,128)(2,1)S(1)} %pad_maximum_fusion.refs_0_.refs_5_.refs_7_), custom_call_target="tpu_custom_call" | custom-call | flops 1207959552 | bytes 4718592 | tf_op jit(solution)/shard_map/score_mass/pallas_call | solution.py:119
  24.5 0.0 collective-permute-done.2.refs_0_.refs_8_.refs_10_
  24.5 0.0 copy-done.4
  24.5 0.0 copy-start.6
  24.5 0.4 collective-permute-start.1
  25.0 0.0 collective-permute-done.6.refs_1_.refs_7_.refs_9_
  25.0 0.0 collective-permute-start.3
  25.0 0.0 collective-permute-done.14.refs_0_.refs_5_.refs_7_
  25.0 0.5 collective-permute-start.15
  25.5 0.0 copy-done.2
  25.5 2.7 %score_mass.5 = (f32[128,128]{1,0:T(8,128)S(1)}, f32[128,128]{1,0:T(8,128)S(1)}) custom-call(s32[16]{0:T(128)S(1)} %copy-done.5, s32[16,16]{1,0:T(8,128)S(1)} %copy-done.3, bf16[64,576,128]{2,1,0:T(8,128)(2,1)S(1)} %bitcast.10, f32[64,128]{1,0:T(8,128)S(1)} %bitcast.24, bf16[704,128]{1,0:T(8,128)(2,1)S(1)} %collective-permute-done.5.refs_0_.refs_6_.refs_8_, ...), custom_call_target="tpu_custom_call" | custom-call | flops 2415919104 | bytes 9437184 | tf_op jit(solution)/shard_map/score_mass/pallas_call | solution.py:119
  28.2 0.0 collective-permute-done.4.refs_2_.refs_10_.refs_12_
  28.2 0.0 collective-permute-done.3.refs_1_.refs_9_.refs_11_
  28.3 0.0 slice-start.2
  28.3 1.2 %score_mass.6 = (f32[384,128]{1,0:T(8,128)S(1)}, f32[384,128]{1,0:T(8,128)S(1)}) custom-call(s32[16]{0:T(128)S(1)} %copy-done.5, s32[16,16]{1,0:T(8,128)S(1)} %copy-done.3, bf16[64,576,128]{2,1,0:T(8,128)(2,1)S(1)} %bitcast.11, f32[64,128]{1,0:T(8,128)S(1)} %bitcast.25, bf16[704,128]{1,0:T(8,128)(2,1)S(1)} %collective-permute-done.2.refs_0_.refs_8_.refs_10_, ...), custom_call_target="tpu_custom_call" | custom-call | flops 3623878656 | bytes 14155776 | tf_op jit(solution)/shard_map/score_mass/pallas_call | solution.py:119
  29.5 1.7 %collective-permute-start.7 = (f32[384,128]{1,0:T(8,128)S(1)}, f32[384,128]{1,0:T(8,128)S(1)}, u32[]{:S(2)}, u32[]{:S(2)}) collective-permute-start(f32[384,128]{1,0:T(8,128)S(1)} %get-tuple-element.22), channel_id=1, source_target_pairs={{0,1},{1,0},{2,3},{3,2},{4,5},{5,4},{6,7},{7,6},{8,9},{9,8},{10,11... | collective-permute-start | bytes 589832 | tf_op jit(solution)/shard_map/ppermute | solution.py:315
  31.2 0.0 collective-permute-done.1.refs_3_
  31.2 0.0 collective-permute-done
  31.2 0.0 copy-done.6
  31.2 1.7 %index_logits.2.refs_6_ = f32[384,128]{1,0:T(8,128)S(1)} custom-call(s32[16]{0:T(128)S(1)} %copy-done.5, s32[16,16]{1,0:T(8,128)S(1)} %copy-done.3, bf16[32,64,128]{2,1,0:T(8,128)(2,1)S(1)} %bitcast.15, bf16[32,64,128]{2,1,0:T(8,128)(2,1)S(1)} %bitcast.19, f32[32,128]{1,0:T(8,128)S(1)} %bitcast.28, f32[32,128]{1,0:T(8,128)S(1)} %collective-permute-done.1.refs_3_, ...), custom_call_target="tpu_custom_call" | custom-call | flops 805306368 | bytes 3145728 | tf_op jit(solution)/shard_map/index_logits/pallas_call | solution.py:204
  32.9 0.0 collective-permute-done.15.refs_1_.refs_6_.refs_8_
  33.0 0.0 slice-done
  33.0 0.9 %score_mass.7 = (f32[128,128]{1,0:T(8,128)S(1)}, f32[128,128]{1,0:T(8,128)S(1)}) custom-call(s32[16]{0:T(128)S(1)} %copy-done.5, s32[16,16]{1,0:T(8,128)S(1)} %copy-done.3, bf16[64,576,128]{2,1,0:T(8,128)(2,1)S(1)} %bitcast.14, f32[64,128]{1,0:T(8,128)S(1)} %bitcast.26, bf16[704,128]{1,0:T(8,128)(2,1)S(1)} %collective-permute-done.14.refs_0_.refs_5_.refs_7_, ...), custom_call_target="tpu_custom_call" | custom-call | flops 2415919104 | bytes 9437184 | tf_op jit(solution)/shard_map/score_mass/pallas_call | solution.py:119
  33.9 0.4 collective-permute-start.16
  34.3 0.9 %collective-permute-done.7.refs_5_ = f32[384,128]{1,0:T(8,128)S(1)} collective-permute-done((f32[384,128]{1,0:T(8,128)S(1)}, f32[384,128]{1,0:T(8,128)S(1)}, u32[]{:S(2)}, u32[]{:S(2)}) %collective-permute-start.7) | collective-permute-done | bytes 196640 | tf_op jit(solution)/shard_map/ppermute | solution.py:315
  35.2 2.6 %index_grad.2 = (f32[128,128]{1,0:T(8,128)S(1)}, f32[128,128]{1,0:T(8,128)S(1)}, f32[128,128]{1,0:T(8,128)S(1)}, f32[128,128]{1,0:T(8,128)S(1)}, f32[128,128]{1,0:T(8,128)S(1)}, /*index=5*/f32[128,128]{1,0:T(8,128)S(1)}) custom-call(s32[16]{0:T(128)S(1)} %copy-done.5, s32[16,16]{1,0:T(8,128)S(1)} %copy-done.3, bf16[32,64,128]{2,1,0:T(8,128)(2,1)S(1)} %bitcast.16, ...), custom_call_target="tpu_custom_call" | custom-call | flops 1610612736 | bytes 6291456 | tf_op jit(solution)/shard_map/index_grad/pallas_call | solution.py:276
  37.8 0.1 collective-permute-start.9
  37.9 0.5 collective-permute-start.11
  38.4 0.9 %index_logits.3.refs_6_ = f32[128,128]{1,0:T(8,128)S(1)} custom-call(s32[16]{0:T(128)S(1)} %copy-done.5, s32[16,16]{1,0:T(8,128)S(1)} %copy-done.3, bf16[32,64,128]{2,1,0:T(8,128)(2,1)S(1)} %bitcast.17, bf16[32,64,128]{2,1,0:T(8,128)(2,1)S(1)} %bitcast.21, f32[32,128]{1,0:T(8,128)S(1)} %bitcast.30, f32[32,128]{1,0:T(8,128)S(1)} %collective-permute-done.1.refs_3_, ...), custom_call_target="tpu_custom_call" | custom-call | flops 268435456 | bytes 1048576 | tf_op jit(solution)/shard_map/index_logits/pallas_call | solution.py:204
  39.3 8.0 %collective-permute-start.8 = (f32[128,128]{1,0:T(8,128)S(1)}, f32[128,128]{1,0:T(8,128)S(1)}, u32[]{:S(2)}, u32[]{:S(2)}) collective-permute-start(f32[128,128]{1,0:T(8,128)S(1)} %get-tuple-element.24), channel_id=1, source_target_pairs={{2,0},{16,2},{6,4},{20,6},{10,8},{24,10},{14,12},{28,14},{18,16},{... | collective-permute-start | bytes 196616 | tf_op jit(solution)/shard_map/ppermute | solution.py:362
  47.3 0.0 collective-permute-done.16.refs_5_
  47.3 0.8 %index_grad.3 = (f32[128,128]{1,0:T(8,128)S(1)}, f32[128,128]{1,0:T(8,128)S(1)}) custom-call(s32[16]{0:T(128)S(1)} %copy-done.5, s32[16,16]{1,0:T(8,128)S(1)} %copy-done.3, bf16[32,64,128]{2,1,0:T(8,128)(2,1)S(1)} %bitcast.18, bf16[32,64,128]{2,1,0:T(8,128)(2,1)S(1)} %bitcast.22, f32[32,128]{1,0:T(8,128)S(1)} %bitcast.31, ...), custom_call_target="tpu_custom_call" | custom-call | flops 536870912 | bytes 2097152 | tf_op jit(solution)/shard_map/index_grad/pallas_call | solution.py:276
  48.1 0.1 collective-permute-start.17
  48.2 0.0 collective-permute-done.9
  48.2 0.1 collective-permute-start.10
  48.3 0.0 collective-permute-done.11
  48.3 9.8 %collective-permute-start.12 = (f32[128,128]{1,0:T(8,128)S(1)}, f32[128,128]{1,0:T(8,128)S(1)}, u32[]{:S(2)}, u32[]{:S(2)}) collective-permute-start(f32[128,128]{1,0:T(8,128)S(1)} %add.42), channel_id=1, source_target_pairs={{0,24},{2,26},{4,28},{6,30},{8,0},{10,2},{12,4},{14,6},{16,8},{18,... | collective-permute-start | bytes 196616 | tf_op jit(solution)/shard_map/ppermute | solution.py:366
  58.1 0.0 collective-permute-done.17
  58.1 0.1 collective-permute-start.18
  58.2 2.9 %collective-permute-start.19 = (f32[128,128]{1,0:T(8,128)S(1)}, f32[128,128]{1,0:T(8,128)S(1)}, u32[]{:S(2)}, u32[]{:S(2)}) collective-permute-start(f32[128,128]{1,0:T(8,128)S(1)} %add.45), channel_id=1, source_target_pairs={{0,21},{1,20},{2,23},{3,22},{4,25},{5,24},{6,27},{7,26},{8,29},{9,... | collective-permute-start | bytes 196616 | tf_op jit(solution)/shard_map/ppermute | solution.py:374
  61.1 0.0 collective-permute-done.8
  61.1 0.0 collective-permute-done.10
  61.1 1.0 %collective-permute-done.12 = f32[128,128]{1,0:T(8,128)S(1)} collective-permute-done((f32[128,128]{1,0:T(8,128)S(1)}, f32[128,128]{1,0:T(8,128)S(1)}, u32[]{:S(2)}, u32[]{:S(2)}) %collective-permute-start.12) | collective-permute-done | bytes 65568 | tf_op jit(solution)/shard_map/ppermute | solution.py:366
  62.1 1.6 %collective-permute-start.13 = (f32[128,128]{1,0:T(8,128)S(1)}, f32[128,128]{1,0:T(8,128)S(1)}, u32[]{:S(2)}, u32[]{:S(2)}) collective-permute-start(f32[128,128]{1,0:T(8,128)S(1)} %add_add_fusion.1), channel_id=1, source_target_pairs={{0,1},{1,0},{2,3},{3,2},{4,5},{5,4},{6,7},{7,6},{8,9},{9,8},{10,11... | collective-permute-start | bytes 196616 | tf_op jit(solution)/shard_map/ppermute | solution.py:315
  63.7 0.5 collective-permute-done.18
  64.2 1.2 %collective-permute-done.19 = f32[128,128]{1,0:T(8,128)S(1)} collective-permute-done((f32[128,128]{1,0:T(8,128)S(1)}, f32[128,128]{1,0:T(8,128)S(1)}, u32[]{:S(2)}, u32[]{:S(2)}) %collective-permute-start.19) | collective-permute-done | bytes 65568 | tf_op jit(solution)/shard_map/ppermute | solution.py:374
  65.4 1.2 %collective-permute-done.13 = f32[128,128]{1,0:T(8,128)S(1)} collective-permute-done((f32[128,128]{1,0:T(8,128)S(1)}, f32[128,128]{1,0:T(8,128)S(1)}, u32[]{:S(2)}, u32[]{:S(2)}) %collective-permute-start.13) | collective-permute-done | bytes 65568 | tf_op jit(solution)/shard_map/ppermute | solution.py:315
  66.6 0.6 add_add_fusion
  (14 shorter events, 0.1 us)
Async XLA Ops:
  0.0 25.5 %copy-start.2 = (f32[128,64]{0,1:T(8,128)S(1)}, f32[128,64]{0,1:T(8,128)}, u32[]{:S(2)}) copy-start(f32[128,64]{0,1:T(8,128)} %param.11) | copy-start | bytes 98308
  0.0 24.5 %copy-start.4 = (f32[128,32]{0,1:T(8,128)S(1)}, f32[128,32]{0,1:T(8,128)}, u32[]{:S(2)}) copy-start(f32[128,32]{0,1:T(8,128)} %param.13) | copy-start | bytes 49156
  1.0 11.6 %collective-permute-start.5 = (bf16[704,128]{1,0:T(8,128)(2,1)S(1)}, bf16[704,128]{1,0:T(8,128)(2,1)S(1)}, u32[]{:S(2)}, u32[]{:S(2)}) collective-permute-start(bf16[704,128]{1,0:T(8,128)(2,1)S(1)} %pad_maximum_fusion.refs_0_.refs_5_.refs_7_), channel_id=1, source_target_pairs={{0,4},{2,6},{4,8},{6,10},{8,12},{10,14},{12,16},{14,18},{16,20},{1... | collective-permute-start | bytes 540680 | tf_op jit(solution)/shard_map/ppermute | solution.py:321
  4.0 20.5 %collective-permute-start.2 = (bf16[704,128]{1,0:T(8,128)(2,1)S(1)}, bf16[704,128]{1,0:T(8,128)(2,1)S(1)}, u32[]{:S(2)}, u32[]{:S(2)}) collective-permute-start(bf16[704,128]{1,0:T(8,128)(2,1)S(1)} %pad_maximum_fusion.refs_0_.refs_5_.refs_7_), channel_id=1, source_target_pairs={{0,8},{2,10},{4,12},{6,14},{8,16},{10,18},{12,20},{14,22},{16,24},... | collective-permute-start | bytes 540680 | tf_op jit(solution)/shard_map/ppermute | solution.py:322
  5.6 22.6 %collective-permute-start.4 = (bf16[704,128]{1,0:T(8,128)(2,1)S(1)}, bf16[704,128]{1,0:T(8,128)(2,1)S(1)}, u32[]{:S(2)}, u32[]{:S(2)}) collective-permute-start(bf16[704,128]{1,0:T(8,128)(2,1)S(1)} %pad_maximum_fusion.refs_0_.refs_5_.refs_7_), channel_id=1, source_target_pairs={{0,2},{2,16},{4,6},{6,20},{8,10},{10,24},{12,14},{14,28},{16,18},{... | collective-permute-start | bytes 540680 | tf_op jit(solution)/shard_map/ppermute | solution.py:323
  12.6 12.4 %collective-permute-start.6 = (bf16[704,128]{1,0:T(8,128)(2,1)S(1)}, bf16[704,128]{1,0:T(8,128)(2,1)S(1)}, u32[]{:S(2)}, u32[]{:S(2)}) collective-permute-start(bf16[704,128]{1,0:T(8,128)(2,1)S(1)} %collective-permute-done.5.refs_0_.refs_6_.refs_8_), channel_id=1, source_target_pairs={{0,2},{2,0},{4,6},{6,4},{8,10},{10,8},{12,14},{14,12},{16,18},{18,... | collective-permute-start | bytes 540680 | tf_op jit(solution)/shard_map/ppermute | solution.py:327
  12.6 12.4 %collective-permute-start.14 = (bf16[704,128]{1,0:T(8,128)(2,1)S(1)}, bf16[704,128]{1,0:T(8,128)(2,1)S(1)}, u32[]{:S(2)}, u32[]{:S(2)}) collective-permute-start(bf16[704,128]{1,0:T(8,128)(2,1)S(1)} %collective-permute-done.5.refs_0_.refs_6_.refs_8_), channel_id=1, source_target_pairs={{0,8},{2,10},{4,12},{6,14},{8,16},{10,18},{12,20},{14,22},{16,24},... | collective-permute-start | bytes 540680 | tf_op jit(solution)/shard_map/ppermute | solution.py:326
  14.0 17.2 %collective-permute-start = (bf16[64,32,128]{2,0,1:T(8,128)(2,1)S(1)}, bf16[64,32,128]{2,0,1:T(8,128)(2,1)S(1)}, u32[]{:S(2)}, u32[]{:S(2)}) collective-permute-start(bf16[64,32,128]{2,0,1:T(8,128)(2,1)S(1)} %copy.13), channel_id=1, source_target_pairs={{0,1},{1,0},{2,3},{3,2},{4,5},{5,4},{6,7},{7,6},{8,9},{9,8},{10,11... | collective-permute-start | bytes 1572872 | tf_op jit(solution)/shard_map/ppermute | solution.py:315
  16.0 3.7 %copy-start = (bf16[128,64,576]{0,2,1:T(8,128)(2,1)S(1)}, bf16[128,64,576]{0,2,1:T(8,128)(2,1)}, u32[]{:S(2)}) copy-start(bf16[128,64,576]{0,2,1:T(8,128)(2,1)} %param.9) | copy-start | bytes 28311556
  19.7 0.8 %copy-start.1 = (f32[128,64]{0,1:T(8,128)S(1)}, f32[128,64]{0,1:T(8,128)}, u32[]{:S(2)}) copy-start(f32[128,64]{0,1:T(8,128)} %param.11) | copy-start | bytes 98308
  20.4 0.7 %copy-start.3 = (s32[16,16]{1,0:T(8,128)S(1)}, s32[16,16]{1,0:T(8,128)}, u32[]{:S(2)}) copy-start(s32[16,16]{1,0:T(8,128)} %live_ref.15) | copy-start | bytes 3076
  21.1 0.7 copy-start.5
  24.5 6.7 %copy-start.6 = (f32[128]{0:T(128)S(1)}, f32[128]{0:T(128)}, u32[]{:S(2)}) copy-start(f32[128]{0:T(128)} %param.15) | copy-start | bytes 1540
  24.5 6.7 %collective-permute-start.1 = (f32[32,128]{1,0:T(8,128)S(1)}, f32[32,128]{1,0:T(8,128)S(1)}, u32[]{:S(2)}, u32[]{:S(2)}) collective-permute-start(f32[32,128]{1,0:T(8,128)S(1)} %bitcast.27), channel_id=1, source_target_pairs={{0,1},{1,0},{2,3},{3,2},{4,5},{5,4},{6,7},{7,6},{8,9},{9,8},{10,11... | collective-permute-start | bytes 49160 | tf_op jit(solution)/shard_map/ppermute | solution.py:315
  25.0 3.3 %collective-permute-start.3 = (bf16[704,128]{1,0:T(8,128)(2,1)S(1)}, bf16[704,128]{1,0:T(8,128)(2,1)S(1)}, u32[]{:S(2)}, u32[]{:S(2)}) collective-permute-start(bf16[704,128]{1,0:T(8,128)(2,1)S(1)} %collective-permute-done.2.refs_0_.refs_8_.refs_10_), channel_id=1, source_target_pairs={{0,2},{2,0},{4,6},{6,4},{8,10},{10,8},{12,14},{14,12},{16,18},{18,... | collective-permute-start | bytes 540680 | tf_op jit(solution)/shard_map/ppermute | solution.py:327
  25.0 8.0 %collective-permute-start.15 = (bf16[704,128]{1,0:T(8,128)(2,1)S(1)}, bf16[704,128]{1,0:T(8,128)(2,1)S(1)}, u32[]{:S(2)}, u32[]{:S(2)}) collective-permute-start(bf16[704,128]{1,0:T(8,128)(2,1)S(1)} %collective-permute-done.14.refs_0_.refs_5_.refs_7_), channel_id=1, source_target_pairs={{0,2},{2,0},{4,6},{6,4},{8,10},{10,8},{12,14},{14,12},{16,18},{18,... | collective-permute-start | bytes 540680 | tf_op jit(solution)/shard_map/ppermute | solution.py:327
  25.5 7.5 %slice-start = ((s8[9437184]{0:T(1024)(128)(4,1)}), s8[4194304]{0:T(1024)(128)(4,1)S(1)}, s32[]{:S(2)}) async-start(s8[9437184]{0:T(1024)(128)(4,1)} %bitcast.12), calls=%async_computation | async-start | bytes 8388608
  25.5 7.5 %slice-start.1 = ((s8[9437184]{0:T(1024)(128)(4,1)}), s8[4194304]{0:T(1024)(128)(4,1)S(1)}, s32[]{:S(2)}) async-start(s8[9437184]{0:T(1024)(128)(4,1)} %bitcast.12), calls=%async_computation.1 | async-start | bytes 8388608
  28.3 4.7 %slice-start.2 = ((s8[9437184]{0:T(1024)(128)(4,1)}), s8[1048576]{0:T(1024)(128)(4,1)S(1)}, s32[]{:S(2)}) async-start(s8[9437184]{0:T(1024)(128)(4,1)} %bitcast.12), calls=%async_computation.2 | async-start | bytes 2097152
  29.5 5.7 %collective-permute-start.7 = (f32[384,128]{1,0:T(8,128)S(1)}, f32[384,128]{1,0:T(8,128)S(1)}, u32[]{:S(2)}, u32[]{:S(2)}) collective-permute-start(f32[384,128]{1,0:T(8,128)S(1)} %get-tuple-element.22), channel_id=1, source_target_pairs={{0,1},{1,0},{2,3},{3,2},{4,5},{5,4},{6,7},{7,6},{8,9},{9,8},{10,11... | collective-permute-start | bytes 589832 | tf_op jit(solution)/shard_map/ppermute | solution.py:315
  33.9 13.4 %collective-permute-start.16 = (f32[128,128]{1,0:T(8,128)S(1)}, f32[128,128]{1,0:T(8,128)S(1)}, u32[]{:S(2)}, u32[]{:S(2)}) collective-permute-start(f32[128,128]{1,0:T(8,128)S(1)} %get-tuple-element.30), channel_id=1, source_target_pairs={{0,1},{1,0},{2,3},{3,2},{4,5},{5,4},{6,7},{7,6},{8,9},{9,8},{10,11... | collective-permute-start | bytes 196616 | tf_op jit(solution)/shard_map/ppermute | solution.py:315
  37.8 10.4 %collective-permute-start.9 = (f32[128,128]{1,0:T(8,128)S(1)}, f32[128,128]{1,0:T(8,128)S(1)}, u32[]{:S(2)}, u32[]{:S(2)}) collective-permute-start(f32[128,128]{1,0:T(8,128)S(1)} %get-tuple-element.26), channel_id=1, source_target_pairs={{0,2},{2,0},{4,6},{6,4},{8,10},{10,8},{12,14},{14,12},{16,18},{18,... | collective-permute-start | bytes 196616 | tf_op jit(solution)/shard_map/ppermute | solution.py:364
  37.9 10.4 %collective-permute-start.11 = (f32[128,128]{1,0:T(8,128)S(1)}, f32[128,128]{1,0:T(8,128)S(1)}, u32[]{:S(2)}, u32[]{:S(2)}) collective-permute-start(f32[128,128]{1,0:T(8,128)S(1)} %get-tuple-element.28), channel_id=1, source_target_pairs={{0,2},{2,0},{4,6},{6,4},{8,10},{10,8},{12,14},{14,12},{16,18},{18,... | collective-permute-start | bytes 196616 | tf_op jit(solution)/shard_map/ppermute | solution.py:364
  39.3 21.8 %collective-permute-start.8 = (f32[128,128]{1,0:T(8,128)S(1)}, f32[128,128]{1,0:T(8,128)S(1)}, u32[]{:S(2)}, u32[]{:S(2)}) collective-permute-start(f32[128,128]{1,0:T(8,128)S(1)} %get-tuple-element.24), channel_id=1, source_target_pairs={{2,0},{16,2},{6,4},{20,6},{10,8},{24,10},{14,12},{28,14},{18,16},{... | collective-permute-start | bytes 196616 | tf_op jit(solution)/shard_map/ppermute | solution.py:362
  48.1 10.0 %collective-permute-start.17 = (f32[128,128]{1,0:T(8,128)S(1)}, f32[128,128]{1,0:T(8,128)S(1)}, u32[]{:S(2)}, u32[]{:S(2)}) collective-permute-start(f32[128,128]{1,0:T(8,128)S(1)} %get-tuple-element.32), channel_id=1, source_target_pairs={{0,2},{2,0},{4,6},{6,4},{8,10},{10,8},{12,14},{14,12},{16,18},{18,... | collective-permute-start | bytes 196616 | tf_op jit(solution)/shard_map/ppermute | solution.py:364
  48.2 12.9 %collective-permute-start.10 = (f32[128,128]{1,0:T(8,128)S(1)}, f32[128,128]{1,0:T(8,128)S(1)}, u32[]{:S(2)}, u32[]{:S(2)}) collective-permute-start(f32[128,128]{1,0:T(8,128)S(1)} %add.40), channel_id=1, source_target_pairs={{0,28},{2,30},{4,0},{6,2},{8,4},{10,6},{12,8},{14,10},{16,12},{18,... | collective-permute-start | bytes 196616 | tf_op jit(solution)/shard_map/ppermute | solution.py:366
  48.3 13.8 %collective-permute-start.12 = (f32[128,128]{1,0:T(8,128)S(1)}, f32[128,128]{1,0:T(8,128)S(1)}, u32[]{:S(2)}, u32[]{:S(2)}) collective-permute-start(f32[128,128]{1,0:T(8,128)S(1)} %add.42), channel_id=1, source_target_pairs={{0,24},{2,26},{4,28},{6,30},{8,0},{10,2},{12,4},{14,6},{16,8},{18,... | collective-permute-start | bytes 196616 | tf_op jit(solution)/shard_map/ppermute | solution.py:366
  58.1 6.1 %collective-permute-start.18 = (f32[128,128]{1,0:T(8,128)S(1)}, f32[128,128]{1,0:T(8,128)S(1)}, u32[]{:S(2)}, u32[]{:S(2)}) collective-permute-start(f32[128,128]{1,0:T(8,128)S(1)} %add.45), channel_id=1, source_target_pairs={{0,20},{1,21},{2,22},{3,23},{4,24},{5,25},{6,26},{7,27},{8,28},{9,... | collective-permute-start | bytes 196616 | tf_op jit(solution)/shard_map/ppermute | solution.py:374
  58.2 7.2 %collective-permute-start.19 = (f32[128,128]{1,0:T(8,128)S(1)}, f32[128,128]{1,0:T(8,128)S(1)}, u32[]{:S(2)}, u32[]{:S(2)}) collective-permute-start(f32[128,128]{1,0:T(8,128)S(1)} %add.45), channel_id=1, source_target_pairs={{0,21},{1,20},{2,23},{3,22},{4,25},{5,24},{6,27},{7,26},{8,29},{9,... | collective-permute-start | bytes 196616 | tf_op jit(solution)/shard_map/ppermute | solution.py:374
  62.1 4.5 %collective-permute-start.13 = (f32[128,128]{1,0:T(8,128)S(1)}, f32[128,128]{1,0:T(8,128)S(1)}, u32[]{:S(2)}, u32[]{:S(2)}) collective-permute-start(f32[128,128]{1,0:T(8,128)S(1)} %add_add_fusion.1), channel_id=1, source_target_pairs={{0,1},{1,0},{2,3},{3,2},{4,5},{5,4},{6,7},{7,6},{8,9},{9,8},{10,11... | collective-permute-start | bytes 196616 | tf_op jit(solution)/shard_map/ppermute | solution.py:315

commit v3 on v2

--- a/solution.py
+++ b/solution.py
@@ -14,10 +14,48 @@
 LOG2E = math.log2(math.e)
 MAIN_SCALE = 1.0 / 192.0**0.5
 LIMIT = 20 * 2**20
+PACK_COST = 10**10
 NT = (((1,), (1,)), ((), ()))
 NN = (((1,), (0,)), ((), ()))
 VMEM = pl.BlockSpec(memory_space=pltpu.VMEM)
 SMEM = pl.BlockSpec(memory_space=pltpu.SMEM)
+HBM = pl.BlockSpec(memory_space=pltpu.HBM)
+
+
+def pack_kernel(latent_ref, index_ref, queries_ref, block_ref, *rest):
+    shares, sems = rest[:-1], rest[-1]
+    latent = latent_ref.shape[0]
+    rows = index_ref.shape[0]
+    n, share = len(shares), shares[0].shape[0]
+    copies = [
+        (latent_ref, block_ref.at[pl.ds(0, latent)]),
+        (index_ref, block_ref.at[pl.ds(latent, rows)]),
+    ]
+    for turn, out in enumerate(shares):
+        start = lax.rem(lax.axis_index("head") + turn, n) * share
+        copies.append((queries_ref.at[pl.ds(start, share)], out))
+    copies = [pltpu.make_async_copy(a, b, sems.at[i]) for i, (a, b) in enumerate(copies)]
+    for copy in copies:
+        copy.start()
+    for copy in copies:
+        copy.wait()
+
+
+def packed_inputs(latent_keys, index_keys, index_queries, n_head):
+    latent, rows = latent_keys.shape
+    tokens, index_here, idx_width = index_queries.shape
+    share = jax.ShapeDtypeStruct((tokens // n_head, index_here, idx_width), index_queries.dtype)
+    block, *shares = pl.pallas_call(
+        pack_kernel,
+        in_specs=[HBM] * 3,
+        out_specs=[VMEM] * (1 + n_head),
+        out_shape=[jax.ShapeDtypeStruct((latent + rows, rows), latent_keys.dtype)] + [share] * n_head,
+        scratch_shapes=[pltpu.SemaphoreType.DMA((2 + n_head,))],
+        cost_estimate=cost(PACK_COST),
+        compiler_params=pltpu.CompilerParams(vmem_limit_bytes=LIMIT),
+        name="pack_keys",
+    )(latent_keys, index_keys, index_queries)
+    return block, shares
 
 
 def facts(slot, order_ref, live_ref):
@@ -303,9 +341,7 @@
 ):
     n_seq = lax.axis_size("seq")
     n_head = lax.axis_size("head")
-    head_place = lax.axis_index("head")
     latent = latent_keys.shape[1]
-    share = q_main.shape[0] // n_head
     devices = range(n_seq)
 
     def ring(distance):
@@ -317,7 +353,7 @@
     forward = [(i, (i + (HOPS - 1 if i % 2 else 1)) % n_seq) for i in devices]
     back = [(b, a) for a, b in forward]
     swap = [(i, i ^ 1) for i in devices]
-    own = jnp.concatenate([latent_keys.T, index_keys], axis=0)
+    own, shares = packed_inputs(latent_keys.T, index_keys, index_queries, n_head)
     arrived = [lax.ppermute(own, "seq", ring(2))]
     arrived.append(lax.ppermute(own, "seq", ring(4)))
     slots = [own, lax.ppermute(own, "seq", forward)]
@@ -326,14 +362,10 @@
             arrived.append(lax.ppermute(arrived[m - 3], "seq", ring(4)))
         slots += [arrived[m - 1], lax.ppermute(arrived[m - 1], "seq", swap)]
 
-    def to_share(array, turn):
-        start = lax.rem(head_place + turn, n_head) * share
-        part = lax.dynamic_slice_in_dim(array, start, share, 0)
-        return part if turn == 0 else around(part, turn)
-
     turns = range(n_head)
     weights = [around(index_weights.T, turn) if turn else index_weights.T for turn in turns]
-    parts = [to_share(index_queries, turn).transpose(1, 0, 2) for turn in turns]
+    parts = [around(shares[turn], turn) if turn else shares[turn] for turn in turns]
+    parts = [part.transpose(1, 0, 2) for part in parts]
 
     tables = slab_order, block_live
     q, lse, lse_share = q_main.transpose(1, 2, 0), lse_main.T, lse_index[None, :]

time: 67.5 us -> 65.3 us (0.967)
  waiting for transfers between devices: 11.7 us -> 19.5 us
  starting transfers between devices: 32.4 us -> 27.4 us
  local copies, waits for them, and re-layouts: 7.49 us -> 3.33 us
  other arithmetic: 1.65 us -> 0.7 us
    ppermute x5, waiting for transfers between devices: 2.02 us -> 6.38 us  [around(): lax.ppermute(array, 'head', [(i, (i + turn) % n_head) for i in range(n_he...]
    ppermute x1, waiting for transfers between devices: 0.01 us -> 3.5 us  [body(): arrived.append(lax.ppermute(arrived[m - 3], 'seq', ring(4)))]
    unnamed x22 -> x18, local copies, waits for them, and re-layouts: 6.22 us -> 2.92 us
    ppermute x1, starting transfers between devices: 7.97 us -> 4.9 us  [body(): total = grads[0] + lax.ppermute(grads[1], 'seq', back)]
    ppermute x2, starting transfers between devices: 9.84 us -> 7.9 us  [body(): total = total + lax.ppermute(both, 'seq', ring(-2 * m))]
    dynamic_slice x1 -> x0, local copies, waits for them, and re-layouts: 1.27 us -> none  [to_share(): part = lax.dynamic_slice_in_dim(array, start, share, 0)]
    concatenate x1 -> x0, other arithmetic: 0.96 us -> none  [body(): own = jnp.concatenate([latent_keys.T, index_keys], axis=0)]
  transfers between devices with their start and end apart: 20 -> 20, of which waited for: 6 -> 7; matrix products, arithmetic and copies ran while one was open for 3% -> 1% of each run, Pallas kernels for 20% -> 21%
where the time goes in v3:
time: 65.3 us; the launch traced here: 65.1 us
  starting transfers between devices  27.4 us (42%)
  waiting for transfers between devices  19.5 us (30%)
  Pallas kernels  14 us (21%)
  local copies, waits for them, and re-layouts  3.33 us (5%)
  other arithmetic  0.7 us (1%)
    ppermute x2, starting transfers between devices, body(): total = total + lax.ppermute(both, 'seq', ring(-2 * m))  7.9 us
    pallas_call x4, Pallas kernels, head_mass(): pl.pallas_call(functools.partial(score_kernel, ids, len(shapes), n_head >...  7.56 us
    ppermute x1, waiting for transfers between devices, body(): arrived = [lax.ppermute(own, 'seq', ring(2))]  6.86 us
    ppermute x5, waiting for transfers between devices, around(): lax.ppermute(array, 'head', [(i, (i + turn) % n_head) for i in range(n_he...  6.38 us
    ppermute x5, starting transfers between devices, around(): lax.ppermute(array, 'head', [(i, (i + turn) % n_head) for i in range(n_he...  5.8 us
    ppermute x1, starting transfers between devices, body(): total = grads[0] + lax.ppermute(grads[1], 'seq', back)  4.9 us
    ppermute x1, waiting for transfers between devices, body(): arrived.append(lax.ppermute(arrived[m - 3], 'seq', ring(4)))  3.5 us
    pallas_call x2, Pallas kernels, index_grad(): pl.pallas_call(functools.partial(grad_kernel, latent, ids, n_head), in_sp...  3.45 us
  transfers between devices with their start and end apart: 20, of which 7 were waited for; matrix products, arithmetic and copies ran while one was open for 1% of the time, Pallas kernels for 21%

profile of v3, /device:TPU:0, one launch (start us, length us, event | category | flops | bytes accessed | tf_op | source)
XLA Modules:
  0.0 65.1 jit_solution(2545467826325859280)
XLA Ops:
  0.0 0.0 copy-start.6
  0.0 1.2 %copy-done.6 = bf16[128,32,128]{2,1,0:T(8,128)(2,1)S(1)} copy-done((bf16[128,32,128]{2,1,0:T(8,128)(2,1)S(1)}, bf16[128,32,128]{2,1,0:T(8,128)(2,1)}, u32[]{:S(2)}) %copy-start.6) | copy-done | bytes 1048600
  1.2 0.9 %copy-done.7 = bf16[128,576]{0,1:T(8,128)(2,1)S(1)} copy-done((bf16[128,576]{0,1:T(8,128)(2,1)S(1)}, bf16[128,576]{0,1:T(8,128)(2,1)}, u32[]{:S(2)}) %copy-start.7) | copy-done | bytes 147480
  2.1 0.8 %copy-done.8 = bf16[128,128]{1,0:T(8,128)(2,1)S(1)} copy-done((bf16[128,128]{1,0:T(8,128)(2,1)S(1)}, bf16[128,128]{1,0:T(8,128)(2,1)}, u32[]{:S(2)}) %copy-start.8) | copy-done | bytes 32792
  2.9 0.0 copy-start.4
  2.9 0.4 pack_keys.1
  3.3 3.0 %collective-permute-start.5 = (bf16[704,128]{1,0:T(8,128)(2,1)S(1)}, bf16[704,128]{1,0:T(8,128)(2,1)S(1)}, u32[]{:S(2)}, u32[]{:S(2)}) collective-permute-start(bf16[704,128]{1,0:T(8,128)(2,1)S(1)} %get-tuple-element.24.refs_0_.refs_5_.refs_7_), channel_id=1, source_target_pairs={{0,4},{2,6},{4,8},{6,10},{8,12},{10,14},{12,16},{14,18},{16,20},{1... | collective-permute-start | bytes 540680 | tf_op jit(solution)/shard_map/ppermute | solution.py:357
  6.3 1.6 %collective-permute-start.2 = (bf16[704,128]{1,0:T(8,128)(2,1)S(1)}, bf16[704,128]{1,0:T(8,128)(2,1)S(1)}, u32[]{:S(2)}, u32[]{:S(2)}) collective-permute-start(bf16[704,128]{1,0:T(8,128)(2,1)S(1)} %get-tuple-element.24.refs_0_.refs_5_.refs_7_), channel_id=1, source_target_pairs={{0,8},{2,10},{4,12},{6,14},{8,16},{10,18},{12,20},{14,22},{16,24},... | collective-permute-start | bytes 540680 | tf_op jit(solution)/shard_map/ppermute | solution.py:358
  7.9 6.9 %collective-permute-done.5.refs_0_.refs_6_.refs_8_ = bf16[704,128]{1,0:T(8,128)(2,1)S(1)} collective-permute-done((bf16[704,128]{1,0:T(8,128)(2,1)S(1)}, bf16[704,128]{1,0:T(8,128)(2,1)S(1)}, u32[]{:S(2)}, u32[]{:S(2)}) %collective-permute-start.5) | collective-permute-done | bytes 180256 | tf_op jit(solution)/shard_map/ppermute | solution.py:357
  14.8 0.0 collective-permute-start.6
  14.8 0.0 collective-permute-start.14
  14.8 0.5 collective-permute-start.4
  15.3 0.0 copy-done.3
  15.3 1.7 %collective-permute-start.1 = (f32[32,128]{1,0:T(8,128)S(1)}, f32[32,128]{1,0:T(8,128)S(1)}, u32[]{:S(2)}, u32[]{:S(2)}) collective-permute-start(f32[32,128]{1,0:T(8,128)S(1)} %bitcast.25), channel_id=1, source_target_pairs={{0,1},{1,0},{2,3},{3,2},{4,5},{5,4},{6,7},{7,6},{8,9},{9,8},{10,11... | collective-permute-start | bytes 49160 | tf_op jit(solution)/shard_map/ppermute | solution.py:351
  16.9 0.2 copy.11
  17.1 0.2 copy.13
  17.4 0.0 copy-done
  17.4 0.0 copy-done.1
  17.4 0.0 copy-done.2
  17.4 0.0 copy-done.4
  17.4 2.7 %score_mass.4.refs_3_ = f32[128,128]{1,0:T(8,128)S(1)} custom-call(s32[16]{0:T(128)S(1)} %copy-done.4, s32[16,16]{1,0:T(8,128)S(1)} %copy-done.2, bf16[64,576,128]{2,1,0:T(8,128)(2,1)S(1)} %bitcast.9, f32[64,128]{1,0:T(8,128)S(1)} %bitcast.21, bf16[704,128]{1,0:T(8,128)(2,1)S(1)} %get-tuple-element.24.refs_0_.refs_5_.refs_7_), custom_call_target="tpu_custom_call" | custom-call | flops 1207959552 | bytes 4718592 | tf_op jit(solution)/shard_map/score_mass/pallas_call | solution.py:157
  20.1 0.0 copy-start.5
  20.1 0.0 collective-permute-done.2.refs_0_.refs_8_.refs_10_
  20.2 0.4 collective-permute-start
  20.6 0.0 collective-permute-done.6.refs_1_.refs_7_.refs_9_
  20.6 0.0 collective-permute-start.3
  20.6 3.5 %collective-permute-done.14.refs_0_.refs_5_.refs_7_ = bf16[704,128]{1,0:T(8,128)(2,1)S(1)} collective-permute-done((bf16[704,128]{1,0:T(8,128)(2,1)S(1)}, bf16[704,128]{1,0:T(8,128)(2,1)S(1)}, u32[]{:S(2)}, u32[]{:S(2)}) %collective-permute-start.14) | collective-permute-done | bytes 180256 | tf_op jit(solution)/shard_map/ppermute | solution.py:362
  24.1 0.0 collective-permute-start.15
  24.1 2.7 %score_mass.5 = (f32[128,128]{1,0:T(8,128)S(1)}, f32[128,128]{1,0:T(8,128)S(1)}) custom-call(s32[16]{0:T(128)S(1)} %copy-done.4, s32[16,16]{1,0:T(8,128)S(1)} %copy-done.2, bf16[64,576,128]{2,1,0:T(8,128)(2,1)S(1)} %bitcast.10, f32[64,128]{1,0:T(8,128)S(1)} %bitcast.22, bf16[704,128]{1,0:T(8,128)(2,1)S(1)} %collective-permute-done.5.refs_0_.refs_6_.refs_8_, ...), custom_call_target="tpu_custom_call" | custom-call | flops 2415919104 | bytes 9437184 | tf_op jit(solution)/shard_map/score_mass/pallas_call | solution.py:157
  26.8 0.0 collective-permute-done.4.refs_2_.refs_10_.refs_12_
  26.9 0.0 collective-permute-done.3.refs_1_.refs_9_.refs_11_
  26.9 1.2 %score_mass.6 = (f32[384,128]{1,0:T(8,128)S(1)}, f32[384,128]{1,0:T(8,128)S(1)}) custom-call(s32[16]{0:T(128)S(1)} %copy-done.4, s32[16,16]{1,0:T(8,128)S(1)} %copy-done.2, bf16[64,576,128]{2,1,0:T(8,128)(2,1)S(1)} %bitcast.11, f32[64,128]{1,0:T(8,128)S(1)} %bitcast.23, bf16[704,128]{1,0:T(8,128)(2,1)S(1)} %collective-permute-done.2.refs_0_.refs_8_.refs_10_, ...), custom_call_target="tpu_custom_call" | custom-call | flops 3623878656 | bytes 14155776 | tf_op jit(solution)/shard_map/score_mass/pallas_call | solution.py:157
  28.1 1.7 %collective-permute-start.7 = (f32[384,128]{1,0:T(8,128)S(1)}, f32[384,128]{1,0:T(8,128)S(1)}, u32[]{:S(2)}, u32[]{:S(2)}) collective-permute-start(f32[384,128]{1,0:T(8,128)S(1)} %get-tuple-element.28), channel_id=1, source_target_pairs={{0,1},{1,0},{2,3},{3,2},{4,5},{5,4},{6,7},{7,6},{8,9},{9,8},{10,11... | collective-permute-start | bytes 589832 | tf_op jit(solution)/shard_map/ppermute | solution.py:351
  29.8 0.0 collective-permute-done.1.refs_3_
  29.8 5.2 %collective-permute-done = bf16[64,32,128]{2,0,1:T(8,128)(2,1)S(1)} collective-permute-done((bf16[64,32,128]{2,0,1:T(8,128)(2,1)S(1)}, bf16[64,32,128]{2,0,1:T(8,128)(2,1)S(1)}, u32[]{:S(2)}, u32[]{:S(2)}) %collective-permute-start) | collective-permute-done | bytes 524320 | tf_op jit(solution)/shard_map/ppermute | solution.py:351
  35.0 0.0 copy-done.5
  35.0 1.7 %index_logits.2.refs_6_ = f32[384,128]{1,0:T(8,128)S(1)} custom-call(s32[16]{0:T(128)S(1)} %copy-done.4, s32[16,16]{1,0:T(8,128)S(1)} %copy-done.2, bf16[32,64,128]{2,1,0:T(8,128)(2,1)S(1)} %bitcast.13, bf16[32,64,128]{2,1,0:T(8,128)(2,1)S(1)} %bitcast.17, f32[32,128]{1,0:T(8,128)S(1)} %bitcast.26, f32[32,128]{1,0:T(8,128)S(1)} %collective-permute-done.1.refs_3_, ...), custom_call_target="tpu_custom_call" | custom-call | flops 805306368 | bytes 3145728 | tf_op jit(solution)/shard_map/index_logits/pallas_call | solution.py:242
  36.7 0.0 collective-permute-done.15.refs_1_.refs_6_.refs_8_
  36.8 0.9 %score_mass.7 = (f32[128,128]{1,0:T(8,128)S(1)}, f32[128,128]{1,0:T(8,128)S(1)}) custom-call(s32[16]{0:T(128)S(1)} %copy-done.4, s32[16,16]{1,0:T(8,128)S(1)} %copy-done.2, bf16[64,576,128]{2,1,0:T(8,128)(2,1)S(1)} %bitcast.12, f32[64,128]{1,0:T(8,128)S(1)} %bitcast.24, bf16[704,128]{1,0:T(8,128)(2,1)S(1)} %collective-permute-done.14.refs_0_.refs_5_.refs_7_, ...), custom_call_target="tpu_custom_call" | custom-call | flops 2415919104 | bytes 9437184 | tf_op jit(solution)/shard_map/score_mass/pallas_call | solution.py:157
  37.7 0.4 collective-permute-start.16
  38.1 0.0 collective-permute-done.7.refs_5_
  38.1 2.6 %index_grad.2 = (f32[128,128]{1,0:T(8,128)S(1)}, f32[128,128]{1,0:T(8,128)S(1)}, f32[128,128]{1,0:T(8,128)S(1)}, f32[128,128]{1,0:T(8,128)S(1)}, f32[128,128]{1,0:T(8,128)S(1)}, /*index=5*/f32[128,128]{1,0:T(8,128)S(1)}) custom-call(s32[16]{0:T(128)S(1)} %copy-done.4, s32[16,16]{1,0:T(8,128)S(1)} %copy-done.2, bf16[32,64,128]{2,1,0:T(8,128)(2,1)S(1)} %bitcast.14, ...), custom_call_target="tpu_custom_call" | custom-call | flops 1610612736 | bytes 6291456 | tf_op jit(solution)/shard_map/index_grad/pallas_call | solution.py:314
  40.8 0.1 collective-permute-start.9
  40.8 0.5 collective-permute-start.11
  41.3 0.9 %index_logits.3.refs_6_ = f32[128,128]{1,0:T(8,128)S(1)} custom-call(s32[16]{0:T(128)S(1)} %copy-done.4, s32[16,16]{1,0:T(8,128)S(1)} %copy-done.2, bf16[32,64,128]{2,1,0:T(8,128)(2,1)S(1)} %bitcast.15, bf16[32,64,128]{2,1,0:T(8,128)(2,1)S(1)} %bitcast.19, f32[32,128]{1,0:T(8,128)S(1)} %bitcast.28, f32[32,128]{1,0:T(8,128)S(1)} %collective-permute-done.1.refs_3_, ...), custom_call_target="tpu_custom_call" | custom-call | flops 268435456 | bytes 1048576 | tf_op jit(solution)/shard_map/index_logits/pallas_call | solution.py:242
  42.2 4.9 %collective-permute-start.8 = (f32[128,128]{1,0:T(8,128)S(1)}, f32[128,128]{1,0:T(8,128)S(1)}, u32[]{:S(2)}, u32[]{:S(2)}) collective-permute-start(f32[128,128]{1,0:T(8,128)S(1)} %get-tuple-element.30), channel_id=1, source_target_pairs={{2,0},{16,2},{6,4},{20,6},{10,8},{24,10},{14,12},{28,14},{18,16},{... | collective-permute-start | bytes 196616 | tf_op jit(solution)/shard_map/ppermute | solution.py:394
  47.1 0.0 collective-permute-done.16.refs_5_
  47.1 0.8 %index_grad.3 = (f32[128,128]{1,0:T(8,128)S(1)}, f32[128,128]{1,0:T(8,128)S(1)}) custom-call(s32[16]{0:T(128)S(1)} %copy-done.4, s32[16,16]{1,0:T(8,128)S(1)} %copy-done.2, bf16[32,64,128]{2,1,0:T(8,128)(2,1)S(1)} %bitcast.16, bf16[32,64,128]{2,1,0:T(8,128)(2,1)S(1)} %bitcast.20, f32[32,128]{1,0:T(8,128)S(1)} %bitcast.29, ...), custom_call_target="tpu_custom_call" | custom-call | flops 536870912 | bytes 2097152 | tf_op jit(solution)/shard_map/index_grad/pallas_call | solution.py:314
  48.0 0.1 collective-permute-start.17
  48.0 0.0 collective-permute-done.9
  48.1 1.2 %collective-permute-start.10 = (f32[128,128]{1,0:T(8,128)S(1)}, f32[128,128]{1,0:T(8,128)S(1)}, u32[]{:S(2)}, u32[]{:S(2)}) collective-permute-start(f32[128,128]{1,0:T(8,128)S(1)} %add.28), channel_id=1, source_target_pairs={{0,28},{2,30},{4,0},{6,2},{8,4},{10,6},{12,8},{14,10},{16,12},{18,... | collective-permute-start | bytes 196616 | tf_op jit(solution)/shard_map/ppermute | solution.py:398
  49.2 0.0 collective-permute-done.11
  49.3 6.7 %collective-permute-start.12 = (f32[128,128]{1,0:T(8,128)S(1)}, f32[128,128]{1,0:T(8,128)S(1)}, u32[]{:S(2)}, u32[]{:S(2)}) collective-permute-start(f32[128,128]{1,0:T(8,128)S(1)} %add.30), channel_id=1, source_target_pairs={{0,24},{2,26},{4,28},{6,30},{8,0},{10,2},{12,4},{14,6},{16,8},{18,... | collective-permute-start | bytes 196616 | tf_op jit(solution)/shard_map/ppermute | solution.py:398
  56.0 0.0 collective-permute-done.17
  56.0 0.1 collective-permute-start.18
  56.1 2.9 %collective-permute-start.19 = (f32[128,128]{1,0:T(8,128)S(1)}, f32[128,128]{1,0:T(8,128)S(1)}, u32[]{:S(2)}, u32[]{:S(2)}) collective-permute-start(f32[128,128]{1,0:T(8,128)S(1)} %add.33), channel_id=1, source_target_pairs={{0,21},{1,20},{2,23},{3,22},{4,25},{5,24},{6,27},{7,26},{8,29},{9,... | collective-permute-start | bytes 196616 | tf_op jit(solution)/shard_map/ppermute | solution.py:406
  59.0 0.0 collective-permute-done.8
  59.0 0.0 collective-permute-done.10
  59.0 1.0 %collective-permute-done.12 = f32[128,128]{1,0:T(8,128)S(1)} collective-permute-done((f32[128,128]{1,0:T(8,128)S(1)}, f32[128,128]{1,0:T(8,128)S(1)}, u32[]{:S(2)}, u32[]{:S(2)}) %collective-permute-start.12) | collective-permute-done | bytes 65568 | tf_op jit(solution)/shard_map/ppermute | solution.py:398
  60.0 1.6 %collective-permute-start.13 = (f32[128,128]{1,0:T(8,128)S(1)}, f32[128,128]{1,0:T(8,128)S(1)}, u32[]{:S(2)}, u32[]{:S(2)}) collective-permute-start(f32[128,128]{1,0:T(8,128)S(1)} %add_add_fusion.1), channel_id=1, source_target_pairs={{0,1},{1,0},{2,3},{3,2},{4,5},{5,4},{6,7},{7,6},{8,9},{9,8},{10,11... | collective-permute-start | bytes 196616 | tf_op jit(solution)/shard_map/ppermute | solution.py:351
  61.5 0.5 collective-permute-done.18
  62.1 1.2 %collective-permute-done.19 = f32[128,128]{1,0:T(8,128)S(1)} collective-permute-done((f32[128,128]{1,0:T(8,128)S(1)}, f32[128,128]{1,0:T(8,128)S(1)}, u32[]{:S(2)}, u32[]{:S(2)}) %collective-permute-start.19) | collective-permute-done | bytes 65568 | tf_op jit(solution)/shard_map/ppermute | solution.py:406
  63.3 1.2 %collective-permute-done.13 = f32[128,128]{1,0:T(8,128)S(1)} collective-permute-done((f32[128,128]{1,0:T(8,128)S(1)}, f32[128,128]{1,0:T(8,128)S(1)}, u32[]{:S(2)}, u32[]{:S(2)}) %collective-permute-start.13) | collective-permute-done | bytes 65568 | tf_op jit(solution)/shard_map/ppermute | solution.py:351
  64.5 0.6 add_add_fusion
  (10 shorter events, 0.1 us)
Async XLA Ops:
  0.0 1.2 %copy-start.6 = (bf16[128,32,128]{2,1,0:T(8,128)(2,1)S(1)}, bf16[128,32,128]{2,1,0:T(8,128)(2,1)}, u32[]{:S(2)}) copy-start(bf16[128,32,128]{2,1,0:T(8,128)(2,1)} %queries_ref.1) | copy-start | bytes 3145732
  1.2 0.9 %copy-start.7 = (bf16[128,576]{0,1:T(8,128)(2,1)S(1)}, bf16[128,576]{0,1:T(8,128)(2,1)}, u32[]{:S(2)}) copy-start(bf16[128,576]{0,1:T(8,128)(2,1)} %param.10) | copy-start | bytes 442372
  2.1 0.8 %copy-start.8 = (bf16[128,128]{1,0:T(8,128)(2,1)S(1)}, bf16[128,128]{1,0:T(8,128)(2,1)}, u32[]{:S(2)}) copy-start(bf16[128,128]{1,0:T(8,128)(2,1)} %index_ref.1) | copy-start | bytes 98308
  2.9 12.4 %copy-start.3 = (f32[128,32]{0,1:T(8,128)S(1)}, f32[128,32]{0,1:T(8,128)}, u32[]{:S(2)}) copy-start(f32[128,32]{0,1:T(8,128)} %param.13) | copy-start | bytes 49156
  2.9 14.5 %copy-start = (bf16[128,64,576]{0,2,1:T(8,128)(2,1)S(1)}, bf16[128,64,576]{0,2,1:T(8,128)(2,1)}, u32[]{:S(2)}) copy-start(bf16[128,64,576]{0,2,1:T(8,128)(2,1)} %param.9) | copy-start | bytes 28311556
  2.9 14.5 %copy-start.1 = (f32[128,64]{0,1:T(8,128)S(1)}, f32[128,64]{0,1:T(8,128)}, u32[]{:S(2)}) copy-start(f32[128,64]{0,1:T(8,128)} %param.11) | copy-start | bytes 98308
  2.9 14.5 %copy-start.2 = (s32[16,16]{1,0:T(8,128)S(1)}, s32[16,16]{1,0:T(8,128)}, u32[]{:S(2)}) copy-start(s32[16,16]{1,0:T(8,128)} %live_ref.15) | copy-start | bytes 3076
  2.9 14.5 %copy-start.4 = (s32[16]{0:T(128)S(1)}, s32[16]{0:T(128)}, u32[]{:S(2)}) copy-start(s32[16]{0:T(128)} %order_ref.15) | copy-start | bytes 196
  3.3 11.5 %collective-permute-start.5 = (bf16[704,128]{1,0:T(8,128)(2,1)S(1)}, bf16[704,128]{1,0:T(8,128)(2,1)S(1)}, u32[]{:S(2)}, u32[]{:S(2)}) collective-permute-start(bf16[704,128]{1,0:T(8,128)(2,1)S(1)} %get-tuple-element.24.refs_0_.refs_5_.refs_7_), channel_id=1, source_target_pairs={{0,4},{2,6},{4,8},{6,10},{8,12},{10,14},{12,16},{14,18},{16,20},{1... | collective-permute-start | bytes 540680 | tf_op jit(solution)/shard_map/ppermute | solution.py:357
  6.3 13.8 %collective-permute-start.2 = (bf16[704,128]{1,0:T(8,128)(2,1)S(1)}, bf16[704,128]{1,0:T(8,128)(2,1)S(1)}, u32[]{:S(2)}, u32[]{:S(2)}) collective-permute-start(bf16[704,128]{1,0:T(8,128)(2,1)S(1)} %get-tuple-element.24.refs_0_.refs_5_.refs_7_), channel_id=1, source_target_pairs={{0,8},{2,10},{4,12},{6,14},{8,16},{10,18},{12,20},{14,22},{16,24},... | collective-permute-start | bytes 540680 | tf_op jit(solution)/shard_map/ppermute | solution.py:358
  14.8 5.8 %collective-permute-start.6 = (bf16[704,128]{1,0:T(8,128)(2,1)S(1)}, bf16[704,128]{1,0:T(8,128)(2,1)S(1)}, u32[]{:S(2)}, u32[]{:S(2)}) collective-permute-start(bf16[704,128]{1,0:T(8,128)(2,1)S(1)} %collective-permute-done.5.refs_0_.refs_6_.refs_8_), channel_id=1, source_target_pairs={{0,2},{2,0},{4,6},{6,4},{8,10},{10,8},{12,14},{14,12},{16,18},{18,... | collective-permute-start | bytes 540680 | tf_op jit(solution)/shard_map/ppermute | solution.py:363
  14.8 9.3 %collective-permute-start.14 = (bf16[704,128]{1,0:T(8,128)(2,1)S(1)}, bf16[704,128]{1,0:T(8,128)(2,1)S(1)}, u32[]{:S(2)}, u32[]{:S(2)}) collective-permute-start(bf16[704,128]{1,0:T(8,128)(2,1)S(1)} %collective-permute-done.5.refs_0_.refs_6_.refs_8_), channel_id=1, source_target_pairs={{0,8},{2,10},{4,12},{6,14},{8,16},{10,18},{12,20},{14,22},{16,24},... | collective-permute-start | bytes 540680 | tf_op jit(solution)/shard_map/ppermute | solution.py:362
  14.8 12.1 %collective-permute-start.4 = (bf16[704,128]{1,0:T(8,128)(2,1)S(1)}, bf16[704,128]{1,0:T(8,128)(2,1)S(1)}, u32[]{:S(2)}, u32[]{:S(2)}) collective-permute-start(bf16[704,128]{1,0:T(8,128)(2,1)S(1)} %get-tuple-element.24.refs_0_.refs_5_.refs_7_), channel_id=1, source_target_pairs={{0,2},{2,16},{4,6},{6,20},{8,10},{10,24},{12,14},{14,28},{16,18},{... | collective-permute-start | bytes 540680 | tf_op jit(solution)/shard_map/ppermute | solution.py:359
  15.3 14.5 %collective-permute-start.1 = (f32[32,128]{1,0:T(8,128)S(1)}, f32[32,128]{1,0:T(8,128)S(1)}, u32[]{:S(2)}, u32[]{:S(2)}) collective-permute-start(f32[32,128]{1,0:T(8,128)S(1)} %bitcast.25), channel_id=1, source_target_pairs={{0,1},{1,0},{2,3},{3,2},{4,5},{5,4},{6,7},{7,6},{8,9},{9,8},{10,11... | collective-permute-start | bytes 49160 | tf_op jit(solution)/shard_map/ppermute | solution.py:351
  20.1 14.9 %copy-start.5 = (f32[128]{0:T(128)S(1)}, f32[128]{0:T(128)}, u32[]{:S(2)}) copy-start(f32[128]{0:T(128)} %param.15) | copy-start | bytes 1540
  20.2 14.9 %collective-permute-start = (bf16[64,32,128]{2,0,1:T(8,128)(2,1)S(1)}, bf16[64,32,128]{2,0,1:T(8,128)(2,1)S(1)}, u32[]{:S(2)}, u32[]{:S(2)}) collective-permute-start(bf16[64,32,128]{2,0,1:T(8,128)(2,1)S(1)} %copy.11), channel_id=1, source_target_pairs={{0,1},{1,0},{2,3},{3,2},{4,5},{5,4},{6,7},{7,6},{8,9},{9,8},{10,11... | collective-permute-start | bytes 1572872 | tf_op jit(solution)/shard_map/ppermute | solution.py:351
  20.6 6.3 %collective-permute-start.3 = (bf16[704,128]{1,0:T(8,128)(2,1)S(1)}, bf16[704,128]{1,0:T(8,128)(2,1)S(1)}, u32[]{:S(2)}, u32[]{:S(2)}) collective-permute-start(bf16[704,128]{1,0:T(8,128)(2,1)S(1)} %collective-permute-done.2.refs_0_.refs_8_.refs_10_), channel_id=1, source_target_pairs={{0,2},{2,0},{4,6},{6,4},{8,10},{10,8},{12,14},{14,12},{16,18},{18,... | collective-permute-start | bytes 540680 | tf_op jit(solution)/shard_map/ppermute | solution.py:363
  24.1 12.7 %collective-permute-start.15 = (bf16[704,128]{1,0:T(8,128)(2,1)S(1)}, bf16[704,128]{1,0:T(8,128)(2,1)S(1)}, u32[]{:S(2)}, u32[]{:S(2)}) collective-permute-start(bf16[704,128]{1,0:T(8,128)(2,1)S(1)} %collective-permute-done.14.refs_0_.refs_5_.refs_7_), channel_id=1, source_target_pairs={{0,2},{2,0},{4,6},{6,4},{8,10},{10,8},{12,14},{14,12},{16,18},{18,... | collective-permute-start | bytes 540680 | tf_op jit(solution)/shard_map/ppermute | solution.py:363
  28.1 10.1 %collective-permute-start.7 = (f32[384,128]{1,0:T(8,128)S(1)}, f32[384,128]{1,0:T(8,128)S(1)}, u32[]{:S(2)}, u32[]{:S(2)}) collective-permute-start(f32[384,128]{1,0:T(8,128)S(1)} %get-tuple-element.28), channel_id=1, source_target_pairs={{0,1},{1,0},{2,3},{3,2},{4,5},{5,4},{6,7},{7,6},{8,9},{9,8},{10,11... | collective-permute-start | bytes 589832 | tf_op jit(solution)/shard_map/ppermute | solution.py:351
  37.7 9.5 %collective-permute-start.16 = (f32[128,128]{1,0:T(8,128)S(1)}, f32[128,128]{1,0:T(8,128)S(1)}, u32[]{:S(2)}, u32[]{:S(2)}) collective-permute-start(f32[128,128]{1,0:T(8,128)S(1)} %get-tuple-element.36), channel_id=1, source_target_pairs={{0,1},{1,0},{2,3},{3,2},{4,5},{5,4},{6,7},{7,6},{8,9},{9,8},{10,11... | collective-permute-start | bytes 196616 | tf_op jit(solution)/shard_map/ppermute | solution.py:351
  40.8 7.3 %collective-permute-start.9 = (f32[128,128]{1,0:T(8,128)S(1)}, f32[128,128]{1,0:T(8,128)S(1)}, u32[]{:S(2)}, u32[]{:S(2)}) collective-permute-start(f32[128,128]{1,0:T(8,128)S(1)} %get-tuple-element.32), channel_id=1, source_target_pairs={{0,2},{2,0},{4,6},{6,4},{8,10},{10,8},{12,14},{14,12},{16,18},{18,... | collective-permute-start | bytes 196616 | tf_op jit(solution)/shard_map/ppermute | solution.py:396
  40.8 8.4 %collective-permute-start.11 = (f32[128,128]{1,0:T(8,128)S(1)}, f32[128,128]{1,0:T(8,128)S(1)}, u32[]{:S(2)}, u32[]{:S(2)}) collective-permute-start(f32[128,128]{1,0:T(8,128)S(1)} %get-tuple-element.34), channel_id=1, source_target_pairs={{0,2},{2,0},{4,6},{6,4},{8,10},{10,8},{12,14},{14,12},{16,18},{18,... | collective-permute-start | bytes 196616 | tf_op jit(solution)/shard_map/ppermute | solution.py:396
  42.2 16.8 %collective-permute-start.8 = (f32[128,128]{1,0:T(8,128)S(1)}, f32[128,128]{1,0:T(8,128)S(1)}, u32[]{:S(2)}, u32[]{:S(2)}) collective-permute-start(f32[128,128]{1,0:T(8,128)S(1)} %get-tuple-element.30), channel_id=1, source_target_pairs={{2,0},{16,2},{6,4},{20,6},{10,8},{24,10},{14,12},{28,14},{18,16},{... | collective-permute-start | bytes 196616 | tf_op jit(solution)/shard_map/ppermute | solution.py:394
  48.0 8.0 %collective-permute-start.17 = (f32[128,128]{1,0:T(8,128)S(1)}, f32[128,128]{1,0:T(8,128)S(1)}, u32[]{:S(2)}, u32[]{:S(2)}) collective-permute-start(f32[128,128]{1,0:T(8,128)S(1)} %get-tuple-element.38), channel_id=1, source_target_pairs={{0,2},{2,0},{4,6},{6,4},{8,10},{10,8},{12,14},{14,12},{16,18},{18,... | collective-permute-start | bytes 196616 | tf_op jit(solution)/shard_map/ppermute | solution.py:396
  48.1 10.9 %collective-permute-start.10 = (f32[128,128]{1,0:T(8,128)S(1)}, f32[128,128]{1,0:T(8,128)S(1)}, u32[]{:S(2)}, u32[]{:S(2)}) collective-permute-start(f32[128,128]{1,0:T(8,128)S(1)} %add.28), channel_id=1, source_target_pairs={{0,28},{2,30},{4,0},{6,2},{8,4},{10,6},{12,8},{14,10},{16,12},{18,... | collective-permute-start | bytes 196616 | tf_op jit(solution)/shard_map/ppermute | solution.py:398
  49.3 10.7 %collective-permute-start.12 = (f32[128,128]{1,0:T(8,128)S(1)}, f32[128,128]{1,0:T(8,128)S(1)}, u32[]{:S(2)}, u32[]{:S(2)}) collective-permute-start(f32[128,128]{1,0:T(8,128)S(1)} %add.30), channel_id=1, source_target_pairs={{0,24},{2,26},{4,28},{6,30},{8,0},{10,2},{12,4},{14,6},{16,8},{18,... | collective-permute-start | bytes 196616 | tf_op jit(solution)/shard_map/ppermute | solution.py:398
  56.0 6.1 %collective-permute-start.18 = (f32[128,128]{1,0:T(8,128)S(1)}, f32[128,128]{1,0:T(8,128)S(1)}, u32[]{:S(2)}, u32[]{:S(2)}) collective-permute-start(f32[128,128]{1,0:T(8,128)S(1)} %add.33), channel_id=1, source_target_pairs={{0,20},{1,21},{2,22},{3,23},{4,24},{5,25},{6,26},{7,27},{8,28},{9,... | collective-permute-start | bytes 196616 | tf_op jit(solution)/shard_map/ppermute | solution.py:406
  56.1 7.2 %collective-permute-start.19 = (f32[128,128]{1,0:T(8,128)S(1)}, f32[128,128]{1,0:T(8,128)S(1)}, u32[]{:S(2)}, u32[]{:S(2)}) collective-permute-start(f32[128,128]{1,0:T(8,128)S(1)} %add.33), channel_id=1, source_target_pairs={{0,21},{1,20},{2,23},{3,22},{4,25},{5,24},{6,27},{7,26},{8,29},{9,... | collective-permute-start | bytes 196616 | tf_op jit(solution)/shard_map/ppermute | solution.py:406
  60.0 4.5 %collective-permute-start.13 = (f32[128,128]{1,0:T(8,128)S(1)}, f32[128,128]{1,0:T(8,128)S(1)}, u32[]{:S(2)}, u32[]{:S(2)}) collective-permute-start(f32[128,128]{1,0:T(8,128)S(1)} %add_add_fusion.1), channel_id=1, source_target_pairs={{0,1},{1,0},{2,3},{3,2},{4,5},{5,4},{6,7},{7,6},{8,9},{9,8},{10,11... | collective-permute-start | bytes 196616 | tf_op jit(solution)/shard_map/ppermute | solution.py:351

commit v4 on v3

--- a/solution.py
+++ b/solution.py
@@ -14,7 +14,7 @@
 LOG2E = math.log2(math.e)
 MAIN_SCALE = 1.0 / 192.0**0.5
 LIMIT = 20 * 2**20
-PACK_COST = 10**10
+CUT_COST = 10**10
 NT = (((1,), (1,)), ((), ()))
 NN = (((1,), (0,)), ((), ()))
 VMEM = pl.BlockSpec(memory_space=pltpu.VMEM)
@@ -22,39 +22,35 @@
 HBM = pl.BlockSpec(memory_space=pltpu.HBM)
 
 
-def pack_kernel(latent_ref, index_ref, queries_ref, block_ref, *rest):
+def cut_kernel(block_ref, queries_ref, block_out, *rest):
+    del block_ref, block_out
     shares, sems = rest[:-1], rest[-1]
-    latent = latent_ref.shape[0]
-    rows = index_ref.shape[0]
     n, share = len(shares), shares[0].shape[0]
-    copies = [
-        (latent_ref, block_ref.at[pl.ds(0, latent)]),
-        (index_ref, block_ref.at[pl.ds(latent, rows)]),
-    ]
+    copies = []
     for turn, out in enumerate(shares):
         start = lax.rem(lax.axis_index("head") + turn, n) * share
-        copies.append((queries_ref.at[pl.ds(start, share)], out))
-    copies = [pltpu.make_async_copy(a, b, sems.at[i]) for i, (a, b) in enumerate(copies)]
+        part = queries_ref.at[pl.ds(start, share)]
+        copies.append(pltpu.make_async_copy(part, out, sems.at[turn]))
     for copy in copies:
         copy.start()
     for copy in copies:
         copy.wait()
 
 
-def packed_inputs(latent_keys, index_keys, index_queries, n_head):
-    latent, rows = latent_keys.shape
+def cut_shares(block, index_queries, n_head):
     tokens, index_here, idx_width = index_queries.shape
     share = jax.ShapeDtypeStruct((tokens // n_head, index_here, idx_width), index_queries.dtype)
     block, *shares = pl.pallas_call(
-        pack_kernel,
-        in_specs=[HBM] * 3,
+        cut_kernel,
+        in_specs=[VMEM, HBM],
         out_specs=[VMEM] * (1 + n_head),
-        out_shape=[jax.ShapeDtypeStruct((latent + rows, rows), latent_keys.dtype)] + [share] * n_head,
-        scratch_shapes=[pltpu.SemaphoreType.DMA((2 + n_head,))],
-        cost_estimate=cost(PACK_COST),
+        out_shape=[jax.ShapeDtypeStruct(block.shape, block.dtype)] + [share] * n_head,
+        input_output_aliases={0: 0},
+        scratch_shapes=[pltpu.SemaphoreType.DMA((n_head,))],
+        cost_estimate=cost(CUT_COST),
         compiler_params=pltpu.CompilerParams(vmem_limit_bytes=LIMIT),
-        name="pack_keys",
-    )(latent_keys, index_keys, index_queries)
+        name="cut_shares",
+    )(block, index_queries)
     return block, shares
 
 
@@ -92,12 +88,15 @@
     return pl.ds(pl.multiple_of(place * rows, rows), blocks * rows)
 
 
-def in_pairs(count, rows, work):
+def in_pairs(count, most, rows, work):
     def two(i, carry):
         work(at(2 * i, rows, 2))
         return carry
 
-    lax.fori_loop(0, count // 2, two, 0)
+    if most == 2:
+        pl.when(count == 2)(lambda: work(pl.ds(0, 2 * rows)))
+    elif most > 2:
+        lax.fori_loop(0, count // 2, two, 0)
 
     @pl.when(count % 2 == 1)
     def _():
@@ -133,7 +132,7 @@
                 total = p if total is None else total + p
         mass[here, :] = total
 
-    in_pairs(count, rows, work)
+    in_pairs(count, len(blocks), rows, work)
     values = [jnp.where(alive, mass[at(place, rows), :], 0.0) for place, _, alive in slots]
     if not pack:
         for out, value in zip(outs, values):
@@ -231,7 +230,7 @@
             logits = logits + acc[:, first : first + share]
         values[here, :] = jnp.exp(logits * scale - lse)
 
-    in_pairs(count, rows, work)
+    in_pairs(count, len(blocks), rows, work)
     out_ref[...] = side_by_side([jnp.where(s[2], values[at(s[0], rows), :], 0.0) for s in slots])
 
 
@@ -302,7 +301,7 @@
                 )
         results[here, :] = total * scale
 
-    in_pairs(count, rows, work)
+    in_pairs(count, len(blocks), rows, work)
     for out, (place, _, alive) in zip(outs, slots):
         out[...] = jnp.where(alive, results[at(place, rows), :], 0.0)
 
@@ -353,7 +352,8 @@
     forward = [(i, (i + (HOPS - 1 if i % 2 else 1)) % n_seq) for i in devices]
     back = [(b, a) for a, b in forward]
     swap = [(i, i ^ 1) for i in devices]
-    own, shares = packed_inputs(latent_keys.T, index_keys, index_queries, n_head)
+    own = jnp.concatenate([latent_keys.T, index_keys], axis=0)
+    own, shares = cut_shares(own, index_queries, n_head)
     arrived = [lax.ppermute(own, "seq", ring(2))]
     arrived.append(lax.ppermute(own, "seq", ring(4)))
     slots = [own, lax.ppermute(own, "seq", forward)]
@@ -403,9 +403,9 @@
         route = [
             (2 * i + x, 2 * ((i - 2 * m) % n_seq) + (x + turn) % 2) for i in devices for x in range(2)
         ]
-        last.append(lax.ppermute(both, ("seq", "head"), route))
+        last.append(lax.ppermute(both.astype(jnp.bfloat16), ("seq", "head"), route))
     total = total + around(total, 1)
-    return total + (last[0] + last[1])
+    return total + (last[0].astype(jnp.float32) + last[1].astype(jnp.float32))
 
 
 def solution(mesh):

time: 65.3 us -> 65.8 us (level); the launches traced: 65.1 us -> 64.5 us
  local copies, waits for them, and re-layouts: 3.33 us -> 1.66 us
  other arithmetic: 0.7 us -> 1.64 us
  starting transfers between devices: 27.4 us -> 28.3 us
    ppermute x2, waiting for transfers between devices: 1.75 us -> 5.5 us  [body(): last.append(lax.ppermute(both.astype(jnp.bfloat16), ('seq', 'head'), route))]
    ppermute x1, waiting for transfers between devices: 3.5 us -> 0.01 us  [body(): arrived.append(lax.ppermute(arrived[m - 3], 'seq', ring(4)))]
    ppermute x2, starting transfers between devices: 2.98 us -> 1.27 us  [body(): last.append(lax.ppermute(both.astype(jnp.bfloat16), ('seq', 'head'), route))]
    ppermute x2, starting transfers between devices: 7.9 us -> 6.19 us  [body(): total = total + lax.ppermute(both, 'seq', ring(-2 * m))]
    unnamed x18 -> x14, local copies, waits for them, and re-layouts: 2.92 us -> 1.25 us
    ppermute x3, starting transfers between devices: 0.64 us -> 2.13 us  [body(): both = grads[2 * m] + lax.ppermute(grads[2 * m + 1], 'seq', swap)]
    ppermute x3, starting transfers between devices: 0.01 us -> 1.46 us  [body(): slots += [arrived[m - 1], lax.ppermute(arrived[m - 1], 'seq', swap)]]
    ppermute x5, starting transfers between devices: 5.8 us -> 6.91 us  [around(): lax.ppermute(array, 'head', [(i, (i + turn) % n_head) for i in range(n_he...]
  transfers between devices with their start and end apart: 20 -> 20, of which waited for: 7 -> 4; matrix products, arithmetic and copies ran while one was open for 1% -> 1% of each run, Pallas kernels for 21% -> 21%
where the time goes in v4:
time: 65.8 us; the launch traced here: 64.5 us
  starting transfers between devices  28.3 us (43%)
  waiting for transfers between devices  19.1 us (29%)
  Pallas kernels  13.5 us (21%)
  local copies, waits for them, and re-layouts  1.66 us (3%)
  other arithmetic  1.64 us (2%)
    pallas_call x4, Pallas kernels, head_mass(): pl.pallas_call(functools.partial(score_kernel, ids, len(shapes), n_head >...  7.55 us
    ppermute x5, starting transfers between devices, around(): lax.ppermute(array, 'head', [(i, (i + turn) % n_head) for i in range(n_he...  6.91 us
    ppermute x1, waiting for transfers between devices, body(): arrived = [lax.ppermute(own, 'seq', ring(2))]  6.86 us
    ppermute x5, waiting for transfers between devices, around(): lax.ppermute(array, 'head', [(i, (i + turn) % n_head) for i in range(n_he...  6.71 us
    ppermute x2, starting transfers between devices, body(): total = total + lax.ppermute(both, 'seq', ring(-2 * m))  6.19 us
    ppermute x2, waiting for transfers between devices, body(): last.append(lax.ppermute(both.astype(jnp.bfloat16), ('seq', 'head'), route))  5.5 us
    ppermute x1, starting transfers between devices, body(): total = grads[0] + lax.ppermute(grads[1], 'seq', back)  5.16 us
    pallas_call x2, Pallas kernels, index_grad(): pl.pallas_call(functools.partial(grad_kernel, latent, ids, n_head), in_sp...  3.25 us
  transfers between devices with their start and end apart: 20, of which 4 were waited for; matrix products, arithmetic and copies ran while one was open for 1% of the time, Pallas kernels for 21%

profile of v4, /device:TPU:0, one launch (start us, length us, event | category | flops | bytes accessed | tf_op | source)
XLA Modules:
  0.0 64.5 jit_solution(2205509919845041665)
XLA Ops:
  0.0 0.9 %pad_maximum_fusion.block_ref = bf16[704,128]{1,0:T(8,128)(2,1)S(1)} fusion(bf16[128,128]{1,0:T(8,128)(2,1)} %param.14, bf16[576,128]{1,0:T(8,128)(2,1)} %bitcast.32), kind=kLoop, calls=%fused_computation.1 | loop fusion | flops 360448 | bytes 360448 | tf_op jit(solution)/shard_map/concatenate | solution.py:355
  0.9 0.0 copy-start.6
  1.0 1.2 %copy-done.6 = bf16[128,32,128]{2,1,0:T(8,128)(2,1)S(1)} copy-done((bf16[128,32,128]{2,1,0:T(8,128)(2,1)S(1)}, bf16[128,32,128]{2,1,0:T(8,128)(2,1)}, u32[]{:S(2)}) %copy-start.6) | copy-done | bytes 1048600
  2.2 0.0 copy-start
  2.2 0.1 cut_shares.1
  2.3 3.0 %collective-permute-start.5 = (bf16[704,128]{1,0:T(8,128)(2,1)S(1)}, bf16[704,128]{1,0:T(8,128)(2,1)S(1)}, u32[]{:S(2)}, u32[]{:S(2)}) collective-permute-start(bf16[704,128]{1,0:T(8,128)(2,1)S(1)} %get-tuple-element.24.refs_0_.refs_5_.refs_7_), channel_id=1, source_target_pairs={{0,4},{2,6},{4,8},{6,10},{8,12},{10,14},{12,16},{14,18},{16,20},{1... | collective-permute-start | bytes 540680 | tf_op jit(solution)/shard_map/ppermute | solution.py:357
  5.3 1.6 %collective-permute-start.2 = (bf16[704,128]{1,0:T(8,128)(2,1)S(1)}, bf16[704,128]{1,0:T(8,128)(2,1)S(1)}, u32[]{:S(2)}, u32[]{:S(2)}) collective-permute-start(bf16[704,128]{1,0:T(8,128)(2,1)S(1)} %get-tuple-element.24.refs_0_.refs_5_.refs_7_), channel_id=1, source_target_pairs={{0,8},{2,10},{4,12},{6,14},{8,16},{10,18},{12,20},{14,22},{16,24},... | collective-permute-start | bytes 540680 | tf_op jit(solution)/shard_map/ppermute | solution.py:358
  6.9 6.9 %collective-permute-done.5.refs_0_.refs_6_.refs_8_ = bf16[704,128]{1,0:T(8,128)(2,1)S(1)} collective-permute-done((bf16[704,128]{1,0:T(8,128)(2,1)S(1)}, bf16[704,128]{1,0:T(8,128)(2,1)S(1)}, u32[]{:S(2)}, u32[]{:S(2)}) %collective-permute-start.5) | collective-permute-done | bytes 180256 | tf_op jit(solution)/shard_map/ppermute | solution.py:357
  13.8 0.0 collective-permute-start.6
  13.8 0.5 collective-permute-start.4
  14.3 0.2 copy.12
  14.5 1.7 %collective-permute-start = (bf16[64,32,128]{2,0,1:T(8,128)(2,1)S(1)}, bf16[64,32,128]{2,0,1:T(8,128)(2,1)S(1)}, u32[]{:S(2)}, u32[]{:S(2)}) collective-permute-start(bf16[64,32,128]{2,0,1:T(8,128)(2,1)S(1)} %copy.12), channel_id=1, source_target_pairs={{0,1},{1,0},{2,3},{3,2},{4,5},{5,4},{6,7},{7,6},{8,9},{9,8},{10,11... | collective-permute-start | bytes 1572872 | tf_op jit(solution)/shard_map/ppermute | solution.py:350
  16.2 0.0 copy-done
  16.2 0.0 copy-done.1
  16.2 0.0 copy-done.2
  16.2 0.0 copy-done.4
  16.2 2.7 %score_mass.4.refs_3_ = f32[128,128]{1,0:T(8,128)S(1)} custom-call(s32[16]{0:T(128)S(1)} %copy-done.4, s32[16,16]{1,0:T(8,128)S(1)} %copy-done.2, bf16[64,576,128]{2,1,0:T(8,128)(2,1)S(1)} %bitcast.9, f32[64,128]{1,0:T(8,128)S(1)} %bitcast.21, bf16[704,128]{1,0:T(8,128)(2,1)S(1)} %get-tuple-element.24.refs_0_.refs_5_.refs_7_), custom_call_target="tpu_custom_call" | custom-call | flops 1207959552 | bytes 4718592 | tf_op jit(solution)/shard_map/score_mass/pallas_call | solution.py:156
  19.0 0.0 copy-start.3
  19.0 0.1 collective-permute-start.14
  19.0 0.0 collective-permute-done.2.refs_0_.refs_8_.refs_10_
  19.1 1.4 %collective-permute-start.3 = (bf16[704,128]{1,0:T(8,128)(2,1)S(1)}, bf16[704,128]{1,0:T(8,128)(2,1)S(1)}, u32[]{:S(2)}, u32[]{:S(2)}) collective-permute-start(bf16[704,128]{1,0:T(8,128)(2,1)S(1)} %collective-permute-done.2.refs_0_.refs_8_.refs_10_), channel_id=1, source_target_pairs={{0,2},{2,0},{4,6},{6,4},{8,10},{10,8},{12,14},{14,12},{16,18},{18,... | collective-permute-start | bytes 540680 | tf_op jit(solution)/shard_map/ppermute | solution.py:363
  20.4 0.0 collective-permute-done.6.refs_1_.refs_7_.refs_9_
  20.5 2.7 %score_mass.5 = (f32[128,128]{1,0:T(8,128)S(1)}, f32[128,128]{1,0:T(8,128)S(1)}) custom-call(s32[16]{0:T(128)S(1)} %copy-done.4, s32[16,16]{1,0:T(8,128)S(1)} %copy-done.2, bf16[64,576,128]{2,1,0:T(8,128)(2,1)S(1)} %bitcast.10, f32[64,128]{1,0:T(8,128)S(1)} %bitcast.22, bf16[704,128]{1,0:T(8,128)(2,1)S(1)} %collective-permute-done.5.refs_0_.refs_6_.refs_8_, ...), custom_call_target="tpu_custom_call" | custom-call | flops 2415919104 | bytes 9437184 | tf_op jit(solution)/shard_map/score_mass/pallas_call | solution.py:156
  23.2 0.0 copy-start.5
  23.2 0.0 collective-permute-done.4.refs_2_.refs_10_.refs_12_
  23.2 0.0 collective-permute-done.3.refs_1_.refs_9_.refs_11_
  23.2 1.2 %score_mass.6 = (f32[384,128]{1,0:T(8,128)S(1)}, f32[384,128]{1,0:T(8,128)S(1)}) custom-call(s32[16]{0:T(128)S(1)} %copy-done.4, s32[16,16]{1,0:T(8,128)S(1)} %copy-done.2, bf16[64,576,128]{2,1,0:T(8,128)(2,1)S(1)} %bitcast.11, f32[64,128]{1,0:T(8,128)S(1)} %bitcast.23, bf16[704,128]{1,0:T(8,128)(2,1)S(1)} %collective-permute-done.2.refs_0_.refs_8_.refs_10_, ...), custom_call_target="tpu_custom_call" | custom-call | flops 3623878656 | bytes 14155776 | tf_op jit(solution)/shard_map/score_mass/pallas_call | solution.py:156
  24.4 1.2 %collective-permute-start.7 = (f32[384,128]{1,0:T(8,128)S(1)}, f32[384,128]{1,0:T(8,128)S(1)}, u32[]{:S(2)}, u32[]{:S(2)}) collective-permute-start(f32[384,128]{1,0:T(8,128)S(1)} %get-tuple-element.28), channel_id=1, source_target_pairs={{0,1},{1,0},{2,3},{3,2},{4,5},{5,4},{6,7},{7,6},{8,9},{9,8},{10,11... | collective-permute-start | bytes 589832 | tf_op jit(solution)/shard_map/ppermute | solution.py:350
  25.7 0.0 copy-done.3
  25.7 0.9 %collective-permute-start.1 = (f32[32,128]{1,0:T(8,128)S(1)}, f32[32,128]{1,0:T(8,128)S(1)}, u32[]{:S(2)}, u32[]{:S(2)}) collective-permute-start(f32[32,128]{1,0:T(8,128)S(1)} %bitcast.25), channel_id=1, source_target_pairs={{0,1},{1,0},{2,3},{3,2},{4,5},{5,4},{6,7},{7,6},{8,9},{9,8},{10,11... | collective-permute-start | bytes 49160 | tf_op jit(solution)/shard_map/ppermute | solution.py:350
  26.5 0.2 copy.14
  26.7 0.0 collective-permute-done.14.refs_0_.refs_5_.refs_7_
  26.7 0.1 collective-permute-start.15
  26.8 6.7 %collective-permute-done.1.refs_3_ = f32[32,128]{1,0:T(8,128)S(1)} collective-permute-done((f32[32,128]{1,0:T(8,128)S(1)}, f32[32,128]{1,0:T(8,128)S(1)}, u32[]{:S(2)}, u32[]{:S(2)}) %collective-permute-start.1) | collective-permute-done | bytes 16416 | tf_op jit(solution)/shard_map/ppermute | solution.py:350
  33.5 0.0 collective-permute-done
  33.5 0.0 copy-done.5
  33.5 1.7 %index_logits.2.refs_6_ = f32[384,128]{1,0:T(8,128)S(1)} custom-call(s32[16]{0:T(128)S(1)} %copy-done.4, s32[16,16]{1,0:T(8,128)S(1)} %copy-done.2, bf16[32,64,128]{2,1,0:T(8,128)(2,1)S(1)} %bitcast.13, bf16[32,64,128]{2,1,0:T(8,128)(2,1)S(1)} %bitcast.17, f32[32,128]{1,0:T(8,128)S(1)} %bitcast.26, f32[32,128]{1,0:T(8,128)S(1)} %collective-permute-done.1.refs_3_, ...), custom_call_target="tpu_custom_call" | custom-call | flops 805306368 | bytes 3145728 | tf_op jit(solution)/shard_map/index_logits/pallas_call | solution.py:241
  35.3 0.0 collective-permute-done.7.refs_5_
  35.3 2.4 %index_grad.2 = (f32[128,128]{1,0:T(8,128)S(1)}, f32[128,128]{1,0:T(8,128)S(1)}, f32[128,128]{1,0:T(8,128)S(1)}, f32[128,128]{1,0:T(8,128)S(1)}, f32[128,128]{1,0:T(8,128)S(1)}, /*index=5*/f32[128,128]{1,0:T(8,128)S(1)}) custom-call(s32[16]{0:T(128)S(1)} %copy-done.4, s32[16,16]{1,0:T(8,128)S(1)} %copy-done.2, bf16[32,64,128]{2,1,0:T(8,128)(2,1)S(1)} %bitcast.14, ...), custom_call_target="tpu_custom_call" | custom-call | flops 1610612736 | bytes 6291456 | tf_op jit(solution)/shard_map/index_grad/pallas_call | solution.py:313
  37.7 0.1 collective-permute-start.9
  37.8 0.5 collective-permute-start.11
  38.3 0.0 collective-permute-done.15.refs_1_.refs_6_.refs_8_
  38.3 0.9 %score_mass.7 = (f32[128,128]{1,0:T(8,128)S(1)}, f32[128,128]{1,0:T(8,128)S(1)}) custom-call(s32[16]{0:T(128)S(1)} %copy-done.4, s32[16,16]{1,0:T(8,128)S(1)} %copy-done.2, bf16[64,576,128]{2,1,0:T(8,128)(2,1)S(1)} %bitcast.12, f32[64,128]{1,0:T(8,128)S(1)} %bitcast.24, bf16[704,128]{1,0:T(8,128)(2,1)S(1)} %collective-permute-done.14.refs_0_.refs_5_.refs_7_, ...), custom_call_target="tpu_custom_call" | custom-call | flops 2415919104 | bytes 9437184 | tf_op jit(solution)/shard_map/score_mass/pallas_call | solution.py:156
  39.2 1.6 %collective-permute-start.16 = (f32[128,128]{1,0:T(8,128)S(1)}, f32[128,128]{1,0:T(8,128)S(1)}, u32[]{:S(2)}, u32[]{:S(2)}) collective-permute-start(f32[128,128]{1,0:T(8,128)S(1)} %get-tuple-element.36), channel_id=1, source_target_pairs={{0,1},{1,0},{2,3},{3,2},{4,5},{5,4},{6,7},{7,6},{8,9},{9,8},{10,11... | collective-permute-start | bytes 196616 | tf_op jit(solution)/shard_map/ppermute | solution.py:350
  40.7 5.2 %collective-permute-start.8 = (f32[128,128]{1,0:T(8,128)S(1)}, f32[128,128]{1,0:T(8,128)S(1)}, u32[]{:S(2)}, u32[]{:S(2)}) collective-permute-start(f32[128,128]{1,0:T(8,128)S(1)} %get-tuple-element.30), channel_id=1, source_target_pairs={{2,0},{16,2},{6,4},{20,6},{10,8},{24,10},{14,12},{28,14},{18,16},{... | collective-permute-start | bytes 196616 | tf_op jit(solution)/shard_map/ppermute | solution.py:394
  45.9 0.0 collective-permute-done.9
  45.9 0.1 collective-permute-start.10
  46.0 0.0 collective-permute-done.11
  46.0 6.1 %collective-permute-start.12 = (f32[128,128]{1,0:T(8,128)S(1)}, f32[128,128]{1,0:T(8,128)S(1)}, u32[]{:S(2)}, u32[]{:S(2)}) collective-permute-start(f32[128,128]{1,0:T(8,128)S(1)} %add.30), channel_id=1, source_target_pairs={{0,24},{2,26},{4,28},{6,30},{8,0},{10,2},{12,4},{14,6},{16,8},{18,... | collective-permute-start | bytes 196616 | tf_op jit(solution)/shard_map/ppermute | solution.py:398
  52.1 0.9 %index_logits.3.refs_6_ = f32[128,128]{1,0:T(8,128)S(1)} custom-call(s32[16]{0:T(128)S(1)} %copy-done.4, s32[16,16]{1,0:T(8,128)S(1)} %copy-done.2, bf16[32,64,128]{2,1,0:T(8,128)(2,1)S(1)} %bitcast.15, bf16[32,64,128]{2,1,0:T(8,128)(2,1)S(1)} %bitcast.19, f32[32,128]{1,0:T(8,128)S(1)} %bitcast.28, f32[32,128]{1,0:T(8,128)S(1)} %collective-permute-done.1.refs_3_, ...), custom_call_target="tpu_custom_call" | custom-call | flops 268435456 | bytes 1048576 | tf_op jit(solution)/shard_map/index_logits/pallas_call | solution.py:241
  53.0 0.0 collective-permute-done.16.refs_5_
  53.1 0.8 %index_grad.3 = (f32[128,128]{1,0:T(8,128)S(1)}, f32[128,128]{1,0:T(8,128)S(1)}) custom-call(s32[16]{0:T(128)S(1)} %copy-done.4, s32[16,16]{1,0:T(8,128)S(1)} %copy-done.2, bf16[32,64,128]{2,1,0:T(8,128)(2,1)S(1)} %bitcast.16, bf16[32,64,128]{2,1,0:T(8,128)(2,1)S(1)} %bitcast.20, f32[32,128]{1,0:T(8,128)S(1)} %bitcast.29, ...), custom_call_target="tpu_custom_call" | custom-call | flops 536870912 | bytes 2097152 | tf_op jit(solution)/shard_map/index_grad/pallas_call | solution.py:313
  53.9 1.6 %collective-permute-start.17 = (f32[128,128]{1,0:T(8,128)S(1)}, f32[128,128]{1,0:T(8,128)S(1)}, u32[]{:S(2)}, u32[]{:S(2)}) collective-permute-start(f32[128,128]{1,0:T(8,128)S(1)} %get-tuple-element.38), channel_id=1, source_target_pairs={{0,2},{2,0},{4,6},{6,4},{8,10},{10,8},{12,14},{14,12},{16,18},{18,... | collective-permute-start | bytes 196616 | tf_op jit(solution)/shard_map/ppermute | solution.py:396
  55.5 0.0 collective-permute-done.8
  55.5 0.0 collective-permute-done.10
  55.5 0.0 collective-permute-done.12
  55.5 1.6 %collective-permute-start.13 = (f32[128,128]{1,0:T(8,128)S(1)}, f32[128,128]{1,0:T(8,128)S(1)}, u32[]{:S(2)}, u32[]{:S(2)}) collective-permute-start(f32[128,128]{1,0:T(8,128)S(1)} %add_add_fusion.1), channel_id=1, source_target_pairs={{0,1},{1,0},{2,3},{3,2},{4,5},{5,4},{6,7},{7,6},{8,9},{9,8},{10,11... | collective-permute-start | bytes 196616 | tf_op jit(solution)/shard_map/ppermute | solution.py:350
  57.1 0.0 collective-permute-done.17
  57.1 1.1 %collective-permute-start.18 = (bf16[128,128]{1,0:T(8,128)(2,1)S(1)}, bf16[128,128]{1,0:T(8,128)(2,1)S(1)}, u32[]{:S(2)}, u32[]{:S(2)}) collective-permute-start(bf16[128,128]{1,0:T(8,128)(2,1)S(1)} %add_convert_fusion), channel_id=1, source_target_pairs={{0,20},{1,21},{2,22},{3,23},{4,24},{5,25},{6,26},{7,27},{8,28},{9,... | collective-permute-start | bytes 98312 | tf_op jit(solution)/shard_map/ppermute | solution.py:406
  58.1 0.2 collective-permute-start.19
  58.3 3.8 %collective-permute-done.18 = bf16[128,128]{1,0:T(8,128)(2,1)S(1)} collective-permute-done((bf16[128,128]{1,0:T(8,128)(2,1)S(1)}, bf16[128,128]{1,0:T(8,128)(2,1)S(1)}, u32[]{:S(2)}, u32[]{:S(2)}) %collective-permute-start.18) | collective-permute-done | bytes 32800 | tf_op jit(solution)/shard_map/ppermute | solution.py:406
  62.2 1.7 %collective-permute-done.19 = bf16[128,128]{1,0:T(8,128)(2,1)S(1)} collective-permute-done((bf16[128,128]{1,0:T(8,128)(2,1)S(1)}, bf16[128,128]{1,0:T(8,128)(2,1)S(1)}, u32[]{:S(2)}, u32[]{:S(2)}) %collective-permute-start.19) | collective-permute-done | bytes 32800 | tf_op jit(solution)/shard_map/ppermute | solution.py:406
  63.8 0.0 collective-permute-done.13
  63.8 0.6 %add_add_fusion = f32[128,128]{1,0:T(8,128)} fusion(bf16[128,128]{1,0:T(8,128)(2,1)S(1)} %collective-permute-done.19, bf16[128,128]{1,0:T(8,128)(2,1)S(1)} %collective-permute-done.18, f32[128,128]{1,0:T(8,128)S(1)} %add_add_fusion.1, f32[128,128]{1,0:T(8,128)S(1)} %collective-permute-done.13), kind=kLoop, calls=%fused_computation.2 | loop fusion | flops 81920 | bytes 262144 | tf_op jit(solution)/shard_map/add | solution.py:408
  (7 shorter events, 0.1 us)
Async XLA Ops:
  0.9 1.2 %copy-start.6 = (bf16[128,32,128]{2,1,0:T(8,128)(2,1)S(1)}, bf16[128,32,128]{2,1,0:T(8,128)(2,1)}, u32[]{:S(2)}) copy-start(bf16[128,32,128]{2,1,0:T(8,128)(2,1)} %queries_ref.1) | copy-start | bytes 3145732
  2.2 14.0 %copy-start = (bf16[128,64,576]{0,2,1:T(8,128)(2,1)S(1)}, bf16[128,64,576]{0,2,1:T(8,128)(2,1)}, u32[]{:S(2)}) copy-start(bf16[128,64,576]{0,2,1:T(8,128)(2,1)} %param.9) | copy-start | bytes 28311556
  2.2 14.0 %copy-start.1 = (f32[128,64]{0,1:T(8,128)S(1)}, f32[128,64]{0,1:T(8,128)}, u32[]{:S(2)}) copy-start(f32[128,64]{0,1:T(8,128)} %param.11) | copy-start | bytes 98308
  2.2 14.1 %copy-start.2 = (s32[16,16]{1,0:T(8,128)S(1)}, s32[16,16]{1,0:T(8,128)}, u32[]{:S(2)}) copy-start(s32[16,16]{1,0:T(8,128)} %live_ref.15) | copy-start | bytes 3076
  2.2 14.1 %copy-start.4 = (s32[16]{0:T(128)S(1)}, s32[16]{0:T(128)}, u32[]{:S(2)}) copy-start(s32[16]{0:T(128)} %order_ref.15) | copy-start | bytes 196
  2.3 11.5 %collective-permute-start.5 = (bf16[704,128]{1,0:T(8,128)(2,1)S(1)}, bf16[704,128]{1,0:T(8,128)(2,1)S(1)}, u32[]{:S(2)}, u32[]{:S(2)}) collective-permute-start(bf16[704,128]{1,0:T(8,128)(2,1)S(1)} %get-tuple-element.24.refs_0_.refs_5_.refs_7_), channel_id=1, source_target_pairs={{0,4},{2,6},{4,8},{6,10},{8,12},{10,14},{12,16},{14,18},{16,20},{1... | collective-permute-start | bytes 540680 | tf_op jit(solution)/shard_map/ppermute | solution.py:357
  5.3 13.7 %collective-permute-start.2 = (bf16[704,128]{1,0:T(8,128)(2,1)S(1)}, bf16[704,128]{1,0:T(8,128)(2,1)S(1)}, u32[]{:S(2)}, u32[]{:S(2)}) collective-permute-start(bf16[704,128]{1,0:T(8,128)(2,1)S(1)} %get-tuple-element.24.refs_0_.refs_5_.refs_7_), channel_id=1, source_target_pairs={{0,8},{2,10},{4,12},{6,14},{8,16},{10,18},{12,20},{14,22},{16,24},... | collective-permute-start | bytes 540680 | tf_op jit(solution)/shard_map/ppermute | solution.py:358
  13.8 6.7 %collective-permute-start.6 = (bf16[704,128]{1,0:T(8,128)(2,1)S(1)}, bf16[704,128]{1,0:T(8,128)(2,1)S(1)}, u32[]{:S(2)}, u32[]{:S(2)}) collective-permute-start(bf16[704,128]{1,0:T(8,128)(2,1)S(1)} %collective-permute-done.5.refs_0_.refs_6_.refs_8_), channel_id=1, source_target_pairs={{0,2},{2,0},{4,6},{6,4},{8,10},{10,8},{12,14},{14,12},{16,18},{18,... | collective-permute-start | bytes 540680 | tf_op jit(solution)/shard_map/ppermute | solution.py:363
  13.8 9.4 %collective-permute-start.4 = (bf16[704,128]{1,0:T(8,128)(2,1)S(1)}, bf16[704,128]{1,0:T(8,128)(2,1)S(1)}, u32[]{:S(2)}, u32[]{:S(2)}) collective-permute-start(bf16[704,128]{1,0:T(8,128)(2,1)S(1)} %get-tuple-element.24.refs_0_.refs_5_.refs_7_), channel_id=1, source_target_pairs={{0,2},{2,16},{4,6},{6,20},{8,10},{10,24},{12,14},{14,28},{16,18},{... | collective-permute-start | bytes 540680 | tf_op jit(solution)/shard_map/ppermute | solution.py:359
  14.5 19.0 %collective-permute-start = (bf16[64,32,128]{2,0,1:T(8,128)(2,1)S(1)}, bf16[64,32,128]{2,0,1:T(8,128)(2,1)S(1)}, u32[]{:S(2)}, u32[]{:S(2)}) collective-permute-start(bf16[64,32,128]{2,0,1:T(8,128)(2,1)S(1)} %copy.12), channel_id=1, source_target_pairs={{0,1},{1,0},{2,3},{3,2},{4,5},{5,4},{6,7},{7,6},{8,9},{9,8},{10,11... | collective-permute-start | bytes 1572872 | tf_op jit(solution)/shard_map/ppermute | solution.py:350
  19.0 6.7 %copy-start.3 = (f32[128,32]{0,1:T(8,128)S(1)}, f32[128,32]{0,1:T(8,128)}, u32[]{:S(2)}) copy-start(f32[128,32]{0,1:T(8,128)} %param.13) | copy-start | bytes 49156
  19.0 7.8 %collective-permute-start.14 = (bf16[704,128]{1,0:T(8,128)(2,1)S(1)}, bf16[704,128]{1,0:T(8,128)(2,1)S(1)}, u32[]{:S(2)}, u32[]{:S(2)}) collective-permute-start(bf16[704,128]{1,0:T(8,128)(2,1)S(1)} %collective-permute-done.5.refs_0_.refs_6_.refs_8_), channel_id=1, source_target_pairs={{0,8},{2,10},{4,12},{6,14},{8,16},{10,18},{12,20},{14,22},{16,24},... | collective-permute-start | bytes 540680 | tf_op jit(solution)/shard_map/ppermute | solution.py:362
  19.1 4.2 %collective-permute-start.3 = (bf16[704,128]{1,0:T(8,128)(2,1)S(1)}, bf16[704,128]{1,0:T(8,128)(2,1)S(1)}, u32[]{:S(2)}, u32[]{:S(2)}) collective-permute-start(bf16[704,128]{1,0:T(8,128)(2,1)S(1)} %collective-permute-done.2.refs_0_.refs_8_.refs_10_), channel_id=1, source_target_pairs={{0,2},{2,0},{4,6},{6,4},{8,10},{10,8},{12,14},{14,12},{16,18},{18,... | collective-permute-start | bytes 540680 | tf_op jit(solution)/shard_map/ppermute | solution.py:363
  23.2 10.3 %copy-start.5 = (f32[128]{0:T(128)S(1)}, f32[128]{0:T(128)}, u32[]{:S(2)}) copy-start(f32[128]{0:T(128)} %param.15) | copy-start | bytes 1540
  24.4 10.8 %collective-permute-start.7 = (f32[384,128]{1,0:T(8,128)S(1)}, f32[384,128]{1,0:T(8,128)S(1)}, u32[]{:S(2)}, u32[]{:S(2)}) collective-permute-start(f32[384,128]{1,0:T(8,128)S(1)} %get-tuple-element.28), channel_id=1, source_target_pairs={{0,1},{1,0},{2,3},{3,2},{4,5},{5,4},{6,7},{7,6},{8,9},{9,8},{10,11... | collective-permute-start | bytes 589832 | tf_op jit(solution)/shard_map/ppermute | solution.py:350
  25.7 7.9 %collective-permute-start.1 = (f32[32,128]{1,0:T(8,128)S(1)}, f32[32,128]{1,0:T(8,128)S(1)}, u32[]{:S(2)}, u32[]{:S(2)}) collective-permute-start(f32[32,128]{1,0:T(8,128)S(1)} %bitcast.25), channel_id=1, source_target_pairs={{0,1},{1,0},{2,3},{3,2},{4,5},{5,4},{6,7},{7,6},{8,9},{9,8},{10,11... | collective-permute-start | bytes 49160 | tf_op jit(solution)/shard_map/ppermute | solution.py:350
  26.7 11.5 %collective-permute-start.15 = (bf16[704,128]{1,0:T(8,128)(2,1)S(1)}, bf16[704,128]{1,0:T(8,128)(2,1)S(1)}, u32[]{:S(2)}, u32[]{:S(2)}) collective-permute-start(bf16[704,128]{1,0:T(8,128)(2,1)S(1)} %collective-permute-done.14.refs_0_.refs_5_.refs_7_), channel_id=1, source_target_pairs={{0,2},{2,0},{4,6},{6,4},{8,10},{10,8},{12,14},{14,12},{16,18},{18,... | collective-permute-start | bytes 540680 | tf_op jit(solution)/shard_map/ppermute | solution.py:363
  37.7 8.2 %collective-permute-start.9 = (f32[128,128]{1,0:T(8,128)S(1)}, f32[128,128]{1,0:T(8,128)S(1)}, u32[]{:S(2)}, u32[]{:S(2)}) collective-permute-start(f32[128,128]{1,0:T(8,128)S(1)} %get-tuple-element.32), channel_id=1, source_target_pairs={{0,2},{2,0},{4,6},{6,4},{8,10},{10,8},{12,14},{14,12},{16,18},{18,... | collective-permute-start | bytes 196616 | tf_op jit(solution)/shard_map/ppermute | solution.py:396
  37.8 8.2 %collective-permute-start.11 = (f32[128,128]{1,0:T(8,128)S(1)}, f32[128,128]{1,0:T(8,128)S(1)}, u32[]{:S(2)}, u32[]{:S(2)}) collective-permute-start(f32[128,128]{1,0:T(8,128)S(1)} %get-tuple-element.34), channel_id=1, source_target_pairs={{0,2},{2,0},{4,6},{6,4},{8,10},{10,8},{12,14},{14,12},{16,18},{18,... | collective-permute-start | bytes 196616 | tf_op jit(solution)/shard_map/ppermute | solution.py:396
  39.2 13.9 %collective-permute-start.16 = (f32[128,128]{1,0:T(8,128)S(1)}, f32[128,128]{1,0:T(8,128)S(1)}, u32[]{:S(2)}, u32[]{:S(2)}) collective-permute-start(f32[128,128]{1,0:T(8,128)S(1)} %get-tuple-element.36), channel_id=1, source_target_pairs={{0,1},{1,0},{2,3},{3,2},{4,5},{5,4},{6,7},{7,6},{8,9},{9,8},{10,11... | collective-permute-start | bytes 196616 | tf_op jit(solution)/shard_map/ppermute | solution.py:350
  40.7 14.7 %collective-permute-start.8 = (f32[128,128]{1,0:T(8,128)S(1)}, f32[128,128]{1,0:T(8,128)S(1)}, u32[]{:S(2)}, u32[]{:S(2)}) collective-permute-start(f32[128,128]{1,0:T(8,128)S(1)} %get-tuple-element.30), channel_id=1, source_target_pairs={{2,0},{16,2},{6,4},{20,6},{10,8},{24,10},{14,12},{28,14},{18,16},{... | collective-permute-start | bytes 196616 | tf_op jit(solution)/shard_map/ppermute | solution.py:394
  45.9 9.5 %collective-permute-start.10 = (f32[128,128]{1,0:T(8,128)S(1)}, f32[128,128]{1,0:T(8,128)S(1)}, u32[]{:S(2)}, u32[]{:S(2)}) collective-permute-start(f32[128,128]{1,0:T(8,128)S(1)} %add.28), channel_id=1, source_target_pairs={{0,28},{2,30},{4,0},{6,2},{8,4},{10,6},{12,8},{14,10},{16,12},{18,... | collective-permute-start | bytes 196616 | tf_op jit(solution)/shard_map/ppermute | solution.py:398
  46.0 9.5 %collective-permute-start.12 = (f32[128,128]{1,0:T(8,128)S(1)}, f32[128,128]{1,0:T(8,128)S(1)}, u32[]{:S(2)}, u32[]{:S(2)}) collective-permute-start(f32[128,128]{1,0:T(8,128)S(1)} %add.30), channel_id=1, source_target_pairs={{0,24},{2,26},{4,28},{6,30},{8,0},{10,2},{12,4},{14,6},{16,8},{18,... | collective-permute-start | bytes 196616 | tf_op jit(solution)/shard_map/ppermute | solution.py:398
  53.9 3.2 %collective-permute-start.17 = (f32[128,128]{1,0:T(8,128)S(1)}, f32[128,128]{1,0:T(8,128)S(1)}, u32[]{:S(2)}, u32[]{:S(2)}) collective-permute-start(f32[128,128]{1,0:T(8,128)S(1)} %get-tuple-element.38), channel_id=1, source_target_pairs={{0,2},{2,0},{4,6},{6,4},{8,10},{10,8},{12,14},{14,12},{16,18},{18,... | collective-permute-start | bytes 196616 | tf_op jit(solution)/shard_map/ppermute | solution.py:396
  55.5 8.3 %collective-permute-start.13 = (f32[128,128]{1,0:T(8,128)S(1)}, f32[128,128]{1,0:T(8,128)S(1)}, u32[]{:S(2)}, u32[]{:S(2)}) collective-permute-start(f32[128,128]{1,0:T(8,128)S(1)} %add_add_fusion.1), channel_id=1, source_target_pairs={{0,1},{1,0},{2,3},{3,2},{4,5},{5,4},{6,7},{7,6},{8,9},{9,8},{10,11... | collective-permute-start | bytes 196616 | tf_op jit(solution)/shard_map/ppermute | solution.py:350
  57.1 5.1 %collective-permute-start.18 = (bf16[128,128]{1,0:T(8,128)(2,1)S(1)}, bf16[128,128]{1,0:T(8,128)(2,1)S(1)}, u32[]{:S(2)}, u32[]{:S(2)}) collective-permute-start(bf16[128,128]{1,0:T(8,128)(2,1)S(1)} %add_convert_fusion), channel_id=1, source_target_pairs={{0,20},{1,21},{2,22},{3,23},{4,24},{5,25},{6,26},{7,27},{8,28},{9,... | collective-permute-start | bytes 98312 | tf_op jit(solution)/shard_map/ppermute | solution.py:406
  58.1 5.7 %collective-permute-start.19 = (bf16[128,128]{1,0:T(8,128)(2,1)S(1)}, bf16[128,128]{1,0:T(8,128)(2,1)S(1)}, u32[]{:S(2)}, u32[]{:S(2)}) collective-permute-start(bf16[128,128]{1,0:T(8,128)(2,1)S(1)} %add_convert_fusion), channel_id=1, source_target_pairs={{0,21},{1,20},{2,23},{3,22},{4,25},{5,24},{6,27},{7,26},{8,29},{9,... | collective-permute-start | bytes 98312 | tf_op jit(solution)/shard_map/ppermute | solution.py:406

commit v5 on v4

--- a/solution.py
+++ b/solution.py
@@ -64,12 +64,12 @@
     return slab - own, (slab <= own) & (live_ref[own, slab] == 1)
 
 
-def packed(ids, order_ref, live_ref):
+def packed(ids, facts_ref):
     count, slots = jnp.int32(0), []
     for i in ids:
-        later, alive = facts(i, order_ref, live_ref)
-        slots.append((count, later, alive))
-        count = count + alive.astype(jnp.int32)
+        alive = facts_ref[2 * i + 1]
+        slots.append((count, facts_ref[2 * i], alive == 1))
+        count = count + alive
     return slots, count
 
 
@@ -107,12 +107,12 @@
     return pl.CostEstimate(flops=flops, transcendentals=0, bytes_accessed=flops // 256)
 
 
-def score_kernel(ids, n_outs, pack, order_ref, live_ref, q_ref, lse_ref, *refs):
+def score_kernel(ids, n_outs, pack, facts_ref, q_ref, lse_ref, *refs):
     blocks, known = refs[: len(ids)], refs[len(ids) : -n_outs - 2]
     outs, (keys, mass) = refs[-n_outs - 2 : -2], refs[-2:]
     heads, latent, tokens = q_ref.shape
     rows = blocks[0].shape[1]
-    slots, count = packed(ids, order_ref, live_ref)
+    slots, count = packed(ids, facts_ref)
     for block, (place, _, alive) in zip(blocks, slots):
 
         @pl.when(alive)
@@ -147,7 +147,7 @@
         out[...] = side_by_side([value[:, n * share : (n + 1) * share] for value in values])
 
 
-def head_mass(tables, q, lse, ids, blocks, known=(), n_head=0):
+def head_mass(known_facts, q, lse, ids, blocks, known=(), n_head=0):
     heads, latent, tokens = q.shape
     n, rows = len(ids), blocks[0].shape[1]
     shapes = [jax.ShapeDtypeStruct((rows, tokens), jnp.float32)] * n
@@ -155,7 +155,7 @@
         shapes = [side_by_side_shape(n + len(known), rows, tokens // n_head)] * n_head
     return pl.pallas_call(
         functools.partial(score_kernel, ids, len(shapes), n_head > 0),
-        in_specs=[SMEM, SMEM] + [VMEM] * (2 + n + len(known)),
+        in_specs=[SMEM] + [VMEM] * (2 + n + len(known)),
         out_specs=[VMEM] * len(shapes),
         out_shape=shapes,
         scratch_shapes=[
@@ -165,7 +165,36 @@
         cost_estimate=cost(2 * tokens * heads * latent * n * rows),
         compiler_params=pltpu.CompilerParams(vmem_limit_bytes=LIMIT),
         name="score_mass",
-    )(*tables, q, lse, *blocks, *known)
+    )(known_facts, q, lse, *blocks, *known)
+
+
+def first_kernel(order_ref, live_ref, q_ref, lse_ref, block_ref, facts_ref, mass_ref, keys, mass):
+    for i in range(HOPS):
+        later, alive = facts(i, order_ref, live_ref)
+        facts_ref[2 * i] = later
+        facts_ref[2 * i + 1] = alive.astype(jnp.int32)
+    score_kernel((0,), 1, False, facts_ref, q_ref, lse_ref, block_ref, mass_ref, keys, mass)
+
+
+def first_mass(order, live, q, lse, block):
+    heads, latent, tokens = q.shape
+    rows = block.shape[1]
+    return pl.pallas_call(
+        first_kernel,
+        in_specs=[SMEM, SMEM] + [VMEM] * 3,
+        out_specs=[SMEM, VMEM],
+        out_shape=[
+            jax.ShapeDtypeStruct((2 * HOPS,), jnp.int32),
+            jax.ShapeDtypeStruct((rows, tokens), jnp.float32),
+        ],
+        scratch_shapes=[
+            pltpu.VMEM((rows, latent), jnp.bfloat16),
+            pltpu.VMEM((rows, tokens), jnp.float32),
+        ],
+        cost_estimate=cost(2 * tokens * heads * latent * rows),
+        compiler_params=pltpu.CompilerParams(vmem_limit_bytes=LIMIT),
+        name="first_mass",
+    )(order, live, q, lse, block)
 
 
 def lanes_of(part, share):
@@ -196,7 +225,7 @@
         row += step
 
 
-def logit_kernel(latent, ids, n_head, order_ref, live_ref, *refs):
+def logit_kernel(latent, ids, n_head, facts_ref, *refs):
     parts, w_refs, lse_ref = refs[:n_head], refs[n_head : 2 * n_head], refs[2 * n_head]
     blocks, (out_ref, w_ref, keys, values) = refs[2 * n_head + 1 : -4], refs[-4:]
     rows, idx_width = blocks[0].shape[1], keys.shape[1]
@@ -207,7 +236,7 @@
     lse = lse_ref[...]
     if share < lse.shape[1]:
         lse = pltpu.roll(lse, lse.shape[1] - lax.axis_index("head") * share, 1)[:, :share]
-    slots, count = packed(ids, order_ref, live_ref)
+    slots, count = packed(ids, facts_ref)
     for block, (place, _, alive) in zip(blocks, slots):
 
         @pl.when(alive)
@@ -234,13 +263,13 @@
     out_ref[...] = side_by_side([jnp.where(s[2], values[at(s[0], rows), :], 0.0) for s in slots])
 
 
-def index_logits(tables, parts, weights, lse, ids, blocks, latent):
+def index_logits(known_facts, parts, weights, lse, ids, blocks, latent):
     n_head, (index_here, share, idx_width) = len(parts), parts[0].shape
     rows = blocks[0].shape[1]
     side = lanes_of(parts[0], share)
     return pl.pallas_call(
         functools.partial(logit_kernel, latent, ids, n_head),
-        in_specs=[SMEM, SMEM] + [VMEM] * (2 * n_head + 1 + len(blocks)),
+        in_specs=[SMEM] + [VMEM] * (2 * n_head + 1 + len(blocks)),
         out_specs=VMEM,
         out_shape=side_by_side_shape(len(blocks), rows, share),
         scratch_shapes=[
@@ -251,10 +280,10 @@
         cost_estimate=cost(2 * len(blocks) * rows * share * n_head * index_here * idx_width),
         compiler_params=pltpu.CompilerParams(vmem_limit_bytes=LIMIT),
         name="index_logits",
-    )(*tables, *parts, *weights, lse, *blocks)
-
-
-def grad_kernel(latent, ids, n_head, order_ref, live_ref, *refs):
+    )(known_facts, *parts, *weights, lse, *blocks)
+
+
+def grad_kernel(latent, ids, n_head, facts_ref, *refs):
     parts, w_refs, masses = refs[:n_head], refs[n_head : 2 * n_head], refs[2 * n_head : 3 * n_head]
     target_ref, (w_ref, keys, grads, results) = refs[3 * n_head], refs[-4:]
     n_blocks = (len(refs) - 3 * n_head - 5) // 2
@@ -265,7 +294,7 @@
     lay_weights(parts, w_refs, w_ref)
     tile = w_ref.shape[1]
     start = lax.axis_index("head") * share
-    slots, count = packed(ids, order_ref, live_ref)
+    slots, count = packed(ids, facts_ref)
     for i, (place, later, alive) in enumerate(slots):
 
         @pl.when(alive)
@@ -306,13 +335,13 @@
         out[...] = jnp.where(alive, results[at(place, rows), :], 0.0)
 
 
-def index_grad(tables, parts, weights, masses, target, ids, blocks, latent):
+def index_grad(known_facts, parts, weights, masses, target, ids, blocks, latent):
     n_head, (index_here, share, idx_width) = len(parts), parts[0].shape
     rows = blocks[0].shape[1]
     side = lanes_of(parts[0], share)
     return pl.pallas_call(
         functools.partial(grad_kernel, latent, ids, n_head),
-        in_specs=[SMEM, SMEM] + [VMEM] * (3 * n_head + 1 + len(blocks)),
+        in_specs=[SMEM] + [VMEM] * (3 * n_head + 1 + len(blocks)),
         out_specs=[VMEM] * len(blocks),
         out_shape=[jax.ShapeDtypeStruct((rows, idx_width), jnp.float32)] * len(blocks),
         scratch_shapes=[
@@ -324,7 +353,7 @@
         cost_estimate=cost(4 * len(blocks) * rows * share * n_head * index_here * idx_width),
         compiler_params=pltpu.CompilerParams(vmem_limit_bytes=LIMIT),
         name="index_grad",
-    )(*tables, *parts, *weights, *masses, target, *blocks)
+    )(known_facts, *parts, *weights, *masses, target, *blocks)
 
 
 def body(
@@ -367,7 +396,6 @@
     parts = [around(shares[turn], turn) if turn else shares[turn] for turn in turns]
     parts = [part.transpose(1, 0, 2) for part in parts]
 
-    tables = slab_order, block_live
     q, lse, lse_share = q_main.transpose(1, 2, 0), lse_main.T, lse_index[None, :]
 
     def blocks(ids):
@@ -377,8 +405,9 @@
     runs[-1] += (1,)
     early = tuple(i for run in runs for i in run)
     late = (HOPS - 2, HOPS - 1)
-    known = []
-    for run in runs[:-1]:
+    tables, own_mass = first_mass(slab_order, block_live, q, lse, own)
+    known = [own_mass]
+    for run in runs[1:-1]:
         known += head_mass(tables, q, lse, run, blocks(run))
     group = head_mass(tables, q, lse, runs[-1], blocks(runs[-1]), known, n_head)
     masses = [list(group)]

time: 65.8 us -> 65.6 us (level)
    pallas_call x0 -> x1, Pallas kernels: none -> 3.31 us  [first_mass(): pl.pallas_call(first_kernel, in_specs=[SMEM, SMEM] + [VMEM] * 3, out_spec...]
    pallas_call x4 -> x3, Pallas kernels: 7.55 us -> 4.39 us  [head_mass(): pl.pallas_call(functools.partial(score_kernel, ids, len(shapes), n_head >...]
  transfers between devices with their start and end apart: 20 -> 20, of which waited for: 4 -> 4; matrix products, arithmetic and copies ran while one was open for 1% -> 1% of each run, Pallas kernels for 21% -> 20%
where the time goes in v5:
time: 65.6 us; the launch traced here: 64.4 us
  starting transfers between devices  28.9 us (44%)
  waiting for transfers between devices  18.8 us (29%)
  Pallas kernels  13.2 us (20%)
  local copies, waits for them, and re-layouts  1.66 us (3%)
  other arithmetic  1.64 us (2%)
    ppermute x5, starting transfers between devices, around(): lax.ppermute(array, 'head', [(i, (i + turn) % n_head) for i in range(n_he...  6.92 us
    ppermute x1, waiting for transfers between devices, body(): arrived = [lax.ppermute(own, 'seq', ring(2))]  6.86 us
    ppermute x2, starting transfers between devices, body(): total = total + lax.ppermute(both, 'seq', ring(-2 * m))  6.47 us
    ppermute x5, waiting for transfers between devices, around(): lax.ppermute(array, 'head', [(i, (i + turn) % n_head) for i in range(n_he...  6.43 us
    ppermute x2, waiting for transfers between devices, body(): last.append(lax.ppermute(both.astype(jnp.bfloat16), ('seq', 'head'), route))  5.5 us
    ppermute x1, starting transfers between devices, body(): total = grads[0] + lax.ppermute(grads[1], 'seq', back)  5.16 us
    pallas_call x3, Pallas kernels, head_mass(): pl.pallas_call(functools.partial(score_kernel, ids, len(shapes), n_head >...  4.39 us
    pallas_call x1, Pallas kernels, first_mass(): pl.pallas_call(first_kernel, in_specs=[SMEM, SMEM] + [VMEM] * 3, out_spec...  3.31 us
  transfers between devices with their start and end apart: 20, of which 4 were waited for; matrix products, arithmetic and copies ran while one was open for 1% of the time, Pallas kernels for 20%

profile of v5, /device:TPU:0, one launch (start us, length us, event | category | flops | bytes accessed | tf_op | source)
XLA Modules:
  0.0 64.4 jit_solution(17695149626115084392)
XLA Ops:
  0.0 0.9 %pad_maximum_fusion.block_ref = bf16[704,128]{1,0:T(8,128)(2,1)S(1)} fusion(bf16[128,128]{1,0:T(8,128)(2,1)} %param.14, bf16[576,128]{1,0:T(8,128)(2,1)} %bitcast.32), kind=kLoop, calls=%fused_computation.1 | loop fusion | flops 360448 | bytes 360448 | tf_op jit(solution)/shard_map/concatenate | solution.py:384
  0.9 0.0 copy-start.6
  1.0 1.2 %copy-done.6 = bf16[128,32,128]{2,1,0:T(8,128)(2,1)S(1)} copy-done((bf16[128,32,128]{2,1,0:T(8,128)(2,1)S(1)}, bf16[128,32,128]{2,1,0:T(8,128)(2,1)}, u32[]{:S(2)}) %copy-start.6) | copy-done | bytes 1048600
  2.2 0.0 copy-start
  2.2 0.0 copy-start.1
  2.2 0.1 cut_shares.1
  2.3 3.0 %collective-permute-start.5 = (bf16[704,128]{1,0:T(8,128)(2,1)S(1)}, bf16[704,128]{1,0:T(8,128)(2,1)S(1)}, u32[]{:S(2)}, u32[]{:S(2)}) collective-permute-start(bf16[704,128]{1,0:T(8,128)(2,1)S(1)} %get-tuple-element.24.block_ref.refs_5_.refs_7_), channel_id=1, source_target_pairs={{0,4},{2,6},{4,8},{6,10},{8,12},{10,14},{12,16},{14,18},{16,20},{1... | collective-permute-start | bytes 540680 | tf_op jit(solution)/shard_map/ppermute | solution.py:386
  5.3 1.6 %collective-permute-start.2 = (bf16[704,128]{1,0:T(8,128)(2,1)S(1)}, bf16[704,128]{1,0:T(8,128)(2,1)S(1)}, u32[]{:S(2)}, u32[]{:S(2)}) collective-permute-start(bf16[704,128]{1,0:T(8,128)(2,1)S(1)} %get-tuple-element.24.block_ref.refs_5_.refs_7_), channel_id=1, source_target_pairs={{0,8},{2,10},{4,12},{6,14},{8,16},{10,18},{12,20},{14,22},{16,24},... | collective-permute-start | bytes 540680 | tf_op jit(solution)/shard_map/ppermute | solution.py:387
  6.9 6.9 %collective-permute-done.5.refs_0_.refs_6_.refs_8_ = bf16[704,128]{1,0:T(8,128)(2,1)S(1)} collective-permute-done((bf16[704,128]{1,0:T(8,128)(2,1)S(1)}, bf16[704,128]{1,0:T(8,128)(2,1)S(1)}, u32[]{:S(2)}, u32[]{:S(2)}) %collective-permute-start.5) | collective-permute-done | bytes 180256 | tf_op jit(solution)/shard_map/ppermute | solution.py:386
  13.8 0.0 collective-permute-start.6
  13.8 0.5 collective-permute-start.4
  14.3 0.2 copy.12
  14.5 1.7 %collective-permute-start = (bf16[64,32,128]{2,0,1:T(8,128)(2,1)S(1)}, bf16[64,32,128]{2,0,1:T(8,128)(2,1)S(1)}, u32[]{:S(2)}, u32[]{:S(2)}) collective-permute-start(bf16[64,32,128]{2,0,1:T(8,128)(2,1)S(1)} %copy.12), channel_id=1, source_target_pairs={{0,1},{1,0},{2,3},{3,2},{4,5},{5,4},{6,7},{7,6},{8,9},{9,8},{10,11... | collective-permute-start | bytes 1572872 | tf_op jit(solution)/shard_map/ppermute | solution.py:379
  16.2 0.0 copy-done
  16.2 0.0 copy-done.1
  16.2 0.0 copy-done.3
  16.2 0.0 copy-done.5
  16.2 3.3 %first_mass.1 = (s32[16]{0:T(128)S(1)}, f32[128,128]{1,0:T(8,128)S(1)}) custom-call(s32[16]{0:T(128)S(1)} %copy-done.5, s32[16,16]{1,0:T(8,128)S(1)} %copy-done.3, bf16[64,576,128]{2,1,0:T(8,128)(2,1)S(1)} %bitcast.9, f32[64,128]{1,0:T(8,128)S(1)} %bitcast.21, bf16[704,128]{1,0:T(8,128)(2,1)S(1)} %get-tuple-element.24.block_ref.refs_5_.refs_7_), custom_call_target="tpu_custom_call" | custom-call | flops 1207959552 | bytes 4718592 | tf_op jit(solution)/shard_map/first_mass/pallas_call | solution.py:182
  19.6 0.1 collective-permute-start.14
  19.6 0.0 collective-permute-done.2.refs_0_.refs_8_.refs_10_
  19.6 1.4 %collective-permute-start.3 = (bf16[704,128]{1,0:T(8,128)(2,1)S(1)}, bf16[704,128]{1,0:T(8,128)(2,1)S(1)}, u32[]{:S(2)}, u32[]{:S(2)}) collective-permute-start(bf16[704,128]{1,0:T(8,128)(2,1)S(1)} %collective-permute-done.2.refs_0_.refs_8_.refs_10_), channel_id=1, source_target_pairs={{0,2},{2,0},{4,6},{6,4},{8,10},{10,8},{12,14},{14,12},{16,18},{18,... | collective-permute-start | bytes 540680 | tf_op jit(solution)/shard_map/ppermute | solution.py:392
  21.0 0.0 collective-permute-done.6.refs_1_.refs_7_.refs_9_
  21.0 2.6 %score_mass.3 = (f32[128,128]{1,0:T(8,128)S(1)}, f32[128,128]{1,0:T(8,128)S(1)}) custom-call(s32[16]{0:T(128)S(1)} %get-tuple-element.25.facts_ref, bf16[64,576,128]{2,1,0:T(8,128)(2,1)S(1)} %bitcast.10, f32[64,128]{1,0:T(8,128)S(1)} %bitcast.22, bf16[704,128]{1,0:T(8,128)(2,1)S(1)} %collective-permute-done.5.refs_0_.refs_6_.refs_8_, ...), custom_call_target="tpu_custom_call" | custom-call | flops 2415919104 | bytes 9437184 | tf_op jit(solution)/shard_map/score_mass/pallas_call | solution.py:156
  23.6 0.0 copy-start.4
  23.6 0.0 collective-permute-done.4.refs_2_.refs_10_.refs_12_
  23.6 0.0 collective-permute-done.3.refs_1_.refs_9_.refs_11_
  23.7 1.0 %score_mass.4 = (f32[384,128]{1,0:T(8,128)S(1)}, f32[384,128]{1,0:T(8,128)S(1)}) custom-call(s32[16]{0:T(128)S(1)} %get-tuple-element.25.facts_ref, bf16[64,576,128]{2,1,0:T(8,128)(2,1)S(1)} %bitcast.11, f32[64,128]{1,0:T(8,128)S(1)} %bitcast.23, bf16[704,128]{1,0:T(8,128)(2,1)S(1)} %collective-permute-done.2.refs_0_.refs_8_.refs_10_, ...), custom_call_target="tpu_custom_call" | custom-call | flops 3623878656 | bytes 14155776 | tf_op jit(solution)/shard_map/score_mass/pallas_call | solution.py:156
  24.7 0.6 collective-permute-start.7
  25.3 0.0 copy-done.2
  25.3 1.5 %collective-permute-start.1 = (f32[32,128]{1,0:T(8,128)S(1)}, f32[32,128]{1,0:T(8,128)S(1)}, u32[]{:S(2)}, u32[]{:S(2)}) collective-permute-start(f32[32,128]{1,0:T(8,128)S(1)} %bitcast.25), channel_id=1, source_target_pairs={{0,1},{1,0},{2,3},{3,2},{4,5},{5,4},{6,7},{7,6},{8,9},{9,8},{10,11... | collective-permute-start | bytes 49160 | tf_op jit(solution)/shard_map/ppermute | solution.py:379
  26.8 0.2 copy.14
  27.0 0.0 collective-permute-done.14.refs_0_.refs_5_.refs_7_
  27.0 0.1 collective-permute-start.15
  27.1 6.4 %collective-permute-done.1.refs_3_ = f32[32,128]{1,0:T(8,128)S(1)} collective-permute-done((f32[32,128]{1,0:T(8,128)S(1)}, f32[32,128]{1,0:T(8,128)S(1)}, u32[]{:S(2)}, u32[]{:S(2)}) %collective-permute-start.1) | collective-permute-done | bytes 16416 | tf_op jit(solution)/shard_map/ppermute | solution.py:379
  33.5 0.0 collective-permute-done
  33.5 0.0 copy-done.4
  33.5 1.6 %index_logits.2.refs_6_ = f32[384,128]{1,0:T(8,128)S(1)} custom-call(s32[16]{0:T(128)S(1)} %get-tuple-element.25.facts_ref, bf16[32,64,128]{2,1,0:T(8,128)(2,1)S(1)} %bitcast.13, bf16[32,64,128]{2,1,0:T(8,128)(2,1)S(1)} %bitcast.17, f32[32,128]{1,0:T(8,128)S(1)} %bitcast.26, f32[32,128]{1,0:T(8,128)S(1)} %collective-permute-done.1.refs_3_, ...), custom_call_target="tpu_custom_call" | custom-call | flops 805306368 | bytes 3145728 | tf_op jit(solution)/shard_map/index_logits/pallas_call | solution.py:270
  35.1 0.0 collective-permute-done.7.refs_5_
  35.2 2.3 %index_grad.2 = (f32[128,128]{1,0:T(8,128)S(1)}, f32[128,128]{1,0:T(8,128)S(1)}, f32[128,128]{1,0:T(8,128)S(1)}, f32[128,128]{1,0:T(8,128)S(1)}, f32[128,128]{1,0:T(8,128)S(1)}, /*index=5*/f32[128,128]{1,0:T(8,128)S(1)}) custom-call(s32[16]{0:T(128)S(1)} %get-tuple-element.25.facts_ref, bf16[32,64,128]{2,1,0:T(8,128)(2,1)S(1)} %bitcast.14, ...), custom_call_target="tpu_custom_call" | custom-call | flops 1610612736 | bytes 6291456 | tf_op jit(solution)/shard_map/index_grad/pallas_call | solution.py:342
  37.5 0.1 collective-permute-start.9
  37.5 0.5 collective-permute-start.11
  38.0 0.0 collective-permute-done.15.refs_1_.refs_6_.refs_8_
  38.0 0.8 %score_mass.5 = (f32[128,128]{1,0:T(8,128)S(1)}, f32[128,128]{1,0:T(8,128)S(1)}) custom-call(s32[16]{0:T(128)S(1)} %get-tuple-element.25.facts_ref, bf16[64,576,128]{2,1,0:T(8,128)(2,1)S(1)} %bitcast.12, f32[64,128]{1,0:T(8,128)S(1)} %bitcast.24, bf16[704,128]{1,0:T(8,128)(2,1)S(1)} %collective-permute-done.14.refs_0_.refs_5_.refs_7_, ...), custom_call_target="tpu_custom_call" | custom-call | flops 2415919104 | bytes 9437184 | tf_op jit(solution)/shard_map/score_mass/pallas_call | solution.py:156
  38.8 1.6 %collective-permute-start.16 = (f32[128,128]{1,0:T(8,128)S(1)}, f32[128,128]{1,0:T(8,128)S(1)}, u32[]{:S(2)}, u32[]{:S(2)}) collective-permute-start(f32[128,128]{1,0:T(8,128)S(1)} %get-tuple-element.40), channel_id=1, source_target_pairs={{0,1},{1,0},{2,3},{3,2},{4,5},{5,4},{6,7},{7,6},{8,9},{9,8},{10,11... | collective-permute-start | bytes 196616 | tf_op jit(solution)/shard_map/ppermute | solution.py:379
  40.3 5.2 %collective-permute-start.8 = (f32[128,128]{1,0:T(8,128)S(1)}, f32[128,128]{1,0:T(8,128)S(1)}, u32[]{:S(2)}, u32[]{:S(2)}) collective-permute-start(f32[128,128]{1,0:T(8,128)S(1)} %get-tuple-element.34), channel_id=1, source_target_pairs={{2,0},{16,2},{6,4},{20,6},{10,8},{24,10},{14,12},{28,14},{18,16},{... | collective-permute-start | bytes 196616 | tf_op jit(solution)/shard_map/ppermute | solution.py:423
  45.5 0.0 collective-permute-done.9
  45.5 0.1 collective-permute-start.10
  45.6 0.0 collective-permute-done.11
  45.6 6.4 %collective-permute-start.12 = (f32[128,128]{1,0:T(8,128)S(1)}, f32[128,128]{1,0:T(8,128)S(1)}, u32[]{:S(2)}, u32[]{:S(2)}) collective-permute-start(f32[128,128]{1,0:T(8,128)S(1)} %add.30), channel_id=1, source_target_pairs={{0,24},{2,26},{4,28},{6,30},{8,0},{10,2},{12,4},{14,6},{16,8},{18,... | collective-permute-start | bytes 196616 | tf_op jit(solution)/shard_map/ppermute | solution.py:427
  52.0 0.8 %index_logits.3.refs_6_ = f32[128,128]{1,0:T(8,128)S(1)} custom-call(s32[16]{0:T(128)S(1)} %get-tuple-element.25.facts_ref, bf16[32,64,128]{2,1,0:T(8,128)(2,1)S(1)} %bitcast.15, bf16[32,64,128]{2,1,0:T(8,128)(2,1)S(1)} %bitcast.19, f32[32,128]{1,0:T(8,128)S(1)} %bitcast.28, f32[32,128]{1,0:T(8,128)S(1)} %collective-permute-done.1.refs_3_, ...), custom_call_target="tpu_custom_call" | custom-call | flops 268435456 | bytes 1048576 | tf_op jit(solution)/shard_map/index_logits/pallas_call | solution.py:270
  52.8 0.0 collective-permute-done.16.refs_5_
  52.8 0.7 %index_grad.3 = (f32[128,128]{1,0:T(8,128)S(1)}, f32[128,128]{1,0:T(8,128)S(1)}) custom-call(s32[16]{0:T(128)S(1)} %get-tuple-element.25.facts_ref, bf16[32,64,128]{2,1,0:T(8,128)(2,1)S(1)} %bitcast.16, bf16[32,64,128]{2,1,0:T(8,128)(2,1)S(1)} %bitcast.20, f32[32,128]{1,0:T(8,128)S(1)} %bitcast.29, f32[32,128]{1,0:T(8,128)S(1)} %collective-permute-done.1.refs_3_, ...), custom_call_target="tpu_custom_call" | custom-call | flops 536870912 | bytes 2097152 | tf_op jit(solution)/shard_map/index_grad/pallas_call | solution.py:342
  53.5 1.6 %collective-permute-start.17 = (f32[128,128]{1,0:T(8,128)S(1)}, f32[128,128]{1,0:T(8,128)S(1)}, u32[]{:S(2)}, u32[]{:S(2)}) collective-permute-start(f32[128,128]{1,0:T(8,128)S(1)} %get-tuple-element.42), channel_id=1, source_target_pairs={{0,2},{2,0},{4,6},{6,4},{8,10},{10,8},{12,14},{14,12},{16,18},{18,... | collective-permute-start | bytes 196616 | tf_op jit(solution)/shard_map/ppermute | solution.py:425
  55.1 0.0 collective-permute-done.8
  55.1 0.0 collective-permute-done.10
  55.1 0.0 collective-permute-done.12
  55.1 1.6 %collective-permute-start.13 = (f32[128,128]{1,0:T(8,128)S(1)}, f32[128,128]{1,0:T(8,128)S(1)}, u32[]{:S(2)}, u32[]{:S(2)}) collective-permute-start(f32[128,128]{1,0:T(8,128)S(1)} %add_add_fusion.1), channel_id=1, source_target_pairs={{0,1},{1,0},{2,3},{3,2},{4,5},{5,4},{6,7},{7,6},{8,9},{9,8},{10,11... | collective-permute-start | bytes 196616 | tf_op jit(solution)/shard_map/ppermute | solution.py:379
  56.7 0.0 collective-permute-done.17
  56.7 1.3 %collective-permute-start.18 = (bf16[128,128]{1,0:T(8,128)(2,1)S(1)}, bf16[128,128]{1,0:T(8,128)(2,1)S(1)}, u32[]{:S(2)}, u32[]{:S(2)}) collective-permute-start(bf16[128,128]{1,0:T(8,128)(2,1)S(1)} %add_convert_fusion), channel_id=1, source_target_pairs={{0,20},{1,21},{2,22},{3,23},{4,24},{5,25},{6,26},{7,27},{8,28},{9,... | collective-permute-start | bytes 98312 | tf_op jit(solution)/shard_map/ppermute | solution.py:435
  58.0 0.2 collective-permute-start.19
  58.2 3.6 %collective-permute-done.18 = bf16[128,128]{1,0:T(8,128)(2,1)S(1)} collective-permute-done((bf16[128,128]{1,0:T(8,128)(2,1)S(1)}, bf16[128,128]{1,0:T(8,128)(2,1)S(1)}, u32[]{:S(2)}, u32[]{:S(2)}) %collective-permute-start.18) | collective-permute-done | bytes 32800 | tf_op jit(solution)/shard_map/ppermute | solution.py:435
  61.9 1.9 %collective-permute-done.19 = bf16[128,128]{1,0:T(8,128)(2,1)S(1)} collective-permute-done((bf16[128,128]{1,0:T(8,128)(2,1)S(1)}, bf16[128,128]{1,0:T(8,128)(2,1)S(1)}, u32[]{:S(2)}, u32[]{:S(2)}) %collective-permute-start.19) | collective-permute-done | bytes 32800 | tf_op jit(solution)/shard_map/ppermute | solution.py:435
  63.7 0.0 collective-permute-done.13
  63.7 0.6 %add_add_fusion = f32[128,128]{1,0:T(8,128)} fusion(bf16[128,128]{1,0:T(8,128)(2,1)S(1)} %collective-permute-done.19, bf16[128,128]{1,0:T(8,128)(2,1)S(1)} %collective-permute-done.18, f32[128,128]{1,0:T(8,128)S(1)} %add_add_fusion.1, f32[128,128]{1,0:T(8,128)S(1)} %collective-permute-done.13), kind=kLoop, calls=%fused_computation.2 | loop fusion | flops 81920 | bytes 262144 | tf_op jit(solution)/shard_map/add | solution.py:437
  (7 shorter events, 0.1 us)
Async XLA Ops:
  0.9 1.2 %copy-start.6 = (bf16[128,32,128]{2,1,0:T(8,128)(2,1)S(1)}, bf16[128,32,128]{2,1,0:T(8,128)(2,1)}, u32[]{:S(2)}) copy-start(bf16[128,32,128]{2,1,0:T(8,128)(2,1)} %queries_ref.1) | copy-start | bytes 3145732
  2.2 14.0 %copy-start = (bf16[128,64,576]{0,2,1:T(8,128)(2,1)S(1)}, bf16[128,64,576]{0,2,1:T(8,128)(2,1)}, u32[]{:S(2)}) copy-start(bf16[128,64,576]{0,2,1:T(8,128)(2,1)} %param.9) | copy-start | bytes 28311556
  2.2 14.0 %copy-start.1 = (f32[128,64]{0,1:T(8,128)S(1)}, f32[128,64]{0,1:T(8,128)}, u32[]{:S(2)}) copy-start(f32[128,64]{0,1:T(8,128)} %param.11) | copy-start | bytes 98308
  2.2 14.1 %copy-start.3 = (s32[16,16]{1,0:T(8,128)S(1)}, s32[16,16]{1,0:T(8,128)}, u32[]{:S(2)}) copy-start(s32[16,16]{1,0:T(8,128)} %live_ref.1) | copy-start | bytes 3076
  2.2 14.1 %copy-start.5 = (s32[16]{0:T(128)S(1)}, s32[16]{0:T(128)}, u32[]{:S(2)}) copy-start(s32[16]{0:T(128)} %order_ref.1) | copy-start | bytes 196
  2.3 11.5 %collective-permute-start.5 = (bf16[704,128]{1,0:T(8,128)(2,1)S(1)}, bf16[704,128]{1,0:T(8,128)(2,1)S(1)}, u32[]{:S(2)}, u32[]{:S(2)}) collective-permute-start(bf16[704,128]{1,0:T(8,128)(2,1)S(1)} %get-tuple-element.24.block_ref.refs_5_.refs_7_), channel_id=1, source_target_pairs={{0,4},{2,6},{4,8},{6,10},{8,12},{10,14},{12,16},{14,18},{16,20},{1... | collective-permute-start | bytes 540680 | tf_op jit(solution)/shard_map/ppermute | solution.py:386
  5.3 14.3 %collective-permute-start.2 = (bf16[704,128]{1,0:T(8,128)(2,1)S(1)}, bf16[704,128]{1,0:T(8,128)(2,1)S(1)}, u32[]{:S(2)}, u32[]{:S(2)}) collective-permute-start(bf16[704,128]{1,0:T(8,128)(2,1)S(1)} %get-tuple-element.24.block_ref.refs_5_.refs_7_), channel_id=1, source_target_pairs={{0,8},{2,10},{4,12},{6,14},{8,16},{10,18},{12,20},{14,22},{16,24},... | collective-permute-start | bytes 540680 | tf_op jit(solution)/shard_map/ppermute | solution.py:387
  13.8 7.2 %collective-permute-start.6 = (bf16[704,128]{1,0:T(8,128)(2,1)S(1)}, bf16[704,128]{1,0:T(8,128)(2,1)S(1)}, u32[]{:S(2)}, u32[]{:S(2)}) collective-permute-start(bf16[704,128]{1,0:T(8,128)(2,1)S(1)} %collective-permute-done.5.refs_0_.refs_6_.refs_8_), channel_id=1, source_target_pairs={{0,2},{2,0},{4,6},{6,4},{8,10},{10,8},{12,14},{14,12},{16,18},{18,... | collective-permute-start | bytes 540680 | tf_op jit(solution)/shard_map/ppermute | solution.py:392
  13.8 9.8 %collective-permute-start.4 = (bf16[704,128]{1,0:T(8,128)(2,1)S(1)}, bf16[704,128]{1,0:T(8,128)(2,1)S(1)}, u32[]{:S(2)}, u32[]{:S(2)}) collective-permute-start(bf16[704,128]{1,0:T(8,128)(2,1)S(1)} %get-tuple-element.24.block_ref.refs_5_.refs_7_), channel_id=1, source_target_pairs={{0,2},{2,16},{4,6},{6,20},{8,10},{10,24},{12,14},{14,28},{16,18},{... | collective-permute-start | bytes 540680 | tf_op jit(solution)/shard_map/ppermute | solution.py:388
  14.5 19.0 %collective-permute-start = (bf16[64,32,128]{2,0,1:T(8,128)(2,1)S(1)}, bf16[64,32,128]{2,0,1:T(8,128)(2,1)S(1)}, u32[]{:S(2)}, u32[]{:S(2)}) collective-permute-start(bf16[64,32,128]{2,0,1:T(8,128)(2,1)S(1)} %copy.12), channel_id=1, source_target_pairs={{0,1},{1,0},{2,3},{3,2},{4,5},{5,4},{6,7},{7,6},{8,9},{9,8},{10,11... | collective-permute-start | bytes 1572872 | tf_op jit(solution)/shard_map/ppermute | solution.py:379
  19.6 7.5 %collective-permute-start.14 = (bf16[704,128]{1,0:T(8,128)(2,1)S(1)}, bf16[704,128]{1,0:T(8,128)(2,1)S(1)}, u32[]{:S(2)}, u32[]{:S(2)}) collective-permute-start(bf16[704,128]{1,0:T(8,128)(2,1)S(1)} %collective-permute-done.5.refs_0_.refs_6_.refs_8_), channel_id=1, source_target_pairs={{0,8},{2,10},{4,12},{6,14},{8,16},{10,18},{12,20},{14,22},{16,24},... | collective-permute-start | bytes 540680 | tf_op jit(solution)/shard_map/ppermute | solution.py:391
  19.6 4.0 %collective-permute-start.3 = (bf16[704,128]{1,0:T(8,128)(2,1)S(1)}, bf16[704,128]{1,0:T(8,128)(2,1)S(1)}, u32[]{:S(2)}, u32[]{:S(2)}) collective-permute-start(bf16[704,128]{1,0:T(8,128)(2,1)S(1)} %collective-permute-done.2.refs_0_.refs_8_.refs_10_), channel_id=1, source_target_pairs={{0,2},{2,0},{4,6},{6,4},{8,10},{10,8},{12,14},{14,12},{16,18},{18,... | collective-permute-start | bytes 540680 | tf_op jit(solution)/shard_map/ppermute | solution.py:392
  21.0 4.3 %copy-start.2 = (f32[128,32]{0,1:T(8,128)S(1)}, f32[128,32]{0,1:T(8,128)}, u32[]{:S(2)}) copy-start(f32[128,32]{0,1:T(8,128)} %param.13) | copy-start | bytes 49156
  23.6 9.9 %copy-start.4 = (f32[128]{0:T(128)S(1)}, f32[128]{0:T(128)}, u32[]{:S(2)}) copy-start(f32[128]{0:T(128)} %param.15) | copy-start | bytes 1540
  24.7 10.4 %collective-permute-start.7 = (f32[384,128]{1,0:T(8,128)S(1)}, f32[384,128]{1,0:T(8,128)S(1)}, u32[]{:S(2)}, u32[]{:S(2)}) collective-permute-start(f32[384,128]{1,0:T(8,128)S(1)} %get-tuple-element.32), channel_id=1, source_target_pairs={{0,1},{1,0},{2,3},{3,2},{4,5},{5,4},{6,7},{7,6},{8,9},{9,8},{10,11... | collective-permute-start | bytes 589832 | tf_op jit(solution)/shard_map/ppermute | solution.py:379
  25.3 8.2 %collective-permute-start.1 = (f32[32,128]{1,0:T(8,128)S(1)}, f32[32,128]{1,0:T(8,128)S(1)}, u32[]{:S(2)}, u32[]{:S(2)}) collective-permute-start(f32[32,128]{1,0:T(8,128)S(1)} %bitcast.25), channel_id=1, source_target_pairs={{0,1},{1,0},{2,3},{3,2},{4,5},{5,4},{6,7},{7,6},{8,9},{9,8},{10,11... | collective-permute-start | bytes 49160 | tf_op jit(solution)/shard_map/ppermute | solution.py:379
  27.0 11.0 %collective-permute-start.15 = (bf16[704,128]{1,0:T(8,128)(2,1)S(1)}, bf16[704,128]{1,0:T(8,128)(2,1)S(1)}, u32[]{:S(2)}, u32[]{:S(2)}) collective-permute-start(bf16[704,128]{1,0:T(8,128)(2,1)S(1)} %collective-permute-done.14.refs_0_.refs_5_.refs_7_), channel_id=1, source_target_pairs={{0,2},{2,0},{4,6},{6,4},{8,10},{10,8},{12,14},{14,12},{16,18},{18,... | collective-permute-start | bytes 540680 | tf_op jit(solution)/shard_map/ppermute | solution.py:392
  37.5 8.1 %collective-permute-start.9 = (f32[128,128]{1,0:T(8,128)S(1)}, f32[128,128]{1,0:T(8,128)S(1)}, u32[]{:S(2)}, u32[]{:S(2)}) collective-permute-start(f32[128,128]{1,0:T(8,128)S(1)} %get-tuple-element.36), channel_id=1, source_target_pairs={{0,2},{2,0},{4,6},{6,4},{8,10},{10,8},{12,14},{14,12},{16,18},{18,... | collective-permute-start | bytes 196616 | tf_op jit(solution)/shard_map/ppermute | solution.py:425
  37.5 8.1 %collective-permute-start.11 = (f32[128,128]{1,0:T(8,128)S(1)}, f32[128,128]{1,0:T(8,128)S(1)}, u32[]{:S(2)}, u32[]{:S(2)}) collective-permute-start(f32[128,128]{1,0:T(8,128)S(1)} %get-tuple-element.38), channel_id=1, source_target_pairs={{0,2},{2,0},{4,6},{6,4},{8,10},{10,8},{12,14},{14,12},{16,18},{18,... | collective-permute-start | bytes 196616 | tf_op jit(solution)/shard_map/ppermute | solution.py:425
  38.8 14.0 %collective-permute-start.16 = (f32[128,128]{1,0:T(8,128)S(1)}, f32[128,128]{1,0:T(8,128)S(1)}, u32[]{:S(2)}, u32[]{:S(2)}) collective-permute-start(f32[128,128]{1,0:T(8,128)S(1)} %get-tuple-element.40), channel_id=1, source_target_pairs={{0,1},{1,0},{2,3},{3,2},{4,5},{5,4},{6,7},{7,6},{8,9},{9,8},{10,11... | collective-permute-start | bytes 196616 | tf_op jit(solution)/shard_map/ppermute | solution.py:379
  40.3 14.8 %collective-permute-start.8 = (f32[128,128]{1,0:T(8,128)S(1)}, f32[128,128]{1,0:T(8,128)S(1)}, u32[]{:S(2)}, u32[]{:S(2)}) collective-permute-start(f32[128,128]{1,0:T(8,128)S(1)} %get-tuple-element.34), channel_id=1, source_target_pairs={{2,0},{16,2},{6,4},{20,6},{10,8},{24,10},{14,12},{28,14},{18,16},{... | collective-permute-start | bytes 196616 | tf_op jit(solution)/shard_map/ppermute | solution.py:423
  45.5 9.6 %collective-permute-start.10 = (f32[128,128]{1,0:T(8,128)S(1)}, f32[128,128]{1,0:T(8,128)S(1)}, u32[]{:S(2)}, u32[]{:S(2)}) collective-permute-start(f32[128,128]{1,0:T(8,128)S(1)} %add.28), channel_id=1, source_target_pairs={{0,28},{2,30},{4,0},{6,2},{8,4},{10,6},{12,8},{14,10},{16,12},{18,... | collective-permute-start | bytes 196616 | tf_op jit(solution)/shard_map/ppermute | solution.py:427
  45.6 9.5 %collective-permute-start.12 = (f32[128,128]{1,0:T(8,128)S(1)}, f32[128,128]{1,0:T(8,128)S(1)}, u32[]{:S(2)}, u32[]{:S(2)}) collective-permute-start(f32[128,128]{1,0:T(8,128)S(1)} %add.30), channel_id=1, source_target_pairs={{0,24},{2,26},{4,28},{6,30},{8,0},{10,2},{12,4},{14,6},{16,8},{18,... | collective-permute-start | bytes 196616 | tf_op jit(solution)/shard_map/ppermute | solution.py:427
  53.5 3.2 %collective-permute-start.17 = (f32[128,128]{1,0:T(8,128)S(1)}, f32[128,128]{1,0:T(8,128)S(1)}, u32[]{:S(2)}, u32[]{:S(2)}) collective-permute-start(f32[128,128]{1,0:T(8,128)S(1)} %get-tuple-element.42), channel_id=1, source_target_pairs={{0,2},{2,0},{4,6},{6,4},{8,10},{10,8},{12,14},{14,12},{16,18},{18,... | collective-permute-start | bytes 196616 | tf_op jit(solution)/shard_map/ppermute | solution.py:425
  55.1 8.6 %collective-permute-start.13 = (f32[128,128]{1,0:T(8,128)S(1)}, f32[128,128]{1,0:T(8,128)S(1)}, u32[]{:S(2)}, u32[]{:S(2)}) collective-permute-start(f32[128,128]{1,0:T(8,128)S(1)} %add_add_fusion.1), channel_id=1, source_target_pairs={{0,1},{1,0},{2,3},{3,2},{4,5},{5,4},{6,7},{7,6},{8,9},{9,8},{10,11... | collective-permute-start | bytes 196616 | tf_op jit(solution)/shard_map/ppermute | solution.py:379
  56.7 5.2 %collective-permute-start.18 = (bf16[128,128]{1,0:T(8,128)(2,1)S(1)}, bf16[128,128]{1,0:T(8,128)(2,1)S(1)}, u32[]{:S(2)}, u32[]{:S(2)}) collective-permute-start(bf16[128,128]{1,0:T(8,128)(2,1)S(1)} %add_convert_fusion), channel_id=1, source_target_pairs={{0,20},{1,21},{2,22},{3,23},{4,24},{5,25},{6,26},{7,27},{8,28},{9,... | collective-permute-start | bytes 98312 | tf_op jit(solution)/shard_map/ppermute | solution.py:435
  58.0 5.7 %collective-permute-start.19 = (bf16[128,128]{1,0:T(8,128)(2,1)S(1)}, bf16[128,128]{1,0:T(8,128)(2,1)S(1)}, u32[]{:S(2)}, u32[]{:S(2)}) collective-permute-start(bf16[128,128]{1,0:T(8,128)(2,1)S(1)} %add_convert_fusion), channel_id=1, source_target_pairs={{0,21},{1,20},{2,23},{3,22},{4,25},{5,24},{6,27},{7,26},{8,29},{9,... | collective-permute-start | bytes 98312 | tf_op jit(solution)/shard_map/ppermute | solution.py:435

commit v6 on v5

--- a/solution.py
+++ b/solution.py
@@ -227,7 +227,7 @@
 
 def logit_kernel(latent, ids, n_head, facts_ref, *refs):
     parts, w_refs, lse_ref = refs[:n_head], refs[n_head : 2 * n_head], refs[2 * n_head]
-    blocks, (out_ref, w_ref, keys, values) = refs[2 * n_head + 1 : -4], refs[-4:]
+    blocks, (out_ref, relu_ref, w_ref, keys, values) = refs[2 * n_head + 1 : -5], refs[-5:]
     rows, idx_width = blocks[0].shape[1], keys.shape[1]
     share = parts[0].shape[1]
     scale = 1.0 / idx_width**0.5
@@ -250,6 +250,7 @@
         for part in parts:
             for run, piece in pieces(part, share, 8):
                 r = lax.dot_general(held, piece, NT, preferred_element_type=jnp.float32)
+                relu_ref[here, row * tile : (row + run) * tile] = r.astype(jnp.bfloat16)
                 for k in range(run):
                     relu = jnp.maximum(r[:, k * tile : (k + 1) * tile], 0.0)
                     acc = acc + relu * w_ref[row + k : row + k + 1, :]
@@ -270,8 +271,11 @@
     return pl.pallas_call(
         functools.partial(logit_kernel, latent, ids, n_head),
         in_specs=[SMEM] + [VMEM] * (2 * n_head + 1 + len(blocks)),
-        out_specs=VMEM,
-        out_shape=side_by_side_shape(len(blocks), rows, share),
+        out_specs=[VMEM, VMEM],
+        out_shape=[
+            side_by_side_shape(len(blocks), rows, share),
+            jax.ShapeDtypeStruct((len(blocks) * rows, n_head * index_here * share), jnp.bfloat16),
+        ],
         scratch_shapes=[
             pltpu.VMEM((n_head * index_here // side, side * share), jnp.float32),
             pltpu.VMEM((len(blocks) * rows, idx_width), jnp.bfloat16),
@@ -283,12 +287,11 @@
     )(known_facts, *parts, *weights, lse, *blocks)
 
 
-def grad_kernel(latent, ids, n_head, facts_ref, *refs):
+def grad_kernel(ids, n_head, facts_ref, *refs):
     parts, w_refs, masses = refs[:n_head], refs[n_head : 2 * n_head], refs[2 * n_head : 3 * n_head]
-    target_ref, (w_ref, keys, grads, results) = refs[3 * n_head], refs[-4:]
-    n_blocks = (len(refs) - 3 * n_head - 5) // 2
-    blocks, outs = refs[3 * n_head + 1 : -n_blocks - 4], refs[-n_blocks - 4 : -4]
-    rows = blocks[0].shape[1]
+    target_ref, relu_ref = refs[3 * n_head : 3 * n_head + 2]
+    outs, (w_ref, grads, results) = refs[3 * n_head + 2 : -3], refs[-3:]
+    rows = outs[0].shape[0]
     share, idx_width = parts[0].shape[1:]
     scale = 1.0 / idx_width**0.5
     lay_weights(parts, w_refs, w_ref)
@@ -309,51 +312,47 @@
             token = lax.broadcasted_iota(jnp.int32, (rows, share), 1) + start
             grad = jnp.where(within + later * rows <= token, value, 0.0)
             grads[at(place, rows), :] = jnp.concatenate([grad] * (tile // share), axis=1)
-            keys[at(place, rows), :] = blocks[i][latent:, :]
 
     def work(here):
-        held = keys[here, :]
         grad = grads[here, :]
-        total = jnp.zeros((held.shape[0], idx_width), jnp.float32)
+        total = jnp.zeros((grad.shape[0], idx_width), jnp.float32)
         row = 0
         for part in parts:
             for run, piece in pieces(part, share, 8):
-                r = lax.dot_general(held, piece, NT, preferred_element_type=jnp.float32)
                 weighted = []
-                for k in range(run):
-                    w = grad * w_ref[row + k : row + k + 1, :]
-                    w = jnp.where(r[:, k * tile : (k + 1) * tile] > 0.0, w, 0.0)
-                    weighted.append(w.astype(jnp.bfloat16))
+                for k in range(row, row + run):
+                    w = (grad * w_ref[k : k + 1, :]).astype(jnp.bfloat16)
+                    r = relu_ref[here, k * tile : (k + 1) * tile]
+                    weighted.append(jnp.where(r > 0, w, jnp.zeros_like(w)))
                 row += run
                 total = total + lax.dot_general(
                     jnp.concatenate(weighted, axis=1), piece, NN, preferred_element_type=jnp.float32
                 )
         results[here, :] = total * scale
 
-    in_pairs(count, len(blocks), rows, work)
+    in_pairs(count, len(ids), rows, work)
     for out, (place, _, alive) in zip(outs, slots):
         out[...] = jnp.where(alive, results[at(place, rows), :], 0.0)
 
 
-def index_grad(known_facts, parts, weights, masses, target, ids, blocks, latent):
+def index_grad(known_facts, parts, weights, masses, target, relu, ids):
     n_head, (index_here, share, idx_width) = len(parts), parts[0].shape
-    rows = blocks[0].shape[1]
+    n, rows = len(ids), relu.shape[0] // len(ids)
     side = lanes_of(parts[0], share)
     return pl.pallas_call(
-        functools.partial(grad_kernel, latent, ids, n_head),
-        in_specs=[SMEM] + [VMEM] * (3 * n_head + 1 + len(blocks)),
-        out_specs=[VMEM] * len(blocks),
-        out_shape=[jax.ShapeDtypeStruct((rows, idx_width), jnp.float32)] * len(blocks),
+        functools.partial(grad_kernel, ids, n_head),
+        in_specs=[SMEM] + [VMEM] * (3 * n_head + 2),
+        out_specs=[VMEM] * n,
+        out_shape=[jax.ShapeDtypeStruct((rows, idx_width), jnp.float32)] * n,
         scratch_shapes=[
             pltpu.VMEM((n_head * index_here // side, side * share), jnp.float32),
-            pltpu.VMEM((len(blocks) * rows, idx_width), jnp.bfloat16),
-            pltpu.VMEM((len(blocks) * rows, side * share), jnp.float32),
-            pltpu.VMEM((len(blocks) * rows, idx_width), jnp.float32),
-        ],
-        cost_estimate=cost(4 * len(blocks) * rows * share * n_head * index_here * idx_width),
+            pltpu.VMEM((n * rows, side * share), jnp.float32),
+            pltpu.VMEM((n * rows, idx_width), jnp.float32),
+        ],
+        cost_estimate=cost(2 * n * rows * share * n_head * index_here * idx_width),
         compiler_params=pltpu.CompilerParams(vmem_limit_bytes=LIMIT),
         name="index_grad",
-    )(known_facts, *parts, *weights, *masses, target, *blocks)
+    )(known_facts, *parts, *weights, *masses, target, relu)
 
 
 def body(
@@ -416,8 +415,8 @@
     for ids, mass in zip((early, late), masses):
         for turn in range(1, n_head):
             mass[turn] = around(mass[turn], turn)
-        target = index_logits(tables, parts, weights, lse_share, ids, blocks(ids), latent)
-        found = index_grad(tables, parts, weights, mass, target, ids, blocks(ids), latent)
+        target, relu = index_logits(tables, parts, weights, lse_share, ids, blocks(ids), latent)
+        found = index_grad(tables, parts, weights, mass, target, relu, ids)
         grads.update(zip(ids, found))
 
     total = grads[0] + lax.ppermute(grads[1], "seq", back)

time: 65.6 us -> 64.9 us (0.989)
  starting transfers between devices: 28.9 us -> 27.3 us
  waiting for transfers between devices: 18.8 us -> 20 us
    ppermute x1, waiting for transfers between devices: 0.01 us -> 1.57 us  [body(): arrived.append(lax.ppermute(arrived[m - 3], 'seq', ring(4)))]
    ppermute x5, starting transfers between devices: 6.92 us -> 5.81 us  [around(): lax.ppermute(array, 'head', [(i, (i + turn) % n_head) for i in range(n_he...]
  transfers between devices with their start and end apart: 20 -> 20, of which waited for: 4 -> 5; matrix products, arithmetic and copies ran while one was open for 1% -> 1% of each run, Pallas kernels for 20% -> 20%
where the time goes in v6:
time: 64.9 us; the launch traced here: 63.6 us
  starting transfers between devices  27.3 us (42%)
  waiting for transfers between devices  20 us (31%)
  Pallas kernels  12.8 us (20%)
  local copies, waits for them, and re-layouts  1.66 us (3%)
  other arithmetic  1.63 us (3%)
    ppermute x1, waiting for transfers between devices, body(): arrived = [lax.ppermute(own, 'seq', ring(2))]  6.86 us
    ppermute x2, starting transfers between devices, body(): total = total + lax.ppermute(both, 'seq', ring(-2 * m))  6.34 us
    ppermute x5, waiting for transfers between devices, around(): lax.ppermute(array, 'head', [(i, (i + turn) % n_head) for i in range(n_he...  6.05 us
    ppermute x5, starting transfers between devices, around(): lax.ppermute(array, 'head', [(i, (i + turn) % n_head) for i in range(n_he...  5.81 us
    ppermute x2, waiting for transfers between devices, body(): last.append(lax.ppermute(both.astype(jnp.bfloat16), ('seq', 'head'), route))  5.5 us
    ppermute x1, starting transfers between devices, body(): total = grads[0] + lax.ppermute(grads[1], 'seq', back)  4.85 us
    pallas_call x3, Pallas kernels, head_mass(): pl.pallas_call(functools.partial(score_kernel, ids, len(shapes), n_head >...  4.39 us
    pallas_call x1, Pallas kernels, first_mass(): pl.pallas_call(first_kernel, in_specs=[SMEM, SMEM] + [VMEM] * 3, out_spec...  3.31 us
  transfers between devices with their start and end apart: 20, of which 5 were waited for; matrix products, arithmetic and copies ran while one was open for 1% of the time, Pallas kernels for 20%

profile of v6, /device:TPU:0, one launch (start us, length us, event | category | flops | bytes accessed | tf_op | source)
XLA Modules:
  0.0 63.6 jit_solution(15097336790530674701)
XLA Ops:
  0.0 0.9 %pad_maximum_fusion.block_ref = bf16[704,128]{1,0:T(8,128)(2,1)S(1)} fusion(bf16[128,128]{1,0:T(8,128)(2,1)} %param.14, bf16[576,128]{1,0:T(8,128)(2,1)} %bitcast.32), kind=kLoop, calls=%fused_computation.1 | loop fusion | flops 360448 | bytes 360448 | tf_op jit(solution)/shard_map/concatenate | solution.py:383
  0.9 0.0 copy-start.6
  1.0 1.2 %copy-done.6 = bf16[128,32,128]{2,1,0:T(8,128)(2,1)S(1)} copy-done((bf16[128,32,128]{2,1,0:T(8,128)(2,1)S(1)}, bf16[128,32,128]{2,1,0:T(8,128)(2,1)}, u32[]{:S(2)}) %copy-start.6) | copy-done | bytes 1048600
  2.2 0.0 copy-start
  2.2 0.1 cut_shares.1
  2.3 3.0 %collective-permute-start.5 = (bf16[704,128]{1,0:T(8,128)(2,1)S(1)}, bf16[704,128]{1,0:T(8,128)(2,1)S(1)}, u32[]{:S(2)}, u32[]{:S(2)}) collective-permute-start(bf16[704,128]{1,0:T(8,128)(2,1)S(1)} %get-tuple-element.28.block_ref.refs_5_), channel_id=1, source_target_pairs={{0,4},{2,6},{4,8},{6,10},{8,12},{10,14},{12,16},{14,18},{16,20},{1... | collective-permute-start | bytes 540680 | tf_op jit(solution)/shard_map/ppermute | solution.py:385
  5.3 1.6 %collective-permute-start.2 = (bf16[704,128]{1,0:T(8,128)(2,1)S(1)}, bf16[704,128]{1,0:T(8,128)(2,1)S(1)}, u32[]{:S(2)}, u32[]{:S(2)}) collective-permute-start(bf16[704,128]{1,0:T(8,128)(2,1)S(1)} %get-tuple-element.28.block_ref.refs_5_), channel_id=1, source_target_pairs={{0,8},{2,10},{4,12},{6,14},{8,16},{10,18},{12,20},{14,22},{16,24},... | collective-permute-start | bytes 540680 | tf_op jit(solution)/shard_map/ppermute | solution.py:386
  6.9 6.9 %collective-permute-done.5.refs_0_.refs_6_ = bf16[704,128]{1,0:T(8,128)(2,1)S(1)} collective-permute-done((bf16[704,128]{1,0:T(8,128)(2,1)S(1)}, bf16[704,128]{1,0:T(8,128)(2,1)S(1)}, u32[]{:S(2)}, u32[]{:S(2)}) %collective-permute-start.5) | collective-permute-done | bytes 180256 | tf_op jit(solution)/shard_map/ppermute | solution.py:385
  13.8 0.0 collective-permute-start.6
  13.8 0.5 collective-permute-start.4
  14.3 0.2 copy.12
  14.5 1.7 %collective-permute-start = (bf16[64,32,128]{2,0,1:T(8,128)(2,1)S(1)}, bf16[64,32,128]{2,0,1:T(8,128)(2,1)S(1)}, u32[]{:S(2)}, u32[]{:S(2)}) collective-permute-start(bf16[64,32,128]{2,0,1:T(8,128)(2,1)S(1)} %copy.12), channel_id=1, source_target_pairs={{0,1},{1,0},{2,3},{3,2},{4,5},{5,4},{6,7},{7,6},{8,9},{9,8},{10,11... | collective-permute-start | bytes 1572872 | tf_op jit(solution)/shard_map/ppermute | solution.py:378
  16.2 0.0 copy-done
  16.2 0.0 copy-done.1
  16.2 0.0 copy-done.3
  16.2 0.0 copy-done.5
  16.2 3.3 %first_mass.1 = (s32[16]{0:T(128)S(1)}, f32[128,128]{1,0:T(8,128)S(1)}) custom-call(s32[16]{0:T(128)S(1)} %copy-done.5, s32[16,16]{1,0:T(8,128)S(1)} %copy-done.3, bf16[64,576,128]{2,1,0:T(8,128)(2,1)S(1)} %bitcast.9, f32[64,128]{1,0:T(8,128)S(1)} %bitcast.21, bf16[704,128]{1,0:T(8,128)(2,1)S(1)} %get-tuple-element.28.block_ref.refs_5_), custom_call_target="tpu_custom_call" | custom-call | flops 1207959552 | bytes 4718592 | tf_op jit(solution)/shard_map/first_mass/pallas_call | solution.py:182
  19.6 0.1 collective-permute-start.14
  19.6 0.0 collective-permute-done.2.refs_0_.refs_8_
  19.6 1.4 %collective-permute-start.3 = (bf16[704,128]{1,0:T(8,128)(2,1)S(1)}, bf16[704,128]{1,0:T(8,128)(2,1)S(1)}, u32[]{:S(2)}, u32[]{:S(2)}) collective-permute-start(bf16[704,128]{1,0:T(8,128)(2,1)S(1)} %collective-permute-done.2.refs_0_.refs_8_), channel_id=1, source_target_pairs={{0,2},{2,0},{4,6},{6,4},{8,10},{10,8},{12,14},{14,12},{16,18},{18,... | collective-permute-start | bytes 540680 | tf_op jit(solution)/shard_map/ppermute | solution.py:391
  21.0 0.0 collective-permute-done.6.refs_1_.refs_7_
  21.0 2.6 %score_mass.3 = (f32[128,128]{1,0:T(8,128)S(1)}, f32[128,128]{1,0:T(8,128)S(1)}) custom-call(s32[16]{0:T(128)S(1)} %get-tuple-element.29.facts_ref, bf16[64,576,128]{2,1,0:T(8,128)(2,1)S(1)} %bitcast.10, f32[64,128]{1,0:T(8,128)S(1)} %bitcast.22, bf16[704,128]{1,0:T(8,128)(2,1)S(1)} %collective-permute-done.5.refs_0_.refs_6_, ...), custom_call_target="tpu_custom_call" | custom-call | flops 2415919104 | bytes 9437184 | tf_op jit(solution)/shard_map/score_mass/pallas_call | solution.py:156
  23.6 0.0 collective-permute-done.4.refs_2_.refs_10_
  23.6 0.0 collective-permute-done.3.refs_1_.refs_9_
  23.6 0.0 copy-start.2
  23.7 0.0 copy-start.4
  23.7 1.0 %score_mass.4 = (f32[384,128]{1,0:T(8,128)S(1)}, f32[384,128]{1,0:T(8,128)S(1)}) custom-call(s32[16]{0:T(128)S(1)} %get-tuple-element.29.facts_ref, bf16[64,576,128]{2,1,0:T(8,128)(2,1)S(1)} %bitcast.11, f32[64,128]{1,0:T(8,128)S(1)} %bitcast.23, bf16[704,128]{1,0:T(8,128)(2,1)S(1)} %collective-permute-done.2.refs_0_.refs_8_, ...), custom_call_target="tpu_custom_call" | custom-call | flops 3623878656 | bytes 14155776 | tf_op jit(solution)/shard_map/score_mass/pallas_call | solution.py:156
  24.7 0.6 collective-permute-start.7
  25.3 1.6 %collective-permute-done.14.refs_0_.refs_5_ = bf16[704,128]{1,0:T(8,128)(2,1)S(1)} collective-permute-done((bf16[704,128]{1,0:T(8,128)(2,1)S(1)}, bf16[704,128]{1,0:T(8,128)(2,1)S(1)}, u32[]{:S(2)}, u32[]{:S(2)}) %collective-permute-start.14) | collective-permute-done | bytes 180256 | tf_op jit(solution)/shard_map/ppermute | solution.py:390
  26.9 0.0 collective-permute-start.15
  26.9 0.0 copy-done.2
  26.9 0.4 collective-permute-start.1
  27.3 0.2 copy.14
  27.5 6.0 %collective-permute-done.1.refs_3_ = f32[32,128]{1,0:T(8,128)S(1)} collective-permute-done((f32[32,128]{1,0:T(8,128)S(1)}, f32[32,128]{1,0:T(8,128)S(1)}, u32[]{:S(2)}, u32[]{:S(2)}) %collective-permute-start.1) | collective-permute-done | bytes 16416 | tf_op jit(solution)/shard_map/ppermute | solution.py:378
  33.5 0.0 collective-permute-done
  33.5 0.0 copy-done.4
  33.5 1.6 %index_logits.2 = (f32[384,128]{1,0:T(8,128)S(1)}, bf16[768,4096]{1,0:T(8,128)(2,1)S(1)}) custom-call(s32[16]{0:T(128)S(1)} %get-tuple-element.29.facts_ref, bf16[32,64,128]{2,1,0:T(8,128)(2,1)S(1)} %bitcast.13, bf16[32,64,128]{2,1,0:T(8,128)(2,1)S(1)} %bitcast.17, f32[32,128]{1,0:T(8,128)S(1)} %bitcast.26, f32[32,128]{1,0:T(8,128)S(1)} %collective-permute-done.1.refs_3_, ...), custom_call_target="tpu_custom_call" | custom-call | flops 805306368 | bytes 3145728 | tf_op jit(solution)/shard_map/index_logits/pallas_call | solution.py:271
  35.1 0.0 collective-permute-done.7.refs_5_
  35.1 2.0 %index_grad.2 = (f32[128,128]{1,0:T(8,128)S(1)}, f32[128,128]{1,0:T(8,128)S(1)}, f32[128,128]{1,0:T(8,128)S(1)}, f32[128,128]{1,0:T(8,128)S(1)}, f32[128,128]{1,0:T(8,128)S(1)}, /*index=5*/f32[128,128]{1,0:T(8,128)S(1)}) custom-call(s32[16]{0:T(128)S(1)} %get-tuple-element.29.facts_ref, bf16[32,64,128]{2,1,0:T(8,128)(2,1)S(1)} %bitcast.14, ...), custom_call_target="tpu_custom_call" | custom-call | flops 805306368 | bytes 3145728 | tf_op jit(solution)/shard_map/index_grad/pallas_call | solution.py:342
  37.1 0.1 collective-permute-start.9
  37.2 0.5 collective-permute-start.11
  37.7 0.0 collective-permute-done.15.refs_1_.refs_6_
  37.7 0.8 %score_mass.5 = (f32[128,128]{1,0:T(8,128)S(1)}, f32[128,128]{1,0:T(8,128)S(1)}) custom-call(s32[16]{0:T(128)S(1)} %get-tuple-element.29.facts_ref, bf16[64,576,128]{2,1,0:T(8,128)(2,1)S(1)} %bitcast.12, f32[64,128]{1,0:T(8,128)S(1)} %bitcast.24, bf16[704,128]{1,0:T(8,128)(2,1)S(1)} %collective-permute-done.14.refs_0_.refs_5_, ...), custom_call_target="tpu_custom_call" | custom-call | flops 2415919104 | bytes 9437184 | tf_op jit(solution)/shard_map/score_mass/pallas_call | solution.py:156
  38.5 1.6 %collective-permute-start.16 = (f32[128,128]{1,0:T(8,128)S(1)}, f32[128,128]{1,0:T(8,128)S(1)}, u32[]{:S(2)}, u32[]{:S(2)}) collective-permute-start(f32[128,128]{1,0:T(8,128)S(1)} %get-tuple-element.46), channel_id=1, source_target_pairs={{0,1},{1,0},{2,3},{3,2},{4,5},{5,4},{6,7},{7,6},{8,9},{9,8},{10,11... | collective-permute-start | bytes 196616 | tf_op jit(solution)/shard_map/ppermute | solution.py:378
  40.0 4.9 %collective-permute-start.8 = (f32[128,128]{1,0:T(8,128)S(1)}, f32[128,128]{1,0:T(8,128)S(1)}, u32[]{:S(2)}, u32[]{:S(2)}) collective-permute-start(f32[128,128]{1,0:T(8,128)S(1)} %get-tuple-element.40), channel_id=1, source_target_pairs={{2,0},{16,2},{6,4},{20,6},{10,8},{24,10},{14,12},{28,14},{18,16},{... | collective-permute-start | bytes 196616 | tf_op jit(solution)/shard_map/ppermute | solution.py:422
  44.9 0.0 collective-permute-done.9
  44.9 0.1 collective-permute-start.10
  45.0 0.0 collective-permute-done.11
  45.0 6.3 %collective-permute-start.12 = (f32[128,128]{1,0:T(8,128)S(1)}, f32[128,128]{1,0:T(8,128)S(1)}, u32[]{:S(2)}, u32[]{:S(2)}) collective-permute-start(f32[128,128]{1,0:T(8,128)S(1)} %add.30), channel_id=1, source_target_pairs={{0,24},{2,26},{4,28},{6,30},{8,0},{10,2},{12,4},{14,6},{16,8},{18,... | collective-permute-start | bytes 196616 | tf_op jit(solution)/shard_map/ppermute | solution.py:426
  51.3 0.8 %index_logits.3 = (f32[128,128]{1,0:T(8,128)S(1)}, bf16[256,4096]{1,0:T(8,128)(2,1)S(1)}) custom-call(s32[16]{0:T(128)S(1)} %get-tuple-element.29.facts_ref, bf16[32,64,128]{2,1,0:T(8,128)(2,1)S(1)} %bitcast.15, bf16[32,64,128]{2,1,0:T(8,128)(2,1)S(1)} %bitcast.19, f32[32,128]{1,0:T(8,128)S(1)} %bitcast.28, f32[32,128]{1,0:T(8,128)S(1)} %collective-permute-done.1.refs_3_, ...), custom_call_target="tpu_custom_call" | custom-call | flops 268435456 | bytes 1048576 | tf_op jit(solution)/shard_map/index_logits/pallas_call | solution.py:271
  52.1 0.0 collective-permute-done.16.refs_5_
  52.1 0.7 %index_grad.3 = (f32[128,128]{1,0:T(8,128)S(1)}, f32[128,128]{1,0:T(8,128)S(1)}) custom-call(s32[16]{0:T(128)S(1)} %get-tuple-element.29.facts_ref, bf16[32,64,128]{2,1,0:T(8,128)(2,1)S(1)} %bitcast.16, bf16[32,64,128]{2,1,0:T(8,128)(2,1)S(1)} %bitcast.20, f32[32,128]{1,0:T(8,128)S(1)} %bitcast.29, f32[32,128]{1,0:T(8,128)S(1)} %collective-permute-done.1.refs_3_, ...), custom_call_target="tpu_custom_call" | custom-call | flops 268435456 | bytes 1048576 | tf_op jit(solution)/shard_map/index_grad/pallas_call | solution.py:342
  52.8 1.2 %collective-permute-start.17 = (f32[128,128]{1,0:T(8,128)S(1)}, f32[128,128]{1,0:T(8,128)S(1)}, u32[]{:S(2)}, u32[]{:S(2)}) collective-permute-start(f32[128,128]{1,0:T(8,128)S(1)} %get-tuple-element.50), channel_id=1, source_target_pairs={{0,2},{2,0},{4,6},{6,4},{8,10},{10,8},{12,14},{14,12},{16,18},{18,... | collective-permute-start | bytes 196616 | tf_op jit(solution)/shard_map/ppermute | solution.py:424
  53.9 0.0 collective-permute-done.8
  53.9 0.0 collective-permute-done.10
  53.9 0.0 collective-permute-done.12
  54.0 1.6 %collective-permute-start.13 = (f32[128,128]{1,0:T(8,128)S(1)}, f32[128,128]{1,0:T(8,128)S(1)}, u32[]{:S(2)}, u32[]{:S(2)}) collective-permute-start(f32[128,128]{1,0:T(8,128)S(1)} %add_add_fusion.1), channel_id=1, source_target_pairs={{0,1},{1,0},{2,3},{3,2},{4,5},{5,4},{6,7},{7,6},{8,9},{9,8},{10,11... | collective-permute-start | bytes 196616 | tf_op jit(solution)/shard_map/ppermute | solution.py:378
  55.5 0.0 collective-permute-done.17
  55.5 1.7 %collective-permute-start.18 = (bf16[128,128]{1,0:T(8,128)(2,1)S(1)}, bf16[128,128]{1,0:T(8,128)(2,1)S(1)}, u32[]{:S(2)}, u32[]{:S(2)}) collective-permute-start(bf16[128,128]{1,0:T(8,128)(2,1)S(1)} %add_convert_fusion), channel_id=1, source_target_pairs={{0,20},{1,21},{2,22},{3,23},{4,24},{5,25},{6,26},{7,27},{8,28},{9,... | collective-permute-start | bytes 98312 | tf_op jit(solution)/shard_map/ppermute | solution.py:434
  57.3 0.2 collective-permute-start.19
  57.5 3.2 %collective-permute-done.18 = bf16[128,128]{1,0:T(8,128)(2,1)S(1)} collective-permute-done((bf16[128,128]{1,0:T(8,128)(2,1)S(1)}, bf16[128,128]{1,0:T(8,128)(2,1)S(1)}, u32[]{:S(2)}, u32[]{:S(2)}) %collective-permute-start.18) | collective-permute-done | bytes 32800 | tf_op jit(solution)/shard_map/ppermute | solution.py:434
  60.7 2.3 %collective-permute-done.19 = bf16[128,128]{1,0:T(8,128)(2,1)S(1)} collective-permute-done((bf16[128,128]{1,0:T(8,128)(2,1)S(1)}, bf16[128,128]{1,0:T(8,128)(2,1)S(1)}, u32[]{:S(2)}, u32[]{:S(2)}) %collective-permute-start.19) | collective-permute-done | bytes 32800 | tf_op jit(solution)/shard_map/ppermute | solution.py:434
  63.0 0.0 collective-permute-done.13
  63.0 0.6 %add_add_fusion = f32[128,128]{1,0:T(8,128)} fusion(bf16[128,128]{1,0:T(8,128)(2,1)S(1)} %collective-permute-done.19, bf16[128,128]{1,0:T(8,128)(2,1)S(1)} %collective-permute-done.18, f32[128,128]{1,0:T(8,128)S(1)} %add_add_fusion.1, f32[128,128]{1,0:T(8,128)S(1)} %collective-permute-done.13), kind=kLoop, calls=%fused_computation.2 | loop fusion | flops 81920 | bytes 262144 | tf_op jit(solution)/shard_map/add | solution.py:436
  (7 shorter events, 0.1 us)
Async XLA Ops:
  0.9 1.2 %copy-start.6 = (bf16[128,32,128]{2,1,0:T(8,128)(2,1)S(1)}, bf16[128,32,128]{2,1,0:T(8,128)(2,1)}, u32[]{:S(2)}) copy-start(bf16[128,32,128]{2,1,0:T(8,128)(2,1)} %queries_ref.1) | copy-start | bytes 3145732
  2.2 14.0 %copy-start = (bf16[128,64,576]{0,2,1:T(8,128)(2,1)S(1)}, bf16[128,64,576]{0,2,1:T(8,128)(2,1)}, u32[]{:S(2)}) copy-start(bf16[128,64,576]{0,2,1:T(8,128)(2,1)} %param.9) | copy-start | bytes 28311556
  2.2 14.0 %copy-start.1 = (f32[128,64]{0,1:T(8,128)S(1)}, f32[128,64]{0,1:T(8,128)}, u32[]{:S(2)}) copy-start(f32[128,64]{0,1:T(8,128)} %param.11) | copy-start | bytes 98308
  2.2 14.1 %copy-start.3 = (s32[16,16]{1,0:T(8,128)S(1)}, s32[16,16]{1,0:T(8,128)}, u32[]{:S(2)}) copy-start(s32[16,16]{1,0:T(8,128)} %live_ref.1) | copy-start | bytes 3076
  2.2 14.1 %copy-start.5 = (s32[16]{0:T(128)S(1)}, s32[16]{0:T(128)}, u32[]{:S(2)}) copy-start(s32[16]{0:T(128)} %order_ref.1) | copy-start | bytes 196
  2.3 11.5 %collective-permute-start.5 = (bf16[704,128]{1,0:T(8,128)(2,1)S(1)}, bf16[704,128]{1,0:T(8,128)(2,1)S(1)}, u32[]{:S(2)}, u32[]{:S(2)}) collective-permute-start(bf16[704,128]{1,0:T(8,128)(2,1)S(1)} %get-tuple-element.28.block_ref.refs_5_), channel_id=1, source_target_pairs={{0,4},{2,6},{4,8},{6,10},{8,12},{10,14},{12,16},{14,18},{16,20},{1... | collective-permute-start | bytes 540680 | tf_op jit(solution)/shard_map/ppermute | solution.py:385
  5.3 14.3 %collective-permute-start.2 = (bf16[704,128]{1,0:T(8,128)(2,1)S(1)}, bf16[704,128]{1,0:T(8,128)(2,1)S(1)}, u32[]{:S(2)}, u32[]{:S(2)}) collective-permute-start(bf16[704,128]{1,0:T(8,128)(2,1)S(1)} %get-tuple-element.28.block_ref.refs_5_), channel_id=1, source_target_pairs={{0,8},{2,10},{4,12},{6,14},{8,16},{10,18},{12,20},{14,22},{16,24},... | collective-permute-start | bytes 540680 | tf_op jit(solution)/shard_map/ppermute | solution.py:386
  13.8 7.2 %collective-permute-start.6 = (bf16[704,128]{1,0:T(8,128)(2,1)S(1)}, bf16[704,128]{1,0:T(8,128)(2,1)S(1)}, u32[]{:S(2)}, u32[]{:S(2)}) collective-permute-start(bf16[704,128]{1,0:T(8,128)(2,1)S(1)} %collective-permute-done.5.refs_0_.refs_6_), channel_id=1, source_target_pairs={{0,2},{2,0},{4,6},{6,4},{8,10},{10,8},{12,14},{14,12},{16,18},{18,... | collective-permute-start | bytes 540680 | tf_op jit(solution)/shard_map/ppermute | solution.py:391
  13.8 9.8 %collective-permute-start.4 = (bf16[704,128]{1,0:T(8,128)(2,1)S(1)}, bf16[704,128]{1,0:T(8,128)(2,1)S(1)}, u32[]{:S(2)}, u32[]{:S(2)}) collective-permute-start(bf16[704,128]{1,0:T(8,128)(2,1)S(1)} %get-tuple-element.28.block_ref.refs_5_), channel_id=1, source_target_pairs={{0,2},{2,16},{4,6},{6,20},{8,10},{10,24},{12,14},{14,28},{16,18},{... | collective-permute-start | bytes 540680 | tf_op jit(solution)/shard_map/ppermute | solution.py:387
  14.5 19.0 %collective-permute-start = (bf16[64,32,128]{2,0,1:T(8,128)(2,1)S(1)}, bf16[64,32,128]{2,0,1:T(8,128)(2,1)S(1)}, u32[]{:S(2)}, u32[]{:S(2)}) collective-permute-start(bf16[64,32,128]{2,0,1:T(8,128)(2,1)S(1)} %copy.12), channel_id=1, source_target_pairs={{0,1},{1,0},{2,3},{3,2},{4,5},{5,4},{6,7},{7,6},{8,9},{9,8},{10,11... | collective-permute-start | bytes 1572872 | tf_op jit(solution)/shard_map/ppermute | solution.py:378
  19.6 7.3 %collective-permute-start.14 = (bf16[704,128]{1,0:T(8,128)(2,1)S(1)}, bf16[704,128]{1,0:T(8,128)(2,1)S(1)}, u32[]{:S(2)}, u32[]{:S(2)}) collective-permute-start(bf16[704,128]{1,0:T(8,128)(2,1)S(1)} %collective-permute-done.5.refs_0_.refs_6_), channel_id=1, source_target_pairs={{0,8},{2,10},{4,12},{6,14},{8,16},{10,18},{12,20},{14,22},{16,24},... | collective-permute-start | bytes 540680 | tf_op jit(solution)/shard_map/ppermute | solution.py:390
  19.6 4.0 %collective-permute-start.3 = (bf16[704,128]{1,0:T(8,128)(2,1)S(1)}, bf16[704,128]{1,0:T(8,128)(2,1)S(1)}, u32[]{:S(2)}, u32[]{:S(2)}) collective-permute-start(bf16[704,128]{1,0:T(8,128)(2,1)S(1)} %collective-permute-done.2.refs_0_.refs_8_), channel_id=1, source_target_pairs={{0,2},{2,0},{4,6},{6,4},{8,10},{10,8},{12,14},{14,12},{16,18},{18,... | collective-permute-start | bytes 540680 | tf_op jit(solution)/shard_map/ppermute | solution.py:391
  23.6 3.3 %copy-start.2 = (f32[128,32]{0,1:T(8,128)S(1)}, f32[128,32]{0,1:T(8,128)}, u32[]{:S(2)}) copy-start(f32[128,32]{0,1:T(8,128)} %param.13) | copy-start | bytes 49156
  23.7 9.9 %copy-start.4 = (f32[128]{0:T(128)S(1)}, f32[128]{0:T(128)}, u32[]{:S(2)}) copy-start(f32[128]{0:T(128)} %param.15) | copy-start | bytes 1540
  24.7 10.4 %collective-permute-start.7 = (f32[384,128]{1,0:T(8,128)S(1)}, f32[384,128]{1,0:T(8,128)S(1)}, u32[]{:S(2)}, u32[]{:S(2)}) collective-permute-start(f32[384,128]{1,0:T(8,128)S(1)} %get-tuple-element.36), channel_id=1, source_target_pairs={{0,1},{1,0},{2,3},{3,2},{4,5},{5,4},{6,7},{7,6},{8,9},{9,8},{10,11... | collective-permute-start | bytes 589832 | tf_op jit(solution)/shard_map/ppermute | solution.py:378
  26.9 10.8 %collective-permute-start.15 = (bf16[704,128]{1,0:T(8,128)(2,1)S(1)}, bf16[704,128]{1,0:T(8,128)(2,1)S(1)}, u32[]{:S(2)}, u32[]{:S(2)}) collective-permute-start(bf16[704,128]{1,0:T(8,128)(2,1)S(1)} %collective-permute-done.14.refs_0_.refs_5_), channel_id=1, source_target_pairs={{0,2},{2,0},{4,6},{6,4},{8,10},{10,8},{12,14},{14,12},{16,18},{18,... | collective-permute-start | bytes 540680 | tf_op jit(solution)/shard_map/ppermute | solution.py:391
  26.9 6.6 %collective-permute-start.1 = (f32[32,128]{1,0:T(8,128)S(1)}, f32[32,128]{1,0:T(8,128)S(1)}, u32[]{:S(2)}, u32[]{:S(2)}) collective-permute-start(f32[32,128]{1,0:T(8,128)S(1)} %bitcast.25), channel_id=1, source_target_pairs={{0,1},{1,0},{2,3},{3,2},{4,5},{5,4},{6,7},{7,6},{8,9},{9,8},{10,11... | collective-permute-start | bytes 49160 | tf_op jit(solution)/shard_map/ppermute | solution.py:378
  37.1 7.8 %collective-permute-start.9 = (f32[128,128]{1,0:T(8,128)S(1)}, f32[128,128]{1,0:T(8,128)S(1)}, u32[]{:S(2)}, u32[]{:S(2)}) collective-permute-start(f32[128,128]{1,0:T(8,128)S(1)} %get-tuple-element.42), channel_id=1, source_target_pairs={{0,2},{2,0},{4,6},{6,4},{8,10},{10,8},{12,14},{14,12},{16,18},{18,... | collective-permute-start | bytes 196616 | tf_op jit(solution)/shard_map/ppermute | solution.py:424
  37.2 7.8 %collective-permute-start.11 = (f32[128,128]{1,0:T(8,128)S(1)}, f32[128,128]{1,0:T(8,128)S(1)}, u32[]{:S(2)}, u32[]{:S(2)}) collective-permute-start(f32[128,128]{1,0:T(8,128)S(1)} %get-tuple-element.44), channel_id=1, source_target_pairs={{0,2},{2,0},{4,6},{6,4},{8,10},{10,8},{12,14},{14,12},{16,18},{18,... | collective-permute-start | bytes 196616 | tf_op jit(solution)/shard_map/ppermute | solution.py:424
  38.5 13.6 %collective-permute-start.16 = (f32[128,128]{1,0:T(8,128)S(1)}, f32[128,128]{1,0:T(8,128)S(1)}, u32[]{:S(2)}, u32[]{:S(2)}) collective-permute-start(f32[128,128]{1,0:T(8,128)S(1)} %get-tuple-element.46), channel_id=1, source_target_pairs={{0,1},{1,0},{2,3},{3,2},{4,5},{5,4},{6,7},{7,6},{8,9},{9,8},{10,11... | collective-permute-start | bytes 196616 | tf_op jit(solution)/shard_map/ppermute | solution.py:378
  40.0 13.9 %collective-permute-start.8 = (f32[128,128]{1,0:T(8,128)S(1)}, f32[128,128]{1,0:T(8,128)S(1)}, u32[]{:S(2)}, u32[]{:S(2)}) collective-permute-start(f32[128,128]{1,0:T(8,128)S(1)} %get-tuple-element.40), channel_id=1, source_target_pairs={{2,0},{16,2},{6,4},{20,6},{10,8},{24,10},{14,12},{28,14},{18,16},{... | collective-permute-start | bytes 196616 | tf_op jit(solution)/shard_map/ppermute | solution.py:422
  44.9 9.0 %collective-permute-start.10 = (f32[128,128]{1,0:T(8,128)S(1)}, f32[128,128]{1,0:T(8,128)S(1)}, u32[]{:S(2)}, u32[]{:S(2)}) collective-permute-start(f32[128,128]{1,0:T(8,128)S(1)} %add.28), channel_id=1, source_target_pairs={{0,28},{2,30},{4,0},{6,2},{8,4},{10,6},{12,8},{14,10},{16,12},{18,... | collective-permute-start | bytes 196616 | tf_op jit(solution)/shard_map/ppermute | solution.py:426
  45.0 8.9 %collective-permute-start.12 = (f32[128,128]{1,0:T(8,128)S(1)}, f32[128,128]{1,0:T(8,128)S(1)}, u32[]{:S(2)}, u32[]{:S(2)}) collective-permute-start(f32[128,128]{1,0:T(8,128)S(1)} %add.30), channel_id=1, source_target_pairs={{0,24},{2,26},{4,28},{6,30},{8,0},{10,2},{12,4},{14,6},{16,8},{18,... | collective-permute-start | bytes 196616 | tf_op jit(solution)/shard_map/ppermute | solution.py:426
  52.8 2.8 %collective-permute-start.17 = (f32[128,128]{1,0:T(8,128)S(1)}, f32[128,128]{1,0:T(8,128)S(1)}, u32[]{:S(2)}, u32[]{:S(2)}) collective-permute-start(f32[128,128]{1,0:T(8,128)S(1)} %get-tuple-element.50), channel_id=1, source_target_pairs={{0,2},{2,0},{4,6},{6,4},{8,10},{10,8},{12,14},{14,12},{16,18},{18,... | collective-permute-start | bytes 196616 | tf_op jit(solution)/shard_map/ppermute | solution.py:424
  54.0 9.0 %collective-permute-start.13 = (f32[128,128]{1,0:T(8,128)S(1)}, f32[128,128]{1,0:T(8,128)S(1)}, u32[]{:S(2)}, u32[]{:S(2)}) collective-permute-start(f32[128,128]{1,0:T(8,128)S(1)} %add_add_fusion.1), channel_id=1, source_target_pairs={{0,1},{1,0},{2,3},{3,2},{4,5},{5,4},{6,7},{7,6},{8,9},{9,8},{10,11... | collective-permute-start | bytes 196616 | tf_op jit(solution)/shard_map/ppermute | solution.py:378
  55.5 5.2 %collective-permute-start.18 = (bf16[128,128]{1,0:T(8,128)(2,1)S(1)}, bf16[128,128]{1,0:T(8,128)(2,1)S(1)}, u32[]{:S(2)}, u32[]{:S(2)}) collective-permute-start(bf16[128,128]{1,0:T(8,128)(2,1)S(1)} %add_convert_fusion), channel_id=1, source_target_pairs={{0,20},{1,21},{2,22},{3,23},{4,24},{5,25},{6,26},{7,27},{8,28},{9,... | collective-permute-start | bytes 98312 | tf_op jit(solution)/shard_map/ppermute | solution.py:434
  57.3 5.7 %collective-permute-start.19 = (bf16[128,128]{1,0:T(8,128)(2,1)S(1)}, bf16[128,128]{1,0:T(8,128)(2,1)S(1)}, u32[]{:S(2)}, u32[]{:S(2)}) collective-permute-start(bf16[128,128]{1,0:T(8,128)(2,1)S(1)} %add_convert_fusion), channel_id=1, source_target_pairs={{0,21},{1,20},{2,23},{3,22},{4,25},{5,24},{6,27},{7,26},{8,29},{9,... | collective-permute-start | bytes 98312 | tf_op jit(solution)/shard_map/ppermute | solution.py:434

commit v7 on v6

--- a/solution.py
+++ b/solution.py
@@ -107,10 +107,24 @@
     return pl.CostEstimate(flops=flops, transcendentals=0, bytes_accessed=flops // 256)
 
 
+def mass_of(keys, q_ref, lse_ref):
+    heads, _, tokens = q_ref.shape
+    total = None
+    for h in range(0, heads, 2):
+        pair = jnp.concatenate([q_ref[h], q_ref[h + 1]], axis=1)
+        s = lax.dot_general(keys, pair, NN, preferred_element_type=jnp.float32)
+        s = s * (MAIN_SCALE * LOG2E)
+        for n in range(2):
+            lse = lse_ref[h + n : h + n + 1, :] * LOG2E
+            p = jnp.exp2(s[:, n * tokens : (n + 1) * tokens] - lse)
+            total = p if total is None else total + p
+    return total
+
+
 def score_kernel(ids, n_outs, pack, facts_ref, q_ref, lse_ref, *refs):
     blocks, known = refs[: len(ids)], refs[len(ids) : -n_outs - 2]
     outs, (keys, mass) = refs[-n_outs - 2 : -2], refs[-2:]
-    heads, latent, tokens = q_ref.shape
+    latent, tokens = q_ref.shape[1:]
     rows = blocks[0].shape[1]
     slots, count = packed(ids, facts_ref)
     for block, (place, _, alive) in zip(blocks, slots):
@@ -120,17 +134,7 @@
             keys[at(place, rows), :] = block[:latent, :].T
 
     def work(here):
-        held = keys[here, :]
-        total = None
-        for h in range(0, heads, 2):
-            pair = jnp.concatenate([q_ref[h], q_ref[h + 1]], axis=1)
-            s = lax.dot_general(held, pair, NN, preferred_element_type=jnp.float32)
-            s = s * (MAIN_SCALE * LOG2E)
-            for n in range(2):
-                lse = lse_ref[h + n : h + n + 1, :] * LOG2E
-                p = jnp.exp2(s[:, n * tokens : (n + 1) * tokens] - lse)
-                total = p if total is None else total + p
-        mass[here, :] = total
+        mass[here, :] = mass_of(keys[here, :], q_ref, lse_ref)
 
     in_pairs(count, len(blocks), rows, work)
     values = [jnp.where(alive, mass[at(place, rows), :], 0.0) for place, _, alive in slots]
@@ -168,12 +172,14 @@
     )(known_facts, q, lse, *blocks, *known)
 
 
-def first_kernel(order_ref, live_ref, q_ref, lse_ref, block_ref, facts_ref, mass_ref, keys, mass):
+def first_kernel(order_ref, live_ref, q_ref, lse_ref, block_ref, facts_ref, mass_ref):
+    own_alive = facts(0, order_ref, live_ref)[1]
+    mass = mass_of(block_ref[: q_ref.shape[1], :].T, q_ref, lse_ref)
+    mass_ref[...] = jnp.where(own_alive, mass, 0.0)
     for i in range(HOPS):
         later, alive = facts(i, order_ref, live_ref)
         facts_ref[2 * i] = later
         facts_ref[2 * i + 1] = alive.astype(jnp.int32)
-    score_kernel((0,), 1, False, facts_ref, q_ref, lse_ref, block_ref, mass_ref, keys, mass)
 
 
 def first_mass(order, live, q, lse, block):
@@ -186,10 +192,6 @@
         out_shape=[
             jax.ShapeDtypeStruct((2 * HOPS,), jnp.int32),
             jax.ShapeDtypeStruct((rows, tokens), jnp.float32),
-        ],
-        scratch_shapes=[
-            pltpu.VMEM((rows, latent), jnp.bfloat16),
-            pltpu.VMEM((rows, tokens), jnp.float32),
         ],
         cost_estimate=cost(2 * tokens * heads * latent * rows),
         compiler_params=pltpu.CompilerParams(vmem_limit_bytes=LIMIT),

time: 64.9 us -> 64.7 us (level)
    ppermute x1, waiting for transfers between devices: 1.57 us -> 2.66 us  [body(): arrived.append(lax.ppermute(arrived[m - 3], 'seq', ring(4)))]
    ppermute x5, waiting for transfers between devices: 6.05 us -> 5.04 us  [around(): lax.ppermute(array, 'head', [(i, (i + turn) % n_head) for i in range(n_he...]
where the time goes in v7:
time: 64.7 us; the launch traced here: 63.4 us
  starting transfers between devices  27.2 us (42%)
  waiting for transfers between devices  20.1 us (31%)
  Pallas kernels  12.6 us (19%)
  local copies, waits for them, and re-layouts  1.66 us (3%)
  other arithmetic  1.63 us (3%)
    ppermute x1, waiting for transfers between devices, body(): arrived = [lax.ppermute(own, 'seq', ring(2))]  6.86 us
    ppermute x2, starting transfers between devices, body(): total = total + lax.ppermute(both, 'seq', ring(-2 * m))  6.11 us
    ppermute x5, starting transfers between devices, around(): lax.ppermute(array, 'head', [(i, (i + turn) % n_head) for i in range(n_he...  5.96 us
    ppermute x2, waiting for transfers between devices, body(): last.append(lax.ppermute(both.astype(jnp.bfloat16), ('seq', 'head'), route))  5.49 us
    ppermute x5, waiting for transfers between devices, around(): lax.ppermute(array, 'head', [(i, (i + turn) % n_head) for i in range(n_he...  5.04 us
    ppermute x1, starting transfers between devices, body(): total = grads[0] + lax.ppermute(grads[1], 'seq', back)  4.85 us
    pallas_call x3, Pallas kernels, head_mass(): pl.pallas_call(functools.partial(score_kernel, ids, len(shapes), n_head >...  4.39 us
    pallas_call x1, Pallas kernels, first_mass(): pl.pallas_call(first_kernel, in_specs=[SMEM, SMEM] + [VMEM] * 3, out_spec...  3.07 us
  transfers between devices with their start and end apart: 20, of which 5 were waited for; matrix products, arithmetic and copies ran while one was open for 1% of the time, Pallas kernels for 20%

profile of v7, /device:TPU:0, one launch (start us, length us, event | category | flops | bytes accessed | tf_op | source)
XLA Modules:
  0.0 63.4 jit_solution(11724313646239710505)
XLA Ops:
  0.0 0.9 %pad_maximum_fusion.block_ref = bf16[704,128]{1,0:T(8,128)(2,1)S(1)} fusion(bf16[128,128]{1,0:T(8,128)(2,1)} %param.14, bf16[576,128]{1,0:T(8,128)(2,1)} %bitcast.32), kind=kLoop, calls=%fused_computation.1 | loop fusion | flops 360448 | bytes 360448 | tf_op jit(solution)/shard_map/concatenate | solution.py:385
  0.9 0.0 copy-start.6
  1.0 1.2 %copy-done.6 = bf16[128,32,128]{2,1,0:T(8,128)(2,1)S(1)} copy-done((bf16[128,32,128]{2,1,0:T(8,128)(2,1)S(1)}, bf16[128,32,128]{2,1,0:T(8,128)(2,1)}, u32[]{:S(2)}) %copy-start.6) | copy-done | bytes 1048600
  2.2 0.0 copy-start
  2.2 0.1 cut_shares.1
  2.3 3.0 %collective-permute-start.5 = (bf16[704,128]{1,0:T(8,128)(2,1)S(1)}, bf16[704,128]{1,0:T(8,128)(2,1)S(1)}, u32[]{:S(2)}, u32[]{:S(2)}) collective-permute-start(bf16[704,128]{1,0:T(8,128)(2,1)S(1)} %get-tuple-element.28.block_ref.refs_5_), channel_id=1, source_target_pairs={{0,4},{2,6},{4,8},{6,10},{8,12},{10,14},{12,16},{14,18},{16,20},{1... | collective-permute-start | bytes 540680 | tf_op jit(solution)/shard_map/ppermute | solution.py:387
  5.3 1.6 %collective-permute-start.2 = (bf16[704,128]{1,0:T(8,128)(2,1)S(1)}, bf16[704,128]{1,0:T(8,128)(2,1)S(1)}, u32[]{:S(2)}, u32[]{:S(2)}) collective-permute-start(bf16[704,128]{1,0:T(8,128)(2,1)S(1)} %get-tuple-element.28.block_ref.refs_5_), channel_id=1, source_target_pairs={{0,8},{2,10},{4,12},{6,14},{8,16},{10,18},{12,20},{14,22},{16,24},... | collective-permute-start | bytes 540680 | tf_op jit(solution)/shard_map/ppermute | solution.py:388
  6.9 6.9 %collective-permute-done.5.refs_0_.refs_6_ = bf16[704,128]{1,0:T(8,128)(2,1)S(1)} collective-permute-done((bf16[704,128]{1,0:T(8,128)(2,1)S(1)}, bf16[704,128]{1,0:T(8,128)(2,1)S(1)}, u32[]{:S(2)}, u32[]{:S(2)}) %collective-permute-start.5) | collective-permute-done | bytes 180256 | tf_op jit(solution)/shard_map/ppermute | solution.py:387
  13.8 0.0 collective-permute-start.6
  13.8 0.5 collective-permute-start.4
  14.3 0.2 copy.12
  14.5 1.7 %collective-permute-start = (bf16[64,32,128]{2,0,1:T(8,128)(2,1)S(1)}, bf16[64,32,128]{2,0,1:T(8,128)(2,1)S(1)}, u32[]{:S(2)}, u32[]{:S(2)}) collective-permute-start(bf16[64,32,128]{2,0,1:T(8,128)(2,1)S(1)} %copy.12), channel_id=1, source_target_pairs={{0,1},{1,0},{2,3},{3,2},{4,5},{5,4},{6,7},{7,6},{8,9},{9,8},{10,11... | collective-permute-start | bytes 1572872 | tf_op jit(solution)/shard_map/ppermute | solution.py:380
  16.2 0.0 copy-done
  16.2 0.0 copy-done.1
  16.2 0.0 copy-done.3
  16.2 0.0 copy-done.5
  16.2 3.1 %first_mass.1 = (s32[16]{0:T(128)S(1)}, f32[128,128]{1,0:T(8,128)S(1)}) custom-call(s32[16]{0:T(128)S(1)} %copy-done.5, s32[16,16]{1,0:T(8,128)S(1)} %copy-done.3, bf16[64,576,128]{2,1,0:T(8,128)(2,1)S(1)} %bitcast.9, f32[64,128]{1,0:T(8,128)S(1)} %bitcast.21, bf16[704,128]{1,0:T(8,128)(2,1)S(1)} %get-tuple-element.28.block_ref.refs_5_), custom_call_target="tpu_custom_call" | custom-call | flops 1207959552 | bytes 4718592 | tf_op jit(solution)/shard_map/first_mass/pallas_call | solution.py:188
  19.3 0.1 collective-permute-start.14
  19.4 0.0 collective-permute-done.2.refs_0_.refs_8_
  19.4 1.4 %collective-permute-start.3 = (bf16[704,128]{1,0:T(8,128)(2,1)S(1)}, bf16[704,128]{1,0:T(8,128)(2,1)S(1)}, u32[]{:S(2)}, u32[]{:S(2)}) collective-permute-start(bf16[704,128]{1,0:T(8,128)(2,1)S(1)} %collective-permute-done.2.refs_0_.refs_8_), channel_id=1, source_target_pairs={{0,2},{2,0},{4,6},{6,4},{8,10},{10,8},{12,14},{14,12},{16,18},{18,... | collective-permute-start | bytes 540680 | tf_op jit(solution)/shard_map/ppermute | solution.py:393
  20.8 0.0 collective-permute-done.6.refs_1_.refs_7_
  20.8 2.6 %score_mass.3 = (f32[128,128]{1,0:T(8,128)S(1)}, f32[128,128]{1,0:T(8,128)S(1)}) custom-call(s32[16]{0:T(128)S(1)} %get-tuple-element.29.facts_ref, bf16[64,576,128]{2,1,0:T(8,128)(2,1)S(1)} %bitcast.10, f32[64,128]{1,0:T(8,128)S(1)} %bitcast.22, bf16[704,128]{1,0:T(8,128)(2,1)S(1)} %collective-permute-done.5.refs_0_.refs_6_, ...), custom_call_target="tpu_custom_call" | custom-call | flops 2415919104 | bytes 9437184 | tf_op jit(solution)/shard_map/score_mass/pallas_call | solution.py:160
  23.4 0.0 collective-permute-done.4.refs_2_.refs_10_
  23.4 0.0 collective-permute-done.3.refs_1_.refs_9_
  23.4 0.0 copy-start.2
  23.4 0.0 copy-start.4
  23.4 1.0 %score_mass.4 = (f32[384,128]{1,0:T(8,128)S(1)}, f32[384,128]{1,0:T(8,128)S(1)}) custom-call(s32[16]{0:T(128)S(1)} %get-tuple-element.29.facts_ref, bf16[64,576,128]{2,1,0:T(8,128)(2,1)S(1)} %bitcast.11, f32[64,128]{1,0:T(8,128)S(1)} %bitcast.23, bf16[704,128]{1,0:T(8,128)(2,1)S(1)} %collective-permute-done.2.refs_0_.refs_8_, ...), custom_call_target="tpu_custom_call" | custom-call | flops 3623878656 | bytes 14155776 | tf_op jit(solution)/shard_map/score_mass/pallas_call | solution.py:160
  24.5 0.6 collective-permute-start.7
  25.1 2.7 %collective-permute-done.14.refs_0_.refs_5_ = bf16[704,128]{1,0:T(8,128)(2,1)S(1)} collective-permute-done((bf16[704,128]{1,0:T(8,128)(2,1)S(1)}, bf16[704,128]{1,0:T(8,128)(2,1)S(1)}, u32[]{:S(2)}, u32[]{:S(2)}) %collective-permute-start.14) | collective-permute-done | bytes 180256 | tf_op jit(solution)/shard_map/ppermute | solution.py:392
  27.7 0.0 collective-permute-start.15
  27.7 0.0 copy-done.2
  27.7 0.5 collective-permute-start.1
  28.3 0.2 copy.14
  28.5 5.0 %collective-permute-done.1.refs_3_ = f32[32,128]{1,0:T(8,128)S(1)} collective-permute-done((f32[32,128]{1,0:T(8,128)S(1)}, f32[32,128]{1,0:T(8,128)S(1)}, u32[]{:S(2)}, u32[]{:S(2)}) %collective-permute-start.1) | collective-permute-done | bytes 16416 | tf_op jit(solution)/shard_map/ppermute | solution.py:380
  33.5 0.0 collective-permute-done
  33.5 0.0 copy-done.4
  33.5 1.6 %index_logits.2 = (f32[384,128]{1,0:T(8,128)S(1)}, bf16[768,4096]{1,0:T(8,128)(2,1)S(1)}) custom-call(s32[16]{0:T(128)S(1)} %get-tuple-element.29.facts_ref, bf16[32,64,128]{2,1,0:T(8,128)(2,1)S(1)} %bitcast.13, bf16[32,64,128]{2,1,0:T(8,128)(2,1)S(1)} %bitcast.17, f32[32,128]{1,0:T(8,128)S(1)} %bitcast.26, f32[32,128]{1,0:T(8,128)S(1)} %collective-permute-done.1.refs_3_, ...), custom_call_target="tpu_custom_call" | custom-call | flops 805306368 | bytes 3145728 | tf_op jit(solution)/shard_map/index_logits/pallas_call | solution.py:273
  35.1 0.0 collective-permute-done.7.refs_5_
  35.1 2.0 %index_grad.2 = (f32[128,128]{1,0:T(8,128)S(1)}, f32[128,128]{1,0:T(8,128)S(1)}, f32[128,128]{1,0:T(8,128)S(1)}, f32[128,128]{1,0:T(8,128)S(1)}, f32[128,128]{1,0:T(8,128)S(1)}, /*index=5*/f32[128,128]{1,0:T(8,128)S(1)}) custom-call(s32[16]{0:T(128)S(1)} %get-tuple-element.29.facts_ref, bf16[32,64,128]{2,1,0:T(8,128)(2,1)S(1)} %bitcast.14, ...), custom_call_target="tpu_custom_call" | custom-call | flops 805306368 | bytes 3145728 | tf_op jit(solution)/shard_map/index_grad/pallas_call | solution.py:344
  37.1 0.1 collective-permute-start.9
  37.2 0.5 collective-permute-start.11
  37.7 0.0 collective-permute-done.15.refs_1_.refs_6_
  37.7 0.8 %score_mass.5 = (f32[128,128]{1,0:T(8,128)S(1)}, f32[128,128]{1,0:T(8,128)S(1)}) custom-call(s32[16]{0:T(128)S(1)} %get-tuple-element.29.facts_ref, bf16[64,576,128]{2,1,0:T(8,128)(2,1)S(1)} %bitcast.12, f32[64,128]{1,0:T(8,128)S(1)} %bitcast.24, bf16[704,128]{1,0:T(8,128)(2,1)S(1)} %collective-permute-done.14.refs_0_.refs_5_, ...), custom_call_target="tpu_custom_call" | custom-call | flops 2415919104 | bytes 9437184 | tf_op jit(solution)/shard_map/score_mass/pallas_call | solution.py:160
  38.5 1.6 %collective-permute-start.16 = (f32[128,128]{1,0:T(8,128)S(1)}, f32[128,128]{1,0:T(8,128)S(1)}, u32[]{:S(2)}, u32[]{:S(2)}) collective-permute-start(f32[128,128]{1,0:T(8,128)S(1)} %get-tuple-element.46), channel_id=1, source_target_pairs={{0,1},{1,0},{2,3},{3,2},{4,5},{5,4},{6,7},{7,6},{8,9},{9,8},{10,11... | collective-permute-start | bytes 196616 | tf_op jit(solution)/shard_map/ppermute | solution.py:380
  40.0 4.9 %collective-permute-start.8 = (f32[128,128]{1,0:T(8,128)S(1)}, f32[128,128]{1,0:T(8,128)S(1)}, u32[]{:S(2)}, u32[]{:S(2)}) collective-permute-start(f32[128,128]{1,0:T(8,128)S(1)} %get-tuple-element.40), channel_id=1, source_target_pairs={{2,0},{16,2},{6,4},{20,6},{10,8},{24,10},{14,12},{28,14},{18,16},{... | collective-permute-start | bytes 196616 | tf_op jit(solution)/shard_map/ppermute | solution.py:424
  44.9 0.0 collective-permute-done.9
  44.9 0.1 collective-permute-start.10
  45.0 0.0 collective-permute-done.11
  45.0 6.0 %collective-permute-start.12 = (f32[128,128]{1,0:T(8,128)S(1)}, f32[128,128]{1,0:T(8,128)S(1)}, u32[]{:S(2)}, u32[]{:S(2)}) collective-permute-start(f32[128,128]{1,0:T(8,128)S(1)} %add.30), channel_id=1, source_target_pairs={{0,24},{2,26},{4,28},{6,30},{8,0},{10,2},{12,4},{14,6},{16,8},{18,... | collective-permute-start | bytes 196616 | tf_op jit(solution)/shard_map/ppermute | solution.py:428
  51.0 0.8 %index_logits.3 = (f32[128,128]{1,0:T(8,128)S(1)}, bf16[256,4096]{1,0:T(8,128)(2,1)S(1)}) custom-call(s32[16]{0:T(128)S(1)} %get-tuple-element.29.facts_ref, bf16[32,64,128]{2,1,0:T(8,128)(2,1)S(1)} %bitcast.15, bf16[32,64,128]{2,1,0:T(8,128)(2,1)S(1)} %bitcast.19, f32[32,128]{1,0:T(8,128)S(1)} %bitcast.28, f32[32,128]{1,0:T(8,128)S(1)} %collective-permute-done.1.refs_3_, ...), custom_call_target="tpu_custom_call" | custom-call | flops 268435456 | bytes 1048576 | tf_op jit(solution)/shard_map/index_logits/pallas_call | solution.py:273
  51.8 0.0 collective-permute-done.16.refs_5_
  51.8 0.7 %index_grad.3 = (f32[128,128]{1,0:T(8,128)S(1)}, f32[128,128]{1,0:T(8,128)S(1)}) custom-call(s32[16]{0:T(128)S(1)} %get-tuple-element.29.facts_ref, bf16[32,64,128]{2,1,0:T(8,128)(2,1)S(1)} %bitcast.16, bf16[32,64,128]{2,1,0:T(8,128)(2,1)S(1)} %bitcast.20, f32[32,128]{1,0:T(8,128)S(1)} %bitcast.29, f32[32,128]{1,0:T(8,128)S(1)} %collective-permute-done.1.refs_3_, ...), custom_call_target="tpu_custom_call" | custom-call | flops 268435456 | bytes 1048576 | tf_op jit(solution)/shard_map/index_grad/pallas_call | solution.py:344
  52.5 1.2 %collective-permute-start.17 = (f32[128,128]{1,0:T(8,128)S(1)}, f32[128,128]{1,0:T(8,128)S(1)}, u32[]{:S(2)}, u32[]{:S(2)}) collective-permute-start(f32[128,128]{1,0:T(8,128)S(1)} %get-tuple-element.50), channel_id=1, source_target_pairs={{0,2},{2,0},{4,6},{6,4},{8,10},{10,8},{12,14},{14,12},{16,18},{18,... | collective-permute-start | bytes 196616 | tf_op jit(solution)/shard_map/ppermute | solution.py:426
  53.7 0.0 collective-permute-done.8
  53.7 0.0 collective-permute-done.10
  53.7 0.0 collective-permute-done.12
  53.7 1.6 %collective-permute-start.13 = (f32[128,128]{1,0:T(8,128)S(1)}, f32[128,128]{1,0:T(8,128)S(1)}, u32[]{:S(2)}, u32[]{:S(2)}) collective-permute-start(f32[128,128]{1,0:T(8,128)S(1)} %add_add_fusion.1), channel_id=1, source_target_pairs={{0,1},{1,0},{2,3},{3,2},{4,5},{5,4},{6,7},{7,6},{8,9},{9,8},{10,11... | collective-permute-start | bytes 196616 | tf_op jit(solution)/shard_map/ppermute | solution.py:380
  55.3 0.0 collective-permute-done.17
  55.3 1.7 %collective-permute-start.18 = (bf16[128,128]{1,0:T(8,128)(2,1)S(1)}, bf16[128,128]{1,0:T(8,128)(2,1)S(1)}, u32[]{:S(2)}, u32[]{:S(2)}) collective-permute-start(bf16[128,128]{1,0:T(8,128)(2,1)S(1)} %add_convert_fusion), channel_id=1, source_target_pairs={{0,20},{1,21},{2,22},{3,23},{4,24},{5,25},{6,26},{7,27},{8,28},{9,... | collective-permute-start | bytes 98312 | tf_op jit(solution)/shard_map/ppermute | solution.py:436
  57.0 0.2 collective-permute-start.19
  57.2 3.2 %collective-permute-done.18 = bf16[128,128]{1,0:T(8,128)(2,1)S(1)} collective-permute-done((bf16[128,128]{1,0:T(8,128)(2,1)S(1)}, bf16[128,128]{1,0:T(8,128)(2,1)S(1)}, u32[]{:S(2)}, u32[]{:S(2)}) %collective-permute-start.18) | collective-permute-done | bytes 32800 | tf_op jit(solution)/shard_map/ppermute | solution.py:436
  60.5 2.3 %collective-permute-done.19 = bf16[128,128]{1,0:T(8,128)(2,1)S(1)} collective-permute-done((bf16[128,128]{1,0:T(8,128)(2,1)S(1)}, bf16[128,128]{1,0:T(8,128)(2,1)S(1)}, u32[]{:S(2)}, u32[]{:S(2)}) %collective-permute-start.19) | collective-permute-done | bytes 32800 | tf_op jit(solution)/shard_map/ppermute | solution.py:436
  62.7 0.0 collective-permute-done.13
  62.7 0.6 %add_add_fusion = f32[128,128]{1,0:T(8,128)} fusion(bf16[128,128]{1,0:T(8,128)(2,1)S(1)} %collective-permute-done.19, bf16[128,128]{1,0:T(8,128)(2,1)S(1)} %collective-permute-done.18, f32[128,128]{1,0:T(8,128)S(1)} %add_add_fusion.1, f32[128,128]{1,0:T(8,128)S(1)} %collective-permute-done.13), kind=kLoop, calls=%fused_computation.2 | loop fusion | flops 81920 | bytes 262144 | tf_op jit(solution)/shard_map/add | solution.py:438
  (7 shorter events, 0.1 us)
Async XLA Ops:
  0.9 1.2 %copy-start.6 = (bf16[128,32,128]{2,1,0:T(8,128)(2,1)S(1)}, bf16[128,32,128]{2,1,0:T(8,128)(2,1)}, u32[]{:S(2)}) copy-start(bf16[128,32,128]{2,1,0:T(8,128)(2,1)} %queries_ref.1) | copy-start | bytes 3145732
  2.2 14.0 %copy-start = (bf16[128,64,576]{0,2,1:T(8,128)(2,1)S(1)}, bf16[128,64,576]{0,2,1:T(8,128)(2,1)}, u32[]{:S(2)}) copy-start(bf16[128,64,576]{0,2,1:T(8,128)(2,1)} %param.9) | copy-start | bytes 28311556
  2.2 14.0 %copy-start.1 = (f32[128,64]{0,1:T(8,128)S(1)}, f32[128,64]{0,1:T(8,128)}, u32[]{:S(2)}) copy-start(f32[128,64]{0,1:T(8,128)} %param.11) | copy-start | bytes 98308
  2.2 14.1 %copy-start.3 = (s32[16,16]{1,0:T(8,128)S(1)}, s32[16,16]{1,0:T(8,128)}, u32[]{:S(2)}) copy-start(s32[16,16]{1,0:T(8,128)} %live_ref.1) | copy-start | bytes 3076
  2.2 14.1 %copy-start.5 = (s32[16]{0:T(128)S(1)}, s32[16]{0:T(128)}, u32[]{:S(2)}) copy-start(s32[16]{0:T(128)} %order_ref.1) | copy-start | bytes 196
  2.3 11.5 %collective-permute-start.5 = (bf16[704,128]{1,0:T(8,128)(2,1)S(1)}, bf16[704,128]{1,0:T(8,128)(2,1)S(1)}, u32[]{:S(2)}, u32[]{:S(2)}) collective-permute-start(bf16[704,128]{1,0:T(8,128)(2,1)S(1)} %get-tuple-element.28.block_ref.refs_5_), channel_id=1, source_target_pairs={{0,4},{2,6},{4,8},{6,10},{8,12},{10,14},{12,16},{14,18},{16,20},{1... | collective-permute-start | bytes 540680 | tf_op jit(solution)/shard_map/ppermute | solution.py:387
  5.3 14.0 %collective-permute-start.2 = (bf16[704,128]{1,0:T(8,128)(2,1)S(1)}, bf16[704,128]{1,0:T(8,128)(2,1)S(1)}, u32[]{:S(2)}, u32[]{:S(2)}) collective-permute-start(bf16[704,128]{1,0:T(8,128)(2,1)S(1)} %get-tuple-element.28.block_ref.refs_5_), channel_id=1, source_target_pairs={{0,8},{2,10},{4,12},{6,14},{8,16},{10,18},{12,20},{14,22},{16,24},... | collective-permute-start | bytes 540680 | tf_op jit(solution)/shard_map/ppermute | solution.py:388
  13.8 7.0 %collective-permute-start.6 = (bf16[704,128]{1,0:T(8,128)(2,1)S(1)}, bf16[704,128]{1,0:T(8,128)(2,1)S(1)}, u32[]{:S(2)}, u32[]{:S(2)}) collective-permute-start(bf16[704,128]{1,0:T(8,128)(2,1)S(1)} %collective-permute-done.5.refs_0_.refs_6_), channel_id=1, source_target_pairs={{0,2},{2,0},{4,6},{6,4},{8,10},{10,8},{12,14},{14,12},{16,18},{18,... | collective-permute-start | bytes 540680 | tf_op jit(solution)/shard_map/ppermute | solution.py:393
  13.8 9.6 %collective-permute-start.4 = (bf16[704,128]{1,0:T(8,128)(2,1)S(1)}, bf16[704,128]{1,0:T(8,128)(2,1)S(1)}, u32[]{:S(2)}, u32[]{:S(2)}) collective-permute-start(bf16[704,128]{1,0:T(8,128)(2,1)S(1)} %get-tuple-element.28.block_ref.refs_5_), channel_id=1, source_target_pairs={{0,2},{2,16},{4,6},{6,20},{8,10},{10,24},{12,14},{14,28},{16,18},{... | collective-permute-start | bytes 540680 | tf_op jit(solution)/shard_map/ppermute | solution.py:389
  14.5 19.0 %collective-permute-start = (bf16[64,32,128]{2,0,1:T(8,128)(2,1)S(1)}, bf16[64,32,128]{2,0,1:T(8,128)(2,1)S(1)}, u32[]{:S(2)}, u32[]{:S(2)}) collective-permute-start(bf16[64,32,128]{2,0,1:T(8,128)(2,1)S(1)} %copy.12), channel_id=1, source_target_pairs={{0,1},{1,0},{2,3},{3,2},{4,5},{5,4},{6,7},{7,6},{8,9},{9,8},{10,11... | collective-permute-start | bytes 1572872 | tf_op jit(solution)/shard_map/ppermute | solution.py:380
  19.3 8.4 %collective-permute-start.14 = (bf16[704,128]{1,0:T(8,128)(2,1)S(1)}, bf16[704,128]{1,0:T(8,128)(2,1)S(1)}, u32[]{:S(2)}, u32[]{:S(2)}) collective-permute-start(bf16[704,128]{1,0:T(8,128)(2,1)S(1)} %collective-permute-done.5.refs_0_.refs_6_), channel_id=1, source_target_pairs={{0,8},{2,10},{4,12},{6,14},{8,16},{10,18},{12,20},{14,22},{16,24},... | collective-permute-start | bytes 540680 | tf_op jit(solution)/shard_map/ppermute | solution.py:392
  19.4 4.0 %collective-permute-start.3 = (bf16[704,128]{1,0:T(8,128)(2,1)S(1)}, bf16[704,128]{1,0:T(8,128)(2,1)S(1)}, u32[]{:S(2)}, u32[]{:S(2)}) collective-permute-start(bf16[704,128]{1,0:T(8,128)(2,1)S(1)} %collective-permute-done.2.refs_0_.refs_8_), channel_id=1, source_target_pairs={{0,2},{2,0},{4,6},{6,4},{8,10},{10,8},{12,14},{14,12},{16,18},{18,... | collective-permute-start | bytes 540680 | tf_op jit(solution)/shard_map/ppermute | solution.py:393
  23.4 4.3 %copy-start.2 = (f32[128,32]{0,1:T(8,128)S(1)}, f32[128,32]{0,1:T(8,128)}, u32[]{:S(2)}) copy-start(f32[128,32]{0,1:T(8,128)} %param.13) | copy-start | bytes 49156
  23.4 10.1 %copy-start.4 = (f32[128]{0:T(128)S(1)}, f32[128]{0:T(128)}, u32[]{:S(2)}) copy-start(f32[128]{0:T(128)} %param.15) | copy-start | bytes 1540
  24.5 10.7 %collective-permute-start.7 = (f32[384,128]{1,0:T(8,128)S(1)}, f32[384,128]{1,0:T(8,128)S(1)}, u32[]{:S(2)}, u32[]{:S(2)}) collective-permute-start(f32[384,128]{1,0:T(8,128)S(1)} %get-tuple-element.36), channel_id=1, source_target_pairs={{0,1},{1,0},{2,3},{3,2},{4,5},{5,4},{6,7},{7,6},{8,9},{9,8},{10,11... | collective-permute-start | bytes 589832 | tf_op jit(solution)/shard_map/ppermute | solution.py:380
  27.7 10.0 %collective-permute-start.15 = (bf16[704,128]{1,0:T(8,128)(2,1)S(1)}, bf16[704,128]{1,0:T(8,128)(2,1)S(1)}, u32[]{:S(2)}, u32[]{:S(2)}) collective-permute-start(bf16[704,128]{1,0:T(8,128)(2,1)S(1)} %collective-permute-done.14.refs_0_.refs_5_), channel_id=1, source_target_pairs={{0,2},{2,0},{4,6},{6,4},{8,10},{10,8},{12,14},{14,12},{16,18},{18,... | collective-permute-start | bytes 540680 | tf_op jit(solution)/shard_map/ppermute | solution.py:393
  27.7 5.8 %collective-permute-start.1 = (f32[32,128]{1,0:T(8,128)S(1)}, f32[32,128]{1,0:T(8,128)S(1)}, u32[]{:S(2)}, u32[]{:S(2)}) collective-permute-start(f32[32,128]{1,0:T(8,128)S(1)} %bitcast.25), channel_id=1, source_target_pairs={{0,1},{1,0},{2,3},{3,2},{4,5},{5,4},{6,7},{7,6},{8,9},{9,8},{10,11... | collective-permute-start | bytes 49160 | tf_op jit(solution)/shard_map/ppermute | solution.py:380
  37.1 7.8 %collective-permute-start.9 = (f32[128,128]{1,0:T(8,128)S(1)}, f32[128,128]{1,0:T(8,128)S(1)}, u32[]{:S(2)}, u32[]{:S(2)}) collective-permute-start(f32[128,128]{1,0:T(8,128)S(1)} %get-tuple-element.42), channel_id=1, source_target_pairs={{0,2},{2,0},{4,6},{6,4},{8,10},{10,8},{12,14},{14,12},{16,18},{18,... | collective-permute-start | bytes 196616 | tf_op jit(solution)/shard_map/ppermute | solution.py:426
  37.2 7.8 %collective-permute-start.11 = (f32[128,128]{1,0:T(8,128)S(1)}, f32[128,128]{1,0:T(8,128)S(1)}, u32[]{:S(2)}, u32[]{:S(2)}) collective-permute-start(f32[128,128]{1,0:T(8,128)S(1)} %get-tuple-element.44), channel_id=1, source_target_pairs={{0,2},{2,0},{4,6},{6,4},{8,10},{10,8},{12,14},{14,12},{16,18},{18,... | collective-permute-start | bytes 196616 | tf_op jit(solution)/shard_map/ppermute | solution.py:426
  38.5 13.3 %collective-permute-start.16 = (f32[128,128]{1,0:T(8,128)S(1)}, f32[128,128]{1,0:T(8,128)S(1)}, u32[]{:S(2)}, u32[]{:S(2)}) collective-permute-start(f32[128,128]{1,0:T(8,128)S(1)} %get-tuple-element.46), channel_id=1, source_target_pairs={{0,1},{1,0},{2,3},{3,2},{4,5},{5,4},{6,7},{7,6},{8,9},{9,8},{10,11... | collective-permute-start | bytes 196616 | tf_op jit(solution)/shard_map/ppermute | solution.py:380
  40.0 13.7 %collective-permute-start.8 = (f32[128,128]{1,0:T(8,128)S(1)}, f32[128,128]{1,0:T(8,128)S(1)}, u32[]{:S(2)}, u32[]{:S(2)}) collective-permute-start(f32[128,128]{1,0:T(8,128)S(1)} %get-tuple-element.40), channel_id=1, source_target_pairs={{2,0},{16,2},{6,4},{20,6},{10,8},{24,10},{14,12},{28,14},{18,16},{... | collective-permute-start | bytes 196616 | tf_op jit(solution)/shard_map/ppermute | solution.py:424
  44.9 8.8 %collective-permute-start.10 = (f32[128,128]{1,0:T(8,128)S(1)}, f32[128,128]{1,0:T(8,128)S(1)}, u32[]{:S(2)}, u32[]{:S(2)}) collective-permute-start(f32[128,128]{1,0:T(8,128)S(1)} %add.28), channel_id=1, source_target_pairs={{0,28},{2,30},{4,0},{6,2},{8,4},{10,6},{12,8},{14,10},{16,12},{18,... | collective-permute-start | bytes 196616 | tf_op jit(solution)/shard_map/ppermute | solution.py:428
  45.0 8.7 %collective-permute-start.12 = (f32[128,128]{1,0:T(8,128)S(1)}, f32[128,128]{1,0:T(8,128)S(1)}, u32[]{:S(2)}, u32[]{:S(2)}) collective-permute-start(f32[128,128]{1,0:T(8,128)S(1)} %add.30), channel_id=1, source_target_pairs={{0,24},{2,26},{4,28},{6,30},{8,0},{10,2},{12,4},{14,6},{16,8},{18,... | collective-permute-start | bytes 196616 | tf_op jit(solution)/shard_map/ppermute | solution.py:428
  52.5 2.8 %collective-permute-start.17 = (f32[128,128]{1,0:T(8,128)S(1)}, f32[128,128]{1,0:T(8,128)S(1)}, u32[]{:S(2)}, u32[]{:S(2)}) collective-permute-start(f32[128,128]{1,0:T(8,128)S(1)} %get-tuple-element.50), channel_id=1, source_target_pairs={{0,2},{2,0},{4,6},{6,4},{8,10},{10,8},{12,14},{14,12},{16,18},{18,... | collective-permute-start | bytes 196616 | tf_op jit(solution)/shard_map/ppermute | solution.py:426
  53.7 9.0 %collective-permute-start.13 = (f32[128,128]{1,0:T(8,128)S(1)}, f32[128,128]{1,0:T(8,128)S(1)}, u32[]{:S(2)}, u32[]{:S(2)}) collective-permute-start(f32[128,128]{1,0:T(8,128)S(1)} %add_add_fusion.1), channel_id=1, source_target_pairs={{0,1},{1,0},{2,3},{3,2},{4,5},{5,4},{6,7},{7,6},{8,9},{9,8},{10,11... | collective-permute-start | bytes 196616 | tf_op jit(solution)/shard_map/ppermute | solution.py:380
  55.3 5.2 %collective-permute-start.18 = (bf16[128,128]{1,0:T(8,128)(2,1)S(1)}, bf16[128,128]{1,0:T(8,128)(2,1)S(1)}, u32[]{:S(2)}, u32[]{:S(2)}) collective-permute-start(bf16[128,128]{1,0:T(8,128)(2,1)S(1)} %add_convert_fusion), channel_id=1, source_target_pairs={{0,20},{1,21},{2,22},{3,23},{4,24},{5,25},{6,26},{7,27},{8,28},{9,... | collective-permute-start | bytes 98312 | tf_op jit(solution)/shard_map/ppermute | solution.py:436
  57.0 5.7 %collective-permute-start.19 = (bf16[128,128]{1,0:T(8,128)(2,1)S(1)}, bf16[128,128]{1,0:T(8,128)(2,1)S(1)}, u32[]{:S(2)}, u32[]{:S(2)}) collective-permute-start(bf16[128,128]{1,0:T(8,128)(2,1)S(1)} %add_convert_fusion), channel_id=1, source_target_pairs={{0,21},{1,20},{2,23},{3,22},{4,25},{5,24},{6,27},{7,26},{8,29},{9,... | collective-permute-start | bytes 98312 | tf_op jit(solution)/shard_map/ppermute | solution.py:436
